TPU v7x, 32 devices: a whole 2x2x4 slice. The times are simulated.
32 devices in a mesh: gx: 4 (over y, core), gy: 2 (over x), gz: 4 (over z).
Axes of the slice: x: 2, y: 2, z: 4, core: 2. Of those that a mesh axis runs over, the one named last changes fastest.
Arguments:
- noisy_image: float32 [32, 64, 512], P('gz', 'gy', 'gx'), may hold values from -6 to 6
- fidelity: float32 [32, 64, 512], P('gz', 'gy', 'gx'), may hold values from 0.5 to 8
- primal_u: float32 [32, 64, 512], P('gz', 'gy', 'gx'), may hold values from -6 to 6
- primal_v: float32 [3, 32, 64, 512], P(None, 'gz', 'gy', 'gx'), may hold values from -2 to 2
- dual_p: float32 [3, 32, 64, 512], P(None, 'gz', 'gy', 'gx'), may hold values from -2.5 to 2.5
- dual_q: float32 [6, 32, 64, 512], P(None, 'gz', 'gy', 'gx'), may hold values from -2.5 to 2.5
Outputs:
- denoised: float32 [32, 64, 512], P('gz', 'gy', 'gx')
- vector_field: float32 [3, 32, 64, 512], P(None, 'gz', 'gy', 'gx')
- grad_dual: float32 [3, 32, 64, 512], P(None, 'gz', 'gy', 'gx')
- sym_dual: float32 [6, 32, 64, 512], P(None, 'gz', 'gy', 'gx')
All inputs are finite; a program needn't handle non-finite values.
Results may differ from a plain program's by a relative error of at most 0.0001.
Values sent between devices are 32-bit elements; how exact they have to be, the bound alone decides.
No kernel may reach another device: no remote copies, remote signals or barrier semaphores. Data moves between devices by JAX's collectives and lax.ppermute only.
A program may use at most 64 MiB of HBM per device.

v0:
```python
import jax
import jax.numpy as jnp
from jax import lax
from jax.sharding import PartitionSpec as P

ITERS = 3


first_alpha = 0.5
second_alpha = 1.0
dual_step = 0.2
primal_step = 0.2
index_pairs = ((0, 0), (1, 1), (2, 2), (0, 1), (0, 2), (1, 2))


def passed_along(shard, axis, by):
    devices = lax.axis_size(axis)
    pairs = [(i, i + by) for i in range(devices) if 0 <= i + by < devices]
    return lax.ppermute(shard, axis, pairs)


def pair_index(left_axis, right_axis):
    for position, entry_pair in enumerate(index_pairs):
        if entry_pair == (left_axis, right_axis) or entry_pair == (right_axis, left_axis):
            return position
    return 0


def first_layer(values, axis_dim):
    return lax.slice_in_dim(values, 0, 1, axis=axis_dim)


def last_layer(values, axis_dim):
    extent = values.shape[axis_dim]
    return lax.slice_in_dim(values, extent - 1, extent, axis=axis_dim)


def following(values, border, axis_dim):
    extent = values.shape[axis_dim]
    return jnp.concatenate(
        [lax.slice_in_dim(values, 1, extent, axis=axis_dim), border], axis=axis_dim
    )


def preceding(values, border, axis_dim):
    extent = values.shape[axis_dim]
    return jnp.concatenate(
        [border, lax.slice_in_dim(values, 0, extent - 1, axis=axis_dim)], axis=axis_dim
    )


def edge_masks(extents, margin):
    device_places = (lax.axis_index("gx"), lax.axis_index("gy"), lax.axis_index("gz"))
    group_sizes = (lax.axis_size("gx"), lax.axis_size("gy"), lax.axis_size("gz"))
    lower_masks = []
    upper_masks = []
    inside = jnp.ones((1, 1, 1, 1), jnp.float32)
    for component in range(3):
        extent = extents[2 - component]
        places = (
            device_places[component] * extent - margin + lax.iota(jnp.int32, extent + 2 * margin)
        )
        full_extent = group_sizes[component] * extent
        shape_list = [1, 1, 1, 1]
        shape_list[3 - component] = extent + 2 * margin
        upper_masks.append((places < full_extent - 1).astype(jnp.float32).reshape(shape_list))
        lower_masks.append((places > 0).astype(jnp.float32).reshape(shape_list))
        within = jnp.logical_and(places >= 0, places < full_extent)
        inside = inside * within.astype(jnp.float32).reshape(shape_list)
    return (lower_masks, upper_masks, inside)


def q_rows(stacked, column):
    return jnp.stack([stacked[pair_index(row_axis, column)] for row_axis in range(3)], axis=0)


def project(stacked, weights, bound):
    magnitude = jnp.sqrt(jnp.sum(weights * stacked * stacked, axis=0, keepdims=True))
    return stacked / jnp.maximum(1.0, magnitude / bound)


def dual_update(bar_u, bar_v, grad_dual, sym_dual, next_u, prev_v, lower_masks, upper_masks):
    grads = jnp.concatenate(
        [upper_masks[component] * (next_u[component] - bar_u) for component in range(3)], axis=0
    )
    trial_p = grad_dual + dual_step * (grads - bar_v)
    new_p = project(trial_p, jnp.ones((3, 1, 1, 1), jnp.float32), first_alpha)
    derivs = [lower_masks[component] * (bar_v - prev_v[component]) for component in range(3)]
    sym_parts = []
    for left_axis, right_axis in index_pairs:
        sym_parts.append(0.5 * (derivs[right_axis][left_axis] + derivs[left_axis][right_axis]))
    trial_q = sym_dual + dual_step * jnp.stack(sym_parts, axis=0)
    weights = jnp.array([1.0, 1.0, 1.0, 2.0, 2.0, 2.0], jnp.float32).reshape((6, 1, 1, 1))
    new_q = project(trial_q, weights, second_alpha)
    return (new_p, new_q)


def primal_update(
    image_u,
    vector_v,
    grad_dual,
    sym_dual,
    noisy,
    weight_map,
    prev_p,
    next_q,
    lower_masks,
    upper_masks,
):
    divergence = jnp.zeros_like(image_u)
    second_div = jnp.zeros_like(vector_v)
    for component in range(3):
        divergence = (
            divergence
            + upper_masks[component] * grad_dual[component : component + 1]
            - prev_p[component]
        )
        second_div = (
            second_div + next_q[component] - lower_masks[component] * q_rows(sym_dual, component)
        )
    new_u = (image_u + primal_step * divergence + primal_step * weight_map * noisy) / (
        1.0 + primal_step * weight_map
    )
    new_v = vector_v + primal_step * (grad_dual + second_div)
    return (new_u, new_v)


def per_device(noisy_image, fidelity, primal_u, primal_v, dual_p, dual_q):
    noisy = noisy_image[None]
    weight_map = fidelity[None]
    image_u = primal_u[None]
    vector_v = primal_v
    grad_dual = dual_p
    sym_dual = dual_q
    lower_masks, upper_masks, unused_inside = edge_masks(noisy_image.shape, 0)
    bar_u = image_u
    bar_v = vector_v
    for step_index in range(ITERS):
        next_u = [
            following(bar_u, passed_along(first_layer(bar_u, 3), "gx", -1), 3),
            following(bar_u, passed_along(first_layer(bar_u, 2), "gy", -1), 2),
            following(bar_u, passed_along(first_layer(bar_u, 1), "gz", -1), 1),
        ]
        prev_v = [
            preceding(bar_v, passed_along(last_layer(bar_v, 3), "gx", 1), 3),
            preceding(bar_v, passed_along(last_layer(bar_v, 2), "gy", 1), 2),
            preceding(bar_v, passed_along(last_layer(bar_v, 1), "gz", 1), 1),
        ]
        grad_dual, sym_dual = dual_update(
            bar_u, bar_v, grad_dual, sym_dual, next_u, prev_v, lower_masks, upper_masks
        )
        grad_x = grad_dual[0:1]
        grad_y = grad_dual[1:2]
        grad_z = grad_dual[2:3]
        prev_p = [
            preceding(grad_x, passed_along(last_layer(grad_x, 3), "gx", 1), 3),
            preceding(grad_y, passed_along(last_layer(grad_y, 2), "gy", 1), 2),
            preceding(grad_z, passed_along(last_layer(grad_z, 1), "gz", 1), 1),
        ]
        rows_x = q_rows(sym_dual, 0)
        rows_y = q_rows(sym_dual, 1)
        rows_z = q_rows(sym_dual, 2)
        next_q = [
            following(rows_x, passed_along(first_layer(rows_x, 3), "gx", -1), 3),
            following(rows_y, passed_along(first_layer(rows_y, 2), "gy", -1), 2),
            following(rows_z, passed_along(first_layer(rows_z, 1), "gz", -1), 1),
        ]
        new_u, new_v = primal_update(
            image_u,
            vector_v,
            grad_dual,
            sym_dual,
            noisy,
            weight_map,
            prev_p,
            next_q,
            lower_masks,
            upper_masks,
        )
        bar_u = 2.0 * new_u - image_u
        bar_v = 2.0 * new_v - vector_v
        image_u = new_u
        vector_v = new_v
    return (image_u[0], vector_v, grad_dual, sym_dual)


def solution(mesh):
    in_specs = (
        P("gz", "gy", "gx"),
        P("gz", "gy", "gx"),
        P("gz", "gy", "gx"),
        P(None, "gz", "gy", "gx"),
        P(None, "gz", "gy", "gx"),
        P(None, "gz", "gy", "gx"),
    )
    out_specs = (
        P("gz", "gy", "gx"),
        P(None, "gz", "gy", "gx"),
        P(None, "gz", "gy", "gx"),
        P(None, "gz", "gy", "gx"),
    )
    return jax.shard_map(
        per_device, mesh=mesh, in_specs=in_specs, out_specs=out_specs, check_vma=False
    )
```

profile of v0, /device:TPU:17, one launch (start us, length us, event | category | flops | bytes accessed | tf_op | source)
XLA Modules:
  0.0 154.1 jit_solution(12084420073467371968)
XLA Ops:
  3.7 4.0 %collective-permute-start.10 = (f32[3,8,1,128]{3,1,2,0:T(8,128)S(1)}, f32[3,8,1,128]{3,1,2,0:T(8,128)S(1)}, u32[]{:S(2)}, u32[]{:S(2)}) collective-permute-start(f32[3,8,1,128]{3,1,2,0:T(8,128)S(1)} %bitcast.80), channel_id=1, source_target_pairs={{0,4},{1,5},{2,6},{3,7},{8,12},{9,13},{10,14},{11,15},{16,20},{17,... | collective-permute-start | bytes 36872 | tf_op jit(solution)/shard_map/ppermute | solution.py:19
  8.4 2.1 %collective-permute-start.2 = (f32[1,1,32,128]{3,2,1,0:T(8,128)S(1)}, f32[1,1,32,128]{3,2,1,0:T(8,128)S(1)}, u32[]{:S(2)}, u32[]{:S(2)}) collective-permute-start(f32[1,1,32,128]{3,2,1,0:T(8,128)S(1)} %slice.596), channel_id=1, source_target_pairs={{1,0},{2,1},{3,2},{5,4},{6,5},{7,6},{9,8},{10,9},{11,10},{13,12},{... | collective-permute-start | bytes 49160 | tf_op jit(solution)/shard_map/ppermute | solution.py:19
  11.3 3.2 %collective-permute-start.11 = (f32[3,1,32,128]{3,2,1,0:T(8,128)S(1)}, f32[3,1,32,128]{3,2,1,0:T(8,128)S(1)}, u32[]{:S(2)}, u32[]{:S(2)}) collective-permute-start(f32[3,1,32,128]{3,2,1,0:T(8,128)S(1)} %slice.489), channel_id=1, source_target_pairs={{0,1},{1,2},{2,3},{4,5},{5,6},{6,7},{8,9},{9,10},{10,11},{12,13},{... | collective-permute-start | bytes 147464 | tf_op jit(solution)/shard_map/ppermute | solution.py:19
  14.5 3.7 %collective-permute-start = (f32[1,8,32,1]{3,2,1,0:T(8,128)S(1)}, f32[1,8,32,1]{3,2,1,0:T(8,128)S(1)}, u32[]{:S(2)}, u32[]{:S(2)}) collective-permute-start(f32[1,8,32,1]{3,2,1,0:T(8,128)S(1)} %bitcast.68), channel_id=1, source_target_pairs={{8,0},{16,8},{24,16},{9,1},{17,9},{25,17},{10,2},{18,10},{26,18},{... | collective-permute-start | bytes 3080 | tf_op jit(solution)/shard_map/ppermute | solution.py:19
  19.4 2.6 %collective-permute-done = f32[1,8,32,1]{3,2,1,0:T(8,128)S(1)} collective-permute-done((f32[1,8,32,1]{3,2,1,0:T(8,128)S(1)}, f32[1,8,32,1]{3,2,1,0:T(8,128)S(1)}, u32[]{:S(2)}, u32[]{:S(2)}) %collective-permute-start) | collective-permute-done | bytes 1056 | tf_op jit(solution)/shard_map/ppermute | solution.py:19
  21.9 1.9 %collective-permute-start.9 = (f32[3,8,32,1]{3,2,1,0:T(8,128)S(1)}, f32[3,8,32,1]{3,2,1,0:T(8,128)S(1)}, u32[]{:S(2)}, u32[]{:S(2)}) collective-permute-start(f32[3,8,32,1]{3,2,1,0:T(8,128)S(1)} %slice.483), channel_id=1, source_target_pairs={{0,8},{8,16},{16,24},{1,9},{9,17},{17,25},{2,10},{10,18},{18,26},{... | collective-permute-start | bytes 9224 | tf_op jit(solution)/shard_map/ppermute | solution.py:19
  24.0 4.5 %collective-permute-done.9 = f32[3,8,32,1]{3,2,1,0:T(8,128)S(1)} collective-permute-done((f32[3,8,32,1]{3,2,1,0:T(8,128)S(1)}, f32[3,8,32,1]{3,2,1,0:T(8,128)S(1)}, u32[]{:S(2)}, u32[]{:S(2)}) %collective-permute-start.9) | collective-permute-done | bytes 3104 | tf_op jit(solution)/shard_map/ppermute | solution.py:19
  31.3 1.3 collective-permute-start.4
  32.6 1.9 %collective-permute-start.5 = (f32[1,1,32,128]{3,2,1,0:T(8,128)S(1)}, f32[1,1,32,128]{3,2,1,0:T(8,128)S(1)}, u32[]{:S(2)}, u32[]{:S(2)}) collective-permute-start(f32[1,1,32,128]{3,2,1,0:T(8,128)S(1)} %slice.604), channel_id=1, source_target_pairs={{0,1},{1,2},{2,3},{4,5},{5,6},{6,7},{8,9},{9,10},{10,11},{12,13},{... | collective-permute-start | bytes 49160 | tf_op jit(solution)/shard_map/ppermute | solution.py:19
  34.5 4.4 %collective-permute-start.3 = (f32[1,8,32,1]{3,2,1,0:T(8,128)S(1)}, f32[1,8,32,1]{3,2,1,0:T(8,128)S(1)}, u32[]{:S(2)}, u32[]{:S(2)}) collective-permute-start(f32[1,8,32,1]{3,2,1,0:T(8,128)S(1)} %slice.598), channel_id=1, source_target_pairs={{0,8},{8,16},{16,24},{1,9},{9,17},{17,25},{2,10},{10,18},{18,26},{... | collective-permute-start | bytes 3080 | tf_op jit(solution)/shard_map/ppermute | solution.py:19
  39.1 1.8 %collective-permute-done.3 = f32[1,8,32,1]{3,2,1,0:T(8,128)S(1)} collective-permute-done((f32[1,8,32,1]{3,2,1,0:T(8,128)S(1)}, f32[1,8,32,1]{3,2,1,0:T(8,128)S(1)}, u32[]{:S(2)}, u32[]{:S(2)}) %collective-permute-start.3) | collective-permute-done | bytes 1056 | tf_op jit(solution)/shard_map/ppermute | solution.py:19
  41.1 1.3 collective-permute-start.7
  42.4 3.6 %collective-permute-start.8 = (f32[1,1,32,128]{3,2,1,0:T(8,128)S(1)}, f32[1,1,32,128]{3,2,1,0:T(8,128)S(1)}, u32[]{:S(2)}, u32[]{:S(2)}) collective-permute-start(f32[1,1,32,128]{3,2,1,0:T(8,128)S(1)} %slice.611), channel_id=1, source_target_pairs={{1,0},{2,1},{3,2},{5,4},{6,5},{7,6},{9,8},{10,9},{11,10},{13,12},{... | collective-permute-start | bytes 49160 | tf_op jit(solution)/shard_map/ppermute | solution.py:19
  46.0 1.9 %collective-permute-start.6 = (f32[1,8,32,1]{3,2,1,0:T(8,128)S(1)}, f32[1,8,32,1]{3,2,1,0:T(8,128)S(1)}, u32[]{:S(2)}, u32[]{:S(2)}) collective-permute-start(f32[1,8,32,1]{3,2,1,0:T(8,128)S(1)} %bitcast.73), channel_id=1, source_target_pairs={{8,0},{16,8},{24,16},{9,1},{17,9},{25,17},{10,2},{18,10},{26,18},{... | collective-permute-start | bytes 3080 | tf_op jit(solution)/shard_map/ppermute | solution.py:19
  48.1 2.1 %collective-permute-start.14 = (f32[3,1,32,128]{3,2,1,0:T(8,128)S(1)}, f32[3,1,32,128]{3,2,1,0:T(8,128)S(1)}, u32[]{:S(2)}, u32[]{:S(2)}) collective-permute-start(f32[3,1,32,128]{3,2,1,0:T(8,128)S(1)} %fusion.135), channel_id=1, source_target_pairs={{1,0},{2,1},{3,2},{5,4},{6,5},{7,6},{9,8},{10,9},{11,10},{13,12},{... | collective-permute-start | bytes 147464 | tf_op jit(solution)/shard_map/ppermute | solution.py:19
  50.1 1.3 collective-permute-start.13
  51.6 1.7 %collective-permute-done.6 = f32[1,8,32,1]{3,2,1,0:T(8,128)S(1)} collective-permute-done((f32[1,8,32,1]{3,2,1,0:T(8,128)S(1)}, f32[1,8,32,1]{3,2,1,0:T(8,128)S(1)}, u32[]{:S(2)}, u32[]{:S(2)}) %collective-permute-start.6) | collective-permute-done | bytes 1056 | tf_op jit(solution)/shard_map/ppermute | solution.py:19
  53.3 1.9 %collective-permute-start.12 = (f32[3,8,32,1]{3,2,1,0:T(8,128)S(1)}, f32[3,8,32,1]{3,2,1,0:T(8,128)S(1)}, u32[]{:S(2)}, u32[]{:S(2)}) collective-permute-start(f32[3,8,32,1]{3,2,1,0:T(8,128)S(1)} %fusion.8), channel_id=1, source_target_pairs={{8,0},{16,8},{24,16},{9,1},{17,9},{25,17},{10,2},{18,10},{26,18},{... | collective-permute-start | bytes 9224 | tf_op jit(solution)/shard_map/ppermute | solution.py:19
  55.4 7.0 %collective-permute-done.12 = f32[3,8,32,1]{3,2,1,0:T(8,128)S(1)} collective-permute-done((f32[3,8,32,1]{3,2,1,0:T(8,128)S(1)}, f32[3,8,32,1]{3,2,1,0:T(8,128)S(1)}, u32[]{:S(2)}, u32[]{:S(2)}) %collective-permute-start.12) | collective-permute-done | bytes 3104 | tf_op jit(solution)/shard_map/ppermute | solution.py:19
  63.1 4.3 %collective-permute-start.22 = (f32[3,8,1,128]{3,1,2,0:T(8,128)S(1)}, f32[3,8,1,128]{3,1,2,0:T(8,128)S(1)}, u32[]{:S(2)}, u32[]{:S(2)}) collective-permute-start(f32[3,8,1,128]{3,1,2,0:T(8,128)S(1)} %bitcast.83), channel_id=1, source_target_pairs={{0,4},{1,5},{2,6},{3,7},{8,12},{9,13},{10,14},{11,15},{16,20},{17,... | collective-permute-start | bytes 36872 | tf_op jit(solution)/shard_map/ppermute | solution.py:19
  67.4 2.7 %collective-permute-start.23 = (f32[3,1,32,128]{3,2,1,0:T(8,128)S(1)}, f32[3,1,32,128]{3,2,1,0:T(8,128)S(1)}, u32[]{:S(2)}, u32[]{:S(2)}) collective-permute-start(f32[3,1,32,128]{3,2,1,0:T(8,128)S(1)} %slice.659), channel_id=1, source_target_pairs={{0,1},{1,2},{2,3},{4,5},{5,6},{6,7},{8,9},{9,10},{10,11},{12,13},{... | collective-permute-start | bytes 147464 | tf_op jit(solution)/shard_map/ppermute | solution.py:19
  70.1 2.3 %collective-permute-start.21 = (f32[3,8,32,1]{3,2,1,0:T(8,128)S(1)}, f32[3,8,32,1]{3,2,1,0:T(8,128)S(1)}, u32[]{:S(2)}, u32[]{:S(2)}) collective-permute-start(f32[3,8,32,1]{3,2,1,0:T(8,128)S(1)} %slice.653), channel_id=1, source_target_pairs={{0,8},{8,16},{16,24},{1,9},{9,17},{17,25},{2,10},{10,18},{18,26},{... | collective-permute-start | bytes 9224 | tf_op jit(solution)/shard_map/ppermute | solution.py:19
  72.5 4.6 %collective-permute-done.21 = f32[3,8,32,1]{3,2,1,0:T(8,128)S(1)} collective-permute-done((f32[3,8,32,1]{3,2,1,0:T(8,128)S(1)}, f32[3,8,32,1]{3,2,1,0:T(8,128)S(1)}, u32[]{:S(2)}, u32[]{:S(2)}) %collective-permute-start.21) | collective-permute-done | bytes 3104 | tf_op jit(solution)/shard_map/ppermute | solution.py:19
  78.7 1.3 collective-permute-start.16
  79.9 1.9 %collective-permute-start.17 = (f32[1,1,32,128]{3,2,1,0:T(8,128)S(1)}, f32[1,1,32,128]{3,2,1,0:T(8,128)S(1)}, u32[]{:S(2)}, u32[]{:S(2)}) collective-permute-start(f32[1,1,32,128]{3,2,1,0:T(8,128)S(1)} %slice.645), channel_id=1, source_target_pairs={{0,1},{1,2},{2,3},{4,5},{5,6},{6,7},{8,9},{9,10},{10,11},{12,13},{... | collective-permute-start | bytes 49160 | tf_op jit(solution)/shard_map/ppermute | solution.py:19
  81.9 4.4 %collective-permute-start.15 = (f32[1,8,32,1]{3,2,1,0:T(8,128)S(1)}, f32[1,8,32,1]{3,2,1,0:T(8,128)S(1)}, u32[]{:S(2)}, u32[]{:S(2)}) collective-permute-start(f32[1,8,32,1]{3,2,1,0:T(8,128)S(1)} %slice.639), channel_id=1, source_target_pairs={{0,8},{8,16},{16,24},{1,9},{9,17},{17,25},{2,10},{10,18},{18,26},{... | collective-permute-start | bytes 3080 | tf_op jit(solution)/shard_map/ppermute | solution.py:19
  86.4 1.8 %collective-permute-done.15 = f32[1,8,32,1]{3,2,1,0:T(8,128)S(1)} collective-permute-done((f32[1,8,32,1]{3,2,1,0:T(8,128)S(1)}, f32[1,8,32,1]{3,2,1,0:T(8,128)S(1)}, u32[]{:S(2)}, u32[]{:S(2)}) %collective-permute-start.15) | collective-permute-done | bytes 1056 | tf_op jit(solution)/shard_map/ppermute | solution.py:19
  88.4 1.3 collective-permute-start.19
  89.7 3.6 %collective-permute-start.20 = (f32[1,1,32,128]{3,2,1,0:T(8,128)S(1)}, f32[1,1,32,128]{3,2,1,0:T(8,128)S(1)}, u32[]{:S(2)}, u32[]{:S(2)}) collective-permute-start(f32[1,1,32,128]{3,2,1,0:T(8,128)S(1)} %slice.652), channel_id=1, source_target_pairs={{1,0},{2,1},{3,2},{5,4},{6,5},{7,6},{9,8},{10,9},{11,10},{13,12},{... | collective-permute-start | bytes 49160 | tf_op jit(solution)/shard_map/ppermute | solution.py:19
  93.4 1.9 %collective-permute-start.18 = (f32[1,8,32,1]{3,2,1,0:T(8,128)S(1)}, f32[1,8,32,1]{3,2,1,0:T(8,128)S(1)}, u32[]{:S(2)}, u32[]{:S(2)}) collective-permute-start(f32[1,8,32,1]{3,2,1,0:T(8,128)S(1)} %bitcast.72), channel_id=1, source_target_pairs={{8,0},{16,8},{24,16},{9,1},{17,9},{25,17},{10,2},{18,10},{26,18},{... | collective-permute-start | bytes 3080 | tf_op jit(solution)/shard_map/ppermute | solution.py:19
  95.4 2.5 %collective-permute-start.26 = (f32[3,1,32,128]{3,2,1,0:T(8,128)S(1)}, f32[3,1,32,128]{3,2,1,0:T(8,128)S(1)}, u32[]{:S(2)}, u32[]{:S(2)}) collective-permute-start(f32[3,1,32,128]{3,2,1,0:T(8,128)S(1)} %fusion.134), channel_id=1, source_target_pairs={{1,0},{2,1},{3,2},{5,4},{6,5},{7,6},{9,8},{10,9},{11,10},{13,12},{... | collective-permute-start | bytes 147464 | tf_op jit(solution)/shard_map/ppermute | solution.py:19
  97.9 1.3 collective-permute-start.25
  99.4 1.3 collective-permute-done.18
  100.7 1.9 %collective-permute-start.24 = (f32[3,8,32,1]{3,2,1,0:T(8,128)S(1)}, f32[3,8,32,1]{3,2,1,0:T(8,128)S(1)}, u32[]{:S(2)}, u32[]{:S(2)}) collective-permute-start(f32[3,8,32,1]{3,2,1,0:T(8,128)S(1)} %fusion.6), channel_id=1, source_target_pairs={{8,0},{16,8},{24,16},{9,1},{17,9},{25,17},{10,2},{18,10},{26,18},{... | collective-permute-start | bytes 9224 | tf_op jit(solution)/shard_map/ppermute | solution.py:19
  102.7 7.0 %collective-permute-done.24 = f32[3,8,32,1]{3,2,1,0:T(8,128)S(1)} collective-permute-done((f32[3,8,32,1]{3,2,1,0:T(8,128)S(1)}, f32[3,8,32,1]{3,2,1,0:T(8,128)S(1)}, u32[]{:S(2)}, u32[]{:S(2)}) %collective-permute-start.24) | collective-permute-done | bytes 3104 | tf_op jit(solution)/shard_map/ppermute | solution.py:19
  110.4 4.3 %collective-permute-start.31 = (f32[3,8,1,128]{3,1,2,0:T(8,128)S(1)}, f32[3,8,1,128]{3,1,2,0:T(8,128)S(1)}, u32[]{:S(2)}, u32[]{:S(2)}) collective-permute-start(f32[3,8,1,128]{3,1,2,0:T(8,128)S(1)} %bitcast.84), channel_id=1, source_target_pairs={{0,4},{1,5},{2,6},{3,7},{8,12},{9,13},{10,14},{11,15},{16,20},{17,... | collective-permute-start | bytes 36872 | tf_op jit(solution)/shard_map/ppermute | solution.py:19
  114.7 2.7 %collective-permute-start.32 = (f32[3,1,32,128]{3,2,1,0:T(8,128)S(1)}, f32[3,1,32,128]{3,2,1,0:T(8,128)S(1)}, u32[]{:S(2)}, u32[]{:S(2)}) collective-permute-start(f32[3,1,32,128]{3,2,1,0:T(8,128)S(1)} %slice.700), channel_id=1, source_target_pairs={{0,1},{1,2},{2,3},{4,5},{5,6},{6,7},{8,9},{9,10},{10,11},{12,13},{... | collective-permute-start | bytes 147464 | tf_op jit(solution)/shard_map/ppermute | solution.py:19
  117.5 2.3 %collective-permute-start.30 = (f32[3,8,32,1]{3,2,1,0:T(8,128)S(1)}, f32[3,8,32,1]{3,2,1,0:T(8,128)S(1)}, u32[]{:S(2)}, u32[]{:S(2)}) collective-permute-start(f32[3,8,32,1]{3,2,1,0:T(8,128)S(1)} %slice.694), channel_id=1, source_target_pairs={{0,8},{8,16},{16,24},{1,9},{9,17},{17,25},{2,10},{10,18},{18,26},{... | collective-permute-start | bytes 9224 | tf_op jit(solution)/shard_map/ppermute | solution.py:19
  119.9 4.6 %collective-permute-done.30 = f32[3,8,32,1]{3,2,1,0:T(8,128)S(1)} collective-permute-done((f32[3,8,32,1]{3,2,1,0:T(8,128)S(1)}, f32[3,8,32,1]{3,2,1,0:T(8,128)S(1)}, u32[]{:S(2)}, u32[]{:S(2)}) %collective-permute-start.30) | collective-permute-done | bytes 3104 | tf_op jit(solution)/shard_map/ppermute | solution.py:19
  126.6 2.5 %collective-permute-start.35 = (f32[3,1,32,128]{3,2,1,0:T(8,128)S(1)}, f32[3,1,32,128]{3,2,1,0:T(8,128)S(1)}, u32[]{:S(2)}, u32[]{:S(2)}) collective-permute-start(f32[3,1,32,128]{3,2,1,0:T(8,128)S(1)} %fusion.133), channel_id=1, source_target_pairs={{1,0},{2,1},{3,2},{5,4},{6,5},{7,6},{9,8},{10,9},{11,10},{13,12},{... | collective-permute-start | bytes 147464 | tf_op jit(solution)/shard_map/ppermute | solution.py:19
  129.2 1.3 collective-permute-start.34
  130.5 1.9 %collective-permute-start.33 = (f32[3,8,32,1]{3,2,1,0:T(8,128)S(1)}, f32[3,8,32,1]{3,2,1,0:T(8,128)S(1)}, u32[]{:S(2)}, u32[]{:S(2)}) collective-permute-start(f32[3,8,32,1]{3,2,1,0:T(8,128)S(1)} %fusion.4), channel_id=1, source_target_pairs={{8,0},{16,8},{24,16},{9,1},{17,9},{25,17},{10,2},{18,10},{26,18},{... | collective-permute-start | bytes 9224 | tf_op jit(solution)/shard_map/ppermute | solution.py:19
  132.5 8.2 %collective-permute-done.33 = f32[3,8,32,1]{3,2,1,0:T(8,128)S(1)} collective-permute-done((f32[3,8,32,1]{3,2,1,0:T(8,128)S(1)}, f32[3,8,32,1]{3,2,1,0:T(8,128)S(1)}, u32[]{:S(2)}, u32[]{:S(2)}) %collective-permute-start.33) | collective-permute-done | bytes 3104 | tf_op jit(solution)/shard_map/ppermute | solution.py:19
  140.6 1.3 fusion.13
  141.9 2.7 %collective-permute-start.29 = (f32[1,1,32,128]{3,2,1,0:T(8,128)S(1)}, f32[1,1,32,128]{3,2,1,0:T(8,128)S(1)}, u32[]{:S(2)}, u32[]{:S(2)}) collective-permute-start(f32[1,1,32,128]{3,2,1,0:T(8,128)S(1)} %slice.692), channel_id=1, source_target_pairs={{0,1},{1,2},{2,3},{4,5},{5,6},{6,7},{8,9},{9,10},{10,11},{12,13},{... | collective-permute-start | bytes 49160 | tf_op jit(solution)/shard_map/ppermute | solution.py:19
  144.7 4.2 %collective-permute-start.28 = (f32[1,8,1,128]{3,2,1,0:T(1,128)S(1)}, f32[1,8,1,128]{3,2,1,0:T(1,128)S(1)}, u32[]{:S(2)}, u32[]{:S(2)}) collective-permute-start(f32[1,8,1,128]{3,2,1,0:T(1,128)S(1)} %slice.689), channel_id=1, source_target_pairs={{0,4},{1,5},{2,6},{3,7},{8,12},{9,13},{10,14},{11,15},{16,20},{17,... | collective-permute-start | bytes 12296 | tf_op jit(solution)/shard_map/ppermute | solution.py:19
  149.0 2.3 %collective-permute-start.27 = (f32[1,8,32,1]{3,2,1,0:T(8,128)S(1)}, f32[1,8,32,1]{3,2,1,0:T(8,128)S(1)}, u32[]{:S(2)}, u32[]{:S(2)}) collective-permute-start(f32[1,8,32,1]{3,2,1,0:T(8,128)S(1)} %slice.686), channel_id=1, source_target_pairs={{0,8},{8,16},{16,24},{1,9},{9,17},{17,25},{2,10},{10,18},{18,26},{... | collective-permute-start | bytes 3080 | tf_op jit(solution)/shard_map/ppermute | solution.py:19
  151.4 1.9 %collective-permute-done.27 = f32[1,8,32,1]{3,2,1,0:T(8,128)S(1)} collective-permute-done((f32[1,8,32,1]{3,2,1,0:T(8,128)S(1)}, f32[1,8,32,1]{3,2,1,0:T(8,128)S(1)}, u32[]{:S(2)}, u32[]{:S(2)}) %collective-permute-start.27) | collective-permute-done | bytes 1056 | tf_op jit(solution)/shard_map/ppermute | solution.py:19
  (163 shorter events, 15.4 us)
Async XLA Ops:
  0.6 13.8 %copy-start.3 = (f32[8,32,128]{2,1,0:T(8,128)S(1)}, f32[8,32,128]{2,1,0:T(8,128)}, u32[]{:S(2)}) copy-start(f32[8,32,128]{2,1,0:T(8,128)} %param.11) | copy-start | bytes 393220
  1.5 22.4 %collective-permute-start.1 = (f32[1,8,1,128]{3,2,1,0:T(1,128)S(1)}, f32[1,8,1,128]{3,2,1,0:T(1,128)S(1)}, u32[]{:S(2)}, u32[]{:S(2)}) collective-permute-start(f32[1,8,1,128]{3,2,1,0:T(1,128)S(1)} %slice.594), channel_id=1, source_target_pairs={{4,0},{5,1},{6,2},{7,3},{12,8},{13,9},{14,10},{15,11},{20,16},{21,... | collective-permute-start | bytes 12296 | tf_op jit(solution)/shard_map/ppermute | solution.py:19
  3.7 24.9 %collective-permute-start.10 = (f32[3,8,1,128]{3,1,2,0:T(8,128)S(1)}, f32[3,8,1,128]{3,1,2,0:T(8,128)S(1)}, u32[]{:S(2)}, u32[]{:S(2)}) collective-permute-start(f32[3,8,1,128]{3,1,2,0:T(8,128)S(1)} %bitcast.80), channel_id=1, source_target_pairs={{0,4},{1,5},{2,6},{3,7},{8,12},{9,13},{10,14},{11,15},{16,20},{17,... | collective-permute-start | bytes 36872 | tf_op jit(solution)/shard_map/ppermute | solution.py:19
  8.4 15.5 %collective-permute-start.2 = (f32[1,1,32,128]{3,2,1,0:T(8,128)S(1)}, f32[1,1,32,128]{3,2,1,0:T(8,128)S(1)}, u32[]{:S(2)}, u32[]{:S(2)}) collective-permute-start(f32[1,1,32,128]{3,2,1,0:T(8,128)S(1)} %slice.596), channel_id=1, source_target_pairs={{1,0},{2,1},{3,2},{5,4},{6,5},{7,6},{9,8},{10,9},{11,10},{13,12},{... | collective-permute-start | bytes 49160 | tf_op jit(solution)/shard_map/ppermute | solution.py:19
  11.3 17.3 %collective-permute-start.11 = (f32[3,1,32,128]{3,2,1,0:T(8,128)S(1)}, f32[3,1,32,128]{3,2,1,0:T(8,128)S(1)}, u32[]{:S(2)}, u32[]{:S(2)}) collective-permute-start(f32[3,1,32,128]{3,2,1,0:T(8,128)S(1)} %slice.489), channel_id=1, source_target_pairs={{0,1},{1,2},{2,3},{4,5},{5,6},{6,7},{8,9},{9,10},{10,11},{12,13},{... | collective-permute-start | bytes 147464 | tf_op jit(solution)/shard_map/ppermute | solution.py:19
  14.5 7.5 %collective-permute-start = (f32[1,8,32,1]{3,2,1,0:T(8,128)S(1)}, f32[1,8,32,1]{3,2,1,0:T(8,128)S(1)}, u32[]{:S(2)}, u32[]{:S(2)}) collective-permute-start(f32[1,8,32,1]{3,2,1,0:T(8,128)S(1)} %bitcast.68), channel_id=1, source_target_pairs={{8,0},{16,8},{24,16},{9,1},{17,9},{25,17},{10,2},{18,10},{26,18},{... | collective-permute-start | bytes 3080 | tf_op jit(solution)/shard_map/ppermute | solution.py:19
  18.2 1.0 copy-start
  21.9 6.6 %collective-permute-start.9 = (f32[3,8,32,1]{3,2,1,0:T(8,128)S(1)}, f32[3,8,32,1]{3,2,1,0:T(8,128)S(1)}, u32[]{:S(2)}, u32[]{:S(2)}) collective-permute-start(f32[3,8,32,1]{3,2,1,0:T(8,128)S(1)} %slice.483), channel_id=1, source_target_pairs={{0,8},{8,16},{16,24},{1,9},{9,17},{17,25},{2,10},{10,18},{18,26},{... | collective-permute-start | bytes 9224 | tf_op jit(solution)/shard_map/ppermute | solution.py:19
  23.9 4.7 %copy-start.5 = (f32[3,8,32,128]{3,2,1,0:T(8,128)S(1)}, f32[3,8,32,128]{3,2,1,0:T(8,128)}, u32[]{:S(2)}) copy-start(f32[3,8,32,128]{3,2,1,0:T(8,128)} %param.13) | copy-start | bytes 1179652
  29.3 1.1 copy-start.4
  29.4 1.0 copy-start.8
  31.3 9.6 %collective-permute-start.4 = (f32[1,8,1,128]{3,2,1,0:T(1,128)S(1)}, f32[1,8,1,128]{3,2,1,0:T(1,128)S(1)}, u32[]{:S(2)}, u32[]{:S(2)}) collective-permute-start(f32[1,8,1,128]{3,2,1,0:T(1,128)S(1)} %slice.601), channel_id=1, source_target_pairs={{0,4},{1,5},{2,6},{3,7},{8,12},{9,13},{10,14},{11,15},{16,20},{17,... | collective-permute-start | bytes 12296 | tf_op jit(solution)/shard_map/ppermute | solution.py:19
  32.6 8.3 %collective-permute-start.5 = (f32[1,1,32,128]{3,2,1,0:T(8,128)S(1)}, f32[1,1,32,128]{3,2,1,0:T(8,128)S(1)}, u32[]{:S(2)}, u32[]{:S(2)}) collective-permute-start(f32[1,1,32,128]{3,2,1,0:T(8,128)S(1)} %slice.604), channel_id=1, source_target_pairs={{0,1},{1,2},{2,3},{4,5},{5,6},{6,7},{8,9},{9,10},{10,11},{12,13},{... | collective-permute-start | bytes 49160 | tf_op jit(solution)/shard_map/ppermute | solution.py:19
  34.5 6.3 %collective-permute-start.3 = (f32[1,8,32,1]{3,2,1,0:T(8,128)S(1)}, f32[1,8,32,1]{3,2,1,0:T(8,128)S(1)}, u32[]{:S(2)}, u32[]{:S(2)}) collective-permute-start(f32[1,8,32,1]{3,2,1,0:T(8,128)S(1)} %slice.598), channel_id=1, source_target_pairs={{0,8},{8,16},{16,24},{1,9},{9,17},{17,25},{2,10},{10,18},{18,26},{... | collective-permute-start | bytes 3080 | tf_op jit(solution)/shard_map/ppermute | solution.py:19
  39.0 1.8 %copy-start.6 = (f32[8,32,128]{2,1,0:T(8,128)S(1)}, f32[8,32,128]{2,1,0:T(8,128)}, u32[]{:S(2)}) copy-start(f32[8,32,128]{2,1,0:T(8,128)} %param.9) | copy-start | bytes 393220
  39.0 1.8 %copy-start.7 = (f32[8,32,128]{2,1,0:T(8,128)S(1)}, f32[8,32,128]{2,1,0:T(8,128)}, u32[]{:S(2)}) copy-start(f32[8,32,128]{2,1,0:T(8,128)} %param.10) | copy-start | bytes 393220
  41.1 14.1 %collective-permute-start.7 = (f32[1,8,1,128]{3,2,1,0:T(1,128)S(1)}, f32[1,8,1,128]{3,2,1,0:T(1,128)S(1)}, u32[]{:S(2)}, u32[]{:S(2)}) collective-permute-start(f32[1,8,1,128]{3,2,1,0:T(1,128)S(1)} %slice.609), channel_id=1, source_target_pairs={{4,0},{5,1},{6,2},{7,3},{12,8},{13,9},{14,10},{15,11},{20,16},{21,... | collective-permute-start | bytes 12296 | tf_op jit(solution)/shard_map/ppermute | solution.py:19
  42.4 12.9 %collective-permute-start.8 = (f32[1,1,32,128]{3,2,1,0:T(8,128)S(1)}, f32[1,1,32,128]{3,2,1,0:T(8,128)S(1)}, u32[]{:S(2)}, u32[]{:S(2)}) collective-permute-start(f32[1,1,32,128]{3,2,1,0:T(8,128)S(1)} %slice.611), channel_id=1, source_target_pairs={{1,0},{2,1},{3,2},{5,4},{6,5},{7,6},{9,8},{10,9},{11,10},{13,12},{... | collective-permute-start | bytes 49160 | tf_op jit(solution)/shard_map/ppermute | solution.py:19
  46.0 7.3 %collective-permute-start.6 = (f32[1,8,32,1]{3,2,1,0:T(8,128)S(1)}, f32[1,8,32,1]{3,2,1,0:T(8,128)S(1)}, u32[]{:S(2)}, u32[]{:S(2)}) collective-permute-start(f32[1,8,32,1]{3,2,1,0:T(8,128)S(1)} %bitcast.73), channel_id=1, source_target_pairs={{8,0},{16,8},{24,16},{9,1},{17,9},{25,17},{10,2},{18,10},{26,18},{... | collective-permute-start | bytes 3080 | tf_op jit(solution)/shard_map/ppermute | solution.py:19
  48.1 14.4 %collective-permute-start.14 = (f32[3,1,32,128]{3,2,1,0:T(8,128)S(1)}, f32[3,1,32,128]{3,2,1,0:T(8,128)S(1)}, u32[]{:S(2)}, u32[]{:S(2)}) collective-permute-start(f32[3,1,32,128]{3,2,1,0:T(8,128)S(1)} %fusion.135), channel_id=1, source_target_pairs={{1,0},{2,1},{3,2},{5,4},{6,5},{7,6},{9,8},{10,9},{11,10},{13,12},{... | collective-permute-start | bytes 147464 | tf_op jit(solution)/shard_map/ppermute | solution.py:19
  50.1 12.3 %collective-permute-start.13 = (f32[3,8,1,128]{3,1,2,0:T(8,128)S(1)}, f32[3,8,1,128]{3,1,2,0:T(8,128)S(1)}, u32[]{:S(2)}, u32[]{:S(2)}) collective-permute-start(f32[3,8,1,128]{3,1,2,0:T(8,128)S(1)} %bitcast.81), channel_id=1, source_target_pairs={{4,0},{5,1},{6,2},{7,3},{12,8},{13,9},{14,10},{15,11},{20,16},{21,... | collective-permute-start | bytes 36872 | tf_op jit(solution)/shard_map/ppermute | solution.py:19
  53.3 9.1 %collective-permute-start.12 = (f32[3,8,32,1]{3,2,1,0:T(8,128)S(1)}, f32[3,8,32,1]{3,2,1,0:T(8,128)S(1)}, u32[]{:S(2)}, u32[]{:S(2)}) collective-permute-start(f32[3,8,32,1]{3,2,1,0:T(8,128)S(1)} %fusion.8), channel_id=1, source_target_pairs={{8,0},{16,8},{24,16},{9,1},{17,9},{25,17},{10,2},{18,10},{26,18},{... | collective-permute-start | bytes 9224 | tf_op jit(solution)/shard_map/ppermute | solution.py:19
  63.1 14.0 %collective-permute-start.22 = (f32[3,8,1,128]{3,1,2,0:T(8,128)S(1)}, f32[3,8,1,128]{3,1,2,0:T(8,128)S(1)}, u32[]{:S(2)}, u32[]{:S(2)}) collective-permute-start(f32[3,8,1,128]{3,1,2,0:T(8,128)S(1)} %bitcast.83), channel_id=1, source_target_pairs={{0,4},{1,5},{2,6},{3,7},{8,12},{9,13},{10,14},{11,15},{16,20},{17,... | collective-permute-start | bytes 36872 | tf_op jit(solution)/shard_map/ppermute | solution.py:19
  67.4 9.8 %collective-permute-start.23 = (f32[3,1,32,128]{3,2,1,0:T(8,128)S(1)}, f32[3,1,32,128]{3,2,1,0:T(8,128)S(1)}, u32[]{:S(2)}, u32[]{:S(2)}) collective-permute-start(f32[3,1,32,128]{3,2,1,0:T(8,128)S(1)} %slice.659), channel_id=1, source_target_pairs={{0,1},{1,2},{2,3},{4,5},{5,6},{6,7},{8,9},{9,10},{10,11},{12,13},{... | collective-permute-start | bytes 147464 | tf_op jit(solution)/shard_map/ppermute | solution.py:19
  70.1 7.0 %collective-permute-start.21 = (f32[3,8,32,1]{3,2,1,0:T(8,128)S(1)}, f32[3,8,32,1]{3,2,1,0:T(8,128)S(1)}, u32[]{:S(2)}, u32[]{:S(2)}) collective-permute-start(f32[3,8,32,1]{3,2,1,0:T(8,128)S(1)} %slice.653), channel_id=1, source_target_pairs={{0,8},{8,16},{16,24},{1,9},{9,17},{17,25},{2,10},{10,18},{18,26},{... | collective-permute-start | bytes 9224 | tf_op jit(solution)/shard_map/ppermute | solution.py:19
  78.7 9.6 %collective-permute-start.16 = (f32[1,8,1,128]{3,2,1,0:T(1,128)S(1)}, f32[1,8,1,128]{3,2,1,0:T(1,128)S(1)}, u32[]{:S(2)}, u32[]{:S(2)}) collective-permute-start(f32[1,8,1,128]{3,2,1,0:T(1,128)S(1)} %slice.642), channel_id=1, source_target_pairs={{0,4},{1,5},{2,6},{3,7},{8,12},{9,13},{10,14},{11,15},{16,20},{17,... | collective-permute-start | bytes 12296 | tf_op jit(solution)/shard_map/ppermute | solution.py:19
  79.9 8.3 %collective-permute-start.17 = (f32[1,1,32,128]{3,2,1,0:T(8,128)S(1)}, f32[1,1,32,128]{3,2,1,0:T(8,128)S(1)}, u32[]{:S(2)}, u32[]{:S(2)}) collective-permute-start(f32[1,1,32,128]{3,2,1,0:T(8,128)S(1)} %slice.645), channel_id=1, source_target_pairs={{0,1},{1,2},{2,3},{4,5},{5,6},{6,7},{8,9},{9,10},{10,11},{12,13},{... | collective-permute-start | bytes 49160 | tf_op jit(solution)/shard_map/ppermute | solution.py:19
  81.9 6.3 %collective-permute-start.15 = (f32[1,8,32,1]{3,2,1,0:T(8,128)S(1)}, f32[1,8,32,1]{3,2,1,0:T(8,128)S(1)}, u32[]{:S(2)}, u32[]{:S(2)}) collective-permute-start(f32[1,8,32,1]{3,2,1,0:T(8,128)S(1)} %slice.639), channel_id=1, source_target_pairs={{0,8},{8,16},{16,24},{1,9},{9,17},{17,25},{2,10},{10,18},{18,26},{... | collective-permute-start | bytes 3080 | tf_op jit(solution)/shard_map/ppermute | solution.py:19
  88.4 14.1 %collective-permute-start.19 = (f32[1,8,1,128]{3,2,1,0:T(1,128)S(1)}, f32[1,8,1,128]{3,2,1,0:T(1,128)S(1)}, u32[]{:S(2)}, u32[]{:S(2)}) collective-permute-start(f32[1,8,1,128]{3,2,1,0:T(1,128)S(1)} %slice.650), channel_id=1, source_target_pairs={{4,0},{5,1},{6,2},{7,3},{12,8},{13,9},{14,10},{15,11},{20,16},{21,... | collective-permute-start | bytes 12296 | tf_op jit(solution)/shard_map/ppermute | solution.py:19
  89.7 12.9 %collective-permute-start.20 = (f32[1,1,32,128]{3,2,1,0:T(8,128)S(1)}, f32[1,1,32,128]{3,2,1,0:T(8,128)S(1)}, u32[]{:S(2)}, u32[]{:S(2)}) collective-permute-start(f32[1,1,32,128]{3,2,1,0:T(8,128)S(1)} %slice.652), channel_id=1, source_target_pairs={{1,0},{2,1},{3,2},{5,4},{6,5},{7,6},{9,8},{10,9},{11,10},{13,12},{... | collective-permute-start | bytes 49160 | tf_op jit(solution)/shard_map/ppermute | solution.py:19
  93.4 7.3 %collective-permute-start.18 = (f32[1,8,32,1]{3,2,1,0:T(8,128)S(1)}, f32[1,8,32,1]{3,2,1,0:T(8,128)S(1)}, u32[]{:S(2)}, u32[]{:S(2)}) collective-permute-start(f32[1,8,32,1]{3,2,1,0:T(8,128)S(1)} %bitcast.72), channel_id=1, source_target_pairs={{8,0},{16,8},{24,16},{9,1},{17,9},{25,17},{10,2},{18,10},{26,18},{... | collective-permute-start | bytes 3080 | tf_op jit(solution)/shard_map/ppermute | solution.py:19
  95.4 14.4 %collective-permute-start.26 = (f32[3,1,32,128]{3,2,1,0:T(8,128)S(1)}, f32[3,1,32,128]{3,2,1,0:T(8,128)S(1)}, u32[]{:S(2)}, u32[]{:S(2)}) collective-permute-start(f32[3,1,32,128]{3,2,1,0:T(8,128)S(1)} %fusion.134), channel_id=1, source_target_pairs={{1,0},{2,1},{3,2},{5,4},{6,5},{7,6},{9,8},{10,9},{11,10},{13,12},{... | collective-permute-start | bytes 147464 | tf_op jit(solution)/shard_map/ppermute | solution.py:19
  97.9 11.8 %collective-permute-start.25 = (f32[3,8,1,128]{3,1,2,0:T(8,128)S(1)}, f32[3,8,1,128]{3,1,2,0:T(8,128)S(1)}, u32[]{:S(2)}, u32[]{:S(2)}) collective-permute-start(f32[3,8,1,128]{3,1,2,0:T(8,128)S(1)} %bitcast.82), channel_id=1, source_target_pairs={{4,0},{5,1},{6,2},{7,3},{12,8},{13,9},{14,10},{15,11},{20,16},{21,... | collective-permute-start | bytes 36872 | tf_op jit(solution)/shard_map/ppermute | solution.py:19
  100.7 9.1 %collective-permute-start.24 = (f32[3,8,32,1]{3,2,1,0:T(8,128)S(1)}, f32[3,8,32,1]{3,2,1,0:T(8,128)S(1)}, u32[]{:S(2)}, u32[]{:S(2)}) collective-permute-start(f32[3,8,32,1]{3,2,1,0:T(8,128)S(1)} %fusion.6), channel_id=1, source_target_pairs={{8,0},{16,8},{24,16},{9,1},{17,9},{25,17},{10,2},{18,10},{26,18},{... | collective-permute-start | bytes 9224 | tf_op jit(solution)/shard_map/ppermute | solution.py:19
  110.4 14.0 %collective-permute-start.31 = (f32[3,8,1,128]{3,1,2,0:T(8,128)S(1)}, f32[3,8,1,128]{3,1,2,0:T(8,128)S(1)}, u32[]{:S(2)}, u32[]{:S(2)}) collective-permute-start(f32[3,8,1,128]{3,1,2,0:T(8,128)S(1)} %bitcast.84), channel_id=1, source_target_pairs={{0,4},{1,5},{2,6},{3,7},{8,12},{9,13},{10,14},{11,15},{16,20},{17,... | collective-permute-start | bytes 36872 | tf_op jit(solution)/shard_map/ppermute | solution.py:19
  114.7 9.8 %collective-permute-start.32 = (f32[3,1,32,128]{3,2,1,0:T(8,128)S(1)}, f32[3,1,32,128]{3,2,1,0:T(8,128)S(1)}, u32[]{:S(2)}, u32[]{:S(2)}) collective-permute-start(f32[3,1,32,128]{3,2,1,0:T(8,128)S(1)} %slice.700), channel_id=1, source_target_pairs={{0,1},{1,2},{2,3},{4,5},{5,6},{6,7},{8,9},{9,10},{10,11},{12,13},{... | collective-permute-start | bytes 147464 | tf_op jit(solution)/shard_map/ppermute | solution.py:19
  117.5 7.0 %collective-permute-start.30 = (f32[3,8,32,1]{3,2,1,0:T(8,128)S(1)}, f32[3,8,32,1]{3,2,1,0:T(8,128)S(1)}, u32[]{:S(2)}, u32[]{:S(2)}) collective-permute-start(f32[3,8,32,1]{3,2,1,0:T(8,128)S(1)} %slice.694), channel_id=1, source_target_pairs={{0,8},{8,16},{16,24},{1,9},{9,17},{17,25},{2,10},{10,18},{18,26},{... | collective-permute-start | bytes 9224 | tf_op jit(solution)/shard_map/ppermute | solution.py:19
  125.5 0.9 copy-start.1
  126.6 14.1 %collective-permute-start.35 = (f32[3,1,32,128]{3,2,1,0:T(8,128)S(1)}, f32[3,1,32,128]{3,2,1,0:T(8,128)S(1)}, u32[]{:S(2)}, u32[]{:S(2)}) collective-permute-start(f32[3,1,32,128]{3,2,1,0:T(8,128)S(1)} %fusion.133), channel_id=1, source_target_pairs={{1,0},{2,1},{3,2},{5,4},{6,5},{7,6},{9,8},{10,9},{11,10},{13,12},{... | collective-permute-start | bytes 147464 | tf_op jit(solution)/shard_map/ppermute | solution.py:19
  129.2 11.5 %collective-permute-start.34 = (f32[3,8,1,128]{3,1,2,0:T(8,128)S(1)}, f32[3,8,1,128]{3,1,2,0:T(8,128)S(1)}, u32[]{:S(2)}, u32[]{:S(2)}) collective-permute-start(f32[3,8,1,128]{3,1,2,0:T(8,128)S(1)} %bitcast.85), channel_id=1, source_target_pairs={{4,0},{5,1},{6,2},{7,3},{12,8},{13,9},{14,10},{15,11},{20,16},{21,... | collective-permute-start | bytes 36872 | tf_op jit(solution)/shard_map/ppermute | solution.py:19
  130.5 10.2 %collective-permute-start.33 = (f32[3,8,32,1]{3,2,1,0:T(8,128)S(1)}, f32[3,8,32,1]{3,2,1,0:T(8,128)S(1)}, u32[]{:S(2)}, u32[]{:S(2)}) collective-permute-start(f32[3,8,32,1]{3,2,1,0:T(8,128)S(1)} %fusion.4), channel_id=1, source_target_pairs={{8,0},{16,8},{24,16},{9,1},{17,9},{25,17},{10,2},{18,10},{26,18},{... | collective-permute-start | bytes 9224 | tf_op jit(solution)/shard_map/ppermute | solution.py:19
  141.9 11.3 %copy-start.2 = (f32[3,8,32,128]{3,2,1,0:T(8,128)}, f32[3,8,32,128]{3,2,1,0:T(8,128)S(1)}, u32[]{:S(2)}) copy-start(f32[3,8,32,128]{3,2,1,0:T(8,128)S(1)} %get-tuple-element.17) | copy-start | bytes 1179652
  141.9 11.3 %collective-permute-start.29 = (f32[1,1,32,128]{3,2,1,0:T(8,128)S(1)}, f32[1,1,32,128]{3,2,1,0:T(8,128)S(1)}, u32[]{:S(2)}, u32[]{:S(2)}) collective-permute-start(f32[1,1,32,128]{3,2,1,0:T(8,128)S(1)} %slice.692), channel_id=1, source_target_pairs={{0,1},{1,2},{2,3},{4,5},{5,6},{6,7},{8,9},{9,10},{10,11},{12,13},{... | collective-permute-start | bytes 49160 | tf_op jit(solution)/shard_map/ppermute | solution.py:19
  144.7 8.6 %collective-permute-start.28 = (f32[1,8,1,128]{3,2,1,0:T(1,128)S(1)}, f32[1,8,1,128]{3,2,1,0:T(1,128)S(1)}, u32[]{:S(2)}, u32[]{:S(2)}) collective-permute-start(f32[1,8,1,128]{3,2,1,0:T(1,128)S(1)} %slice.689), channel_id=1, source_target_pairs={{0,4},{1,5},{2,6},{3,7},{8,12},{9,13},{10,14},{11,15},{16,20},{17,... | collective-permute-start | bytes 12296 | tf_op jit(solution)/shard_map/ppermute | solution.py:19
  149.0 4.2 %collective-permute-start.27 = (f32[1,8,32,1]{3,2,1,0:T(8,128)S(1)}, f32[1,8,32,1]{3,2,1,0:T(8,128)S(1)}, u32[]{:S(2)}, u32[]{:S(2)}) collective-permute-start(f32[1,8,32,1]{3,2,1,0:T(8,128)S(1)} %slice.686), channel_id=1, source_target_pairs={{0,8},{8,16},{16,24},{1,9},{9,17},{17,25},{2,10},{10,18},{18,26},{... | collective-permute-start | bytes 3080 | tf_op jit(solution)/shard_map/ppermute | solution.py:19
where the time goes:
time: 157 us; the launch traced here: 154 us
  starting transfers between devices  89.7 us (57%)
  waiting for transfers between devices  47.1 us (30%)
  other arithmetic  7.78 us (5%)
  local copies, waits for them, and re-layouts  7.62 us (5%)
  between operations  1.94 us (1%)
    ppermute x36, starting transfers between devices, passed_along(): return lax.ppermute(shard, axis, pairs)  89.7 us
    ppermute x36, waiting for transfers between devices, passed_along(): return lax.ppermute(shard, axis, pairs)  47.1 us
  transfers between devices with their start and end apart: 36, of which 12 were waited for; matrix products, arithmetic and copies ran while one was open for 3% of the time, Pallas kernels for 0%

commit v1 on v0

v1 whole, which is shorter than its diff:
```python
import functools
import itertools

import jax
import jax.numpy as jnp
from jax import lax
from jax.experimental import pallas as pl
from jax.experimental.pallas import tpu as pltpu
from jax.sharding import PartitionSpec as P

ITERS = 3
HALO = ITERS
ROW0 = 8
SLOT = 8
LANES = 128

first_alpha = 0.5
second_alpha = 1.0
dual_step = 0.2
primal_step = 0.2

AXES = ("gx", "gy", "gz")
FIELDS = 15
F, W, U, V, PF, QF = 0, 1, 2, 3, 6, 9
GROUPS = (FIELDS + 1) // 2


def spans(low):
    chosen = [(F, 2), (W, 2), (U, 3), (V, 3), (V + 1, 3), (V + 2, 3)]
    chosen += [(PF + i, 2 if low else 3) for i in range(3)]
    chosen += [(QF + i, 3 if low else 2) for i in range(6)]
    if not low:
        chosen += [(U, 3)]
    return [(field, 0 if low else -count, count) for field, count in chosen]


def entries(low):
    return [(field, first + i) for field, first, count in spans(low) for i in range(count)]


SENT = len(entries(True))


def colours(size):
    return ("even", "odd")[: min(size - 1, 2)]


def partner(place, colour, size):
    other = place ^ 1 if colour == "even" else ((place + 1) ^ 1) - 1
    return other if 0 <= other < size else None


def exchange(values, moves, sizes):
    pairs = []
    for place in itertools.product(*(range(sizes[axis]) for axis in AXES)):
        other = list(place)
        for axis, colour in moves.items():
            other[AXES.index(axis)] = partner(place[AXES.index(axis)], colour, sizes[axis])
        if None in other:
            spare = [axis for axis in AXES if axis not in moves and sizes[axis] % 2 == 0]
            if not spare:
                continue
            other = list(place)
            other[AXES.index(spare[0])] ^= 1
        source, target = 0, 0
        for axis, here, there in zip(AXES, place, other):
            source = source * sizes[axis] + here
            target = target * sizes[axis] + there
        pairs.append((source, target))
    return lax.ppermute(values, AXES, pairs)


def sends_low(colour, parity):
    return (colour == "even") == (parity == 1)


def colour_of(side, parity):
    return "even" if (side == "low") == (parity == 1) else "odd"


def pick(received, colour):
    return received.get(colour, received["even"])


def pack_z(extents, zs, pos, f, w, u, v, p, q, *rest):
    outs = dict(zip(zs, rest[: len(zs)]))
    sem = rest[len(zs)]
    nz = extents[0]

    def source(field, first, count):
        first = first % nz if first < 0 else first
        layers = pl.ds(first, count)
        if field < V:
            return (f, w, u)[field].at[layers]
        stacked, base = ((v, V), (p, PF), (q, QF))[(field >= PF) + (field >= QF)]
        return stacked.at[field - base, layers]

    for parity in (0, 1):

        @pl.when(pos[2] % 2 == parity)
        def _():
            copies = []
            for colour, out in outs.items():
                at = 0
                for field, first, count in spans(sends_low(colour, parity)):
                    copies.append(
                        pltpu.make_async_copy(source(field, first, count), out.at[pl.ds(at, count)], sem)
                    )
                    at += count
            for copy in copies:
                copy.start()
            for copy in copies:
                copy.wait()


def pack_own(extents, ys, zs, pos, f, w, u, v, p, q, ext, *rest):
    nz, ny, _ = extents
    rows = ny + 2 * ROW0
    combos = list(itertools.product(zs, ys))
    y_outs = dict(zip(ys, rest[: len(ys)]))
    yz_outs = dict(zip(combos, rest[len(ys) : len(ys) + len(combos)]))
    sem = rest[-1]
    own = (pl.ds(HALO, nz), pl.ds(ROW0, ny))
    copies = [
        pltpu.make_async_copy(array, ext.at[(field,) + own], sem)
        for field, array in ((F, f), (W, w), (U, u))
    ]
    copies += [
        pltpu.make_async_copy(array, ext.at[(pl.ds(field, count),) + own], sem)
        for field, array, count in ((V, v, 3), (PF, p, 3), (QF, q, 6))
    ]
    for copy in copies:
        copy.start()
    for copy in copies:
        copy.wait()
    flat = ext.reshape(FIELDS * (nz + 2 * HALO) * rows, LANES)

    def layer(side_layer, extent):
        return side_layer % extent

    for parity in (0, 1):

        @pl.when(pos[1] % 2 == parity)
        def _():
            for colour in ys:
                for i, (field, at) in enumerate(entries(sends_low(colour, parity))):
                    start = (field * (nz + 2 * HALO) + HALO) * rows + ROW0 + layer(at, ny)
                    y_outs[colour][i] = flat[pl.ds(start, nz, stride=rows), :]

    for z_parity, y_parity in itertools.product((0, 1), (0, 1)):

        @pl.when(jnp.logical_and(pos[2] % 2 == z_parity, pos[1] % 2 == y_parity))
        def _():
            for z_colour, y_colour in combos:
                first_row = ROW0 + (0 if sends_low(y_colour, y_parity) else ny - HALO)
                for i, (field, at) in enumerate(entries(sends_low(z_colour, z_parity))):
                    yz_outs[z_colour, y_colour][pl.ds(i * HALO, HALO), :] = ext[
                        field, HALO + layer(at, nz), pl.ds(first_row, HALO), :
                    ]


def tile_starts(ny):
    return [ROW0 - HALO + 8 * i for i in range(-(-(ny + 2 * HALO) // 8))]


def join_halo(extents, xs, ys, zs, pos, ext_in, *rest):
    del ext_in
    nz, ny, _ = extents
    rows = ny + 2 * ROW0
    levels = nz + 2 * HALO
    combos = list(itertools.product(zs, ys))
    z_got = dict(zip(zs, rest))
    rest = rest[len(zs) :]
    y_got = dict(zip(ys, rest))
    rest = rest[len(ys) :]
    yz_got = dict(zip(combos, rest))
    rest = rest[len(combos) :]
    ext, strip = rest[:2]
    x_outs = dict(zip(xs, rest[2:]))
    flat = ext.reshape(FIELDS * levels * rows, LANES)

    def placed(side, extent):
        if side == "low":
            return entries(False)
        return [(field, extent + at) for field, at in entries(True)]

    if zs:
        for parity in (0, 1):

            @pl.when(pos[2] % 2 == parity)
            def _():
                for side in ("low", "high"):
                    got = pick(z_got, colour_of(side, parity))
                    for i, (field, at) in list(enumerate(placed(side, nz)))[::-1]:
                        ext[field, HALO + at, pl.ds(ROW0, ny), :] = got[i]

    if ys:
        for parity in (0, 1):

            @pl.when(pos[1] % 2 == parity)
            def _():
                for side in ("low", "high"):
                    got = pick(y_got, colour_of(side, parity))
                    for i, (field, at) in list(enumerate(placed(side, ny)))[::-1]:
                        start = (field * levels + HALO) * rows + ROW0 + at
                        flat[pl.ds(start, nz, stride=rows), :] = got[i]

    if combos:
        for z_parity, y_parity in itertools.product((0, 1), (0, 1)):

            @pl.when(jnp.logical_and(pos[2] % 2 == z_parity, pos[1] % 2 == y_parity))
            def _():
                for z_side, y_side in itertools.product(("low", "high"), ("low", "high")):
                    z_colour, y_colour = colour_of(z_side, z_parity), colour_of(y_side, y_parity)
                    z_colour = z_colour if z_colour in zs else "even"
                    y_colour = y_colour if y_colour in ys else "even"
                    got = yz_got[z_colour, y_colour]
                    row = ROW0 + (-HALO if y_side == "low" else ny)
                    for i, (field, at) in list(enumerate(placed(z_side, nz)))[::-1]:
                        ext[field, HALO + at, pl.ds(row, HALO), :] = got[pl.ds(i * HALO, HALO), :]

    lane = lax.broadcasted_iota(jnp.int32, (8, LANES), 1)
    for row in tile_starts(ny):

        def gather(field, carry):
            total = jnp.zeros((8, LANES), jnp.float32)
            for level in range(levels):
                turned = pltpu.roll(ext[field, level, pl.ds(row, 8), :], level * SLOT + HALO, 1)
                here = lane < (level + 1) * SLOT
                total = jnp.where(jnp.logical_and(here, lane >= level * SLOT), turned, total)
            strip[field, pl.ds(row, 8), :] = total
            return carry

        lax.fori_loop(0, FIELDS, gather, 0)

    slot = lane % SLOT
    for colour in xs:
        low = (pos[0] % 2 == 1) if colour == "even" else (pos[0] % 2 == 0)
        turn = jnp.where(low, LANES - 3, 4)
        keep = jnp.where(low, slot - 3, 3 - slot) >= 0
        for group, row in itertools.product(range(GROUPS), tile_starts(ny)):
            mine = strip[2 * group, pl.ds(row, 8), :]
            if 2 * group + 1 < FIELDS:
                other = pltpu.roll(strip[2 * group + 1, pl.ds(row, 8), :], turn, 1)
                mine = jnp.where(keep, mine, other)
            x_outs[colour][group, pl.ds(row - tile_starts(ny)[0], 8), :] = mine


def shrink(total, bound):
    return lax.rsqrt(jnp.maximum(1.0, total * (1.0 / (bound * bound))))


def dual_step_of(bar, next_bar, prev_bar, p, q, upper, lower):
    t = [p[a] + upper[a] * (next_bar[a] - bar[0]) - bar[1 + a] for a in range(3)]
    scale = shrink(t[0] * t[0] + t[1] * t[1] + t[2] * t[2], first_alpha)
    d = [[lower[b] * (bar[1 + a] - prev_bar[b][a]) for a in range(3)] for b in range(3)]
    s = [q[a] + d[a][a] for a in range(3)]
    for i, (a, b) in enumerate(((0, 1), (0, 2), (1, 2))):
        s.append(q[3 + i] + 0.5 * (d[b][a] + d[a][b]))
    off = s[3] * s[3] + s[4] * s[4] + s[5] * s[5]
    q_scale = shrink(s[0] * s[0] + s[1] * s[1] + s[2] * s[2] + (off + off), second_alpha)
    return [value * scale for value in t], [value * q_scale for value in s]


ROWS_OF_Q = ((0, 3, 4), (3, 1, 5), (4, 5, 2))


def primal_step_of(u, v, a_map, b_map, p, q, prev_p, next_q, upper, lower):
    div = None
    for a in range(3):
        term = upper[a] * p[a] - lower[a] * prev_p[a]
        div = term if div is None else div + term
    new_u = (u + primal_step * div) * b_map + a_map
    new_v = []
    for a in range(3):
        total = p[a]
        for b in range(3):
            total = total + (upper[b] * next_q[b][a] - lower[b] * q[ROWS_OF_Q[b][a]])
        new_v.append(v[a] + primal_step * total)
    bar = [(2.0 * dual_step) * new_u - dual_step * u]
    bar += [(2.0 * dual_step) * new_v[a] - dual_step * v[a] for a in range(3)]
    return new_u, new_v, bar


def solve(extents, sizes, xs, pos, ext_in, strip_in, *rest):
    del ext_in
    nz, ny, nx = extents
    rows = ny + 2 * ROW0
    levels = nz + 2 * HALO
    x_got = dict(zip(xs, rest[: len(xs)]))
    ext, out_u, out_v, out_p, out_q, side, bars, side_bars, sem = rest[len(xs) :]
    starts = tile_starts(ny)
    lane = lax.broadcasted_iota(jnp.int32, (8, LANES), 1)
    sub = lax.broadcasted_iota(jnp.int32, (8, LANES), 0)
    slot = lane % SLOT
    f32 = jnp.float32

    def masks(places, full):
        upper = jnp.logical_and(places >= 0, places < full - 1)
        lower = jnp.logical_and(places > 0, places < full)
        return upper.astype(f32), lower.astype(f32)

    full = [sizes[axis] * extent for axis, extent in zip(AXES, (nx, ny, nz))]
    y_masks = [masks(pos[1] * ny + (row - ROW0) + sub, full[1]) for row in starts]
    x_main = masks(pos[0] * nx + lane, full[0])
    x_side = [masks(pos[0] * nx + first + slot, full[0]) for first in (-HALO, nx - HALO)]
    z_side = masks(pos[2] * nz - HALO + lane // SLOT, full[2])

    def z_main(level):
        place = pos[2] * nz - HALO + level
        upper = jnp.where(jnp.logical_and(place >= 0, place < full[2] - 1), 1.0, 0.0)
        lower = jnp.where(jnp.logical_and(place > 0, place < full[2]), 1.0, 0.0)
        return upper.astype(f32), lower.astype(f32)

    def fill(got_low, got_high):
        for field, (i, row) in itertools.product(range(FIELDS), enumerate(starts)):
            own = strip_in[field, pl.ds(row, 8), :]
            at = (field // 2, pl.ds(8 * i, 8), slice(None))
            low, high = got_low[at], got_high[at]
            if field % 2:
                low, high = pltpu.roll(low, LANES - 4, 1), pltpu.roll(high, 3, 1)
            side[field, 0, pl.ds(row, 8), :] = jnp.where(slot < HALO, low, own)
            side[field, 1, pl.ds(row, 8), :] = jnp.where(slot < HALO, own, high)

    for parity in (0, 1):

        @pl.when(pos[0] % 2 == parity)
        def _():
            fill(pick(x_got, colour_of("low", parity)), pick(x_got, colour_of("high", parity)))

    def prepare(load, store, store_bar):
        f, w = load(F), load(W)
        inverse = 1.0 / (1.0 + primal_step * w)
        store(F, (primal_step * w * f) * inverse)
        store(W, inverse)
        for a in range(4):
            store_bar(a, dual_step * load(U + a))

    def main_refs(level, row):
        at = (level, pl.ds(row, 8), slice(None))

        def load(field):
            return ext[(field,) + at]

        def store(field, value):
            ext[(field,) + at] = value

        def store_bar(a, value):
            bars[a, level + 1, pl.ds(row, 8), :] = value

        return load, store, store_bar

    def side_refs(which, row):
        at = (which, pl.ds(row, 8), slice(None))

        def load(field):
            return side[(field,) + at]

        def store(field, value):
            side[(field,) + at] = value

        def store_bar(a, value):
            side_bars[(a,) + at] = value

        return load, store, store_bar

    def prepare_level(level, carry):
        for row in starts:
            prepare(*main_refs(level, row))
        return carry

    for which, row in itertools.product((0, 1), starts):
        prepare(*side_refs(which, row))
    lax.fori_loop(0, levels, prepare_level, 0)

    first, last = lane == 0, lane == LANES - 1

    def from_low(values, level):
        return pltpu.roll(values, LANES - HALO + 1 - SLOT * level, 1)

    def from_high(values, level):
        return pltpu.roll(values, LANES - 1 - HALO - SLOT * level, 1)

    def dual_main(level, carry):
        z_upper, z_lower = z_main(level)
        for (i, row) in enumerate(starts):
            load, store, _ = main_refs(level, row)
            here = pl.ds(row, 8)
            bar = [bars[a, level + 1, here, :] for a in range(4)]
            edge = from_high(side_bars[0, 1, here, :], level)
            next_bar = [
                jnp.where(last, edge, pltpu.roll(bar[0], LANES - 1, 1)),
                bars[0, level + 1, pl.ds(row + 1, 8), :],
                bars[0, level + 2, here, :],
            ]
            prev_bar = [
                [
                    jnp.where(
                        first,
                        from_low(side_bars[1 + a, 0, here, :], level),
                        pltpu.roll(bar[1 + a], 1, 1),
                    )
                    for a in range(3)
                ],
                [bars[1 + a, level + 1, pl.ds(row - 1, 8), :] for a in range(3)],
                [bars[1 + a, level, here, :] for a in range(3)],
            ]
            p, q = dual_step_of(
                bar,
                next_bar,
                prev_bar,
                [load(PF + a) for a in range(3)],
                [load(QF + a) for a in range(6)],
                (x_main[0], y_masks[i][0], z_upper),
                (x_main[1], y_masks[i][1], z_lower),
            )
            for a in range(3):
                store(PF + a, p[a])
            for a in range(6):
                store(QF + a, q[a])
        return carry

    def primal_main(level, carry):
        z_upper, z_lower = z_main(level)
        for (i, row) in enumerate(starts):
            load, store, store_bar = main_refs(level, row)
            here = pl.ds(row, 8)
            p = [load(PF + a) for a in range(3)]
            q = [load(QF + a) for a in range(6)]
            prev_p = [
                jnp.where(first, from_low(side[PF, 0, here, :], level), pltpu.roll(p[0], 1, 1)),
                ext[PF + 1, level, pl.ds(row - 1, 8), :],
                ext[PF + 2, level - 1, here, :],
            ]
            next_q = [
                [
                    jnp.where(
                        last,
                        from_high(side[QF + j, 1, here, :], level),
                        pltpu.roll(q[j], LANES - 1, 1),
                    )
                    for j in ROWS_OF_Q[0]
                ],
                [ext[QF + j, level, pl.ds(row + 1, 8), :] for j in ROWS_OF_Q[1]],
                [ext[QF + j, level + 1, here, :] for j in ROWS_OF_Q[2]],
            ]
            new_u, new_v, bar = primal_step_of(
                load(U),
                [load(V + a) for a in range(3)],
                load(F),
                load(W),
                p,
                q,
                prev_p,
                next_q,
                (x_main[0], y_masks[i][0], z_upper),
                (x_main[1], y_masks[i][1], z_lower),
            )
            for a, value in enumerate([new_u] + new_v):
                store(U + a, value)
            for a in range(4):
                store_bar(a, bar[a])
        return carry

    def dual_side(which):
        updates = []
        for (i, row) in enumerate(starts):
            load, _, _ = side_refs(which, row)
            here = pl.ds(row, 8)
            bar = [side_bars[a, which, here, :] for a in range(4)]
            next_bar = [
                pltpu.roll(bar[0], LANES - 1, 1),
                side_bars[0, which, pl.ds(row + 1, 8), :],
                pltpu.roll(bar[0], LANES - SLOT, 1),
            ]
            prev_bar = [
                [pltpu.roll(bar[1 + a], 1, 1) for a in range(3)],
                [side_bars[1 + a, which, pl.ds(row - 1, 8), :] for a in range(3)],
                [pltpu.roll(bar[1 + a], SLOT, 1) for a in range(3)],
            ]
            p, q = dual_step_of(
                bar,
                next_bar,
                prev_bar,
                [load(PF + a) for a in range(3)],
                [load(QF + a) for a in range(6)],
                (x_side[which][0], y_masks[i][0], z_side[0]),
                (x_side[which][1], y_masks[i][1], z_side[1]),
            )
            for a, value in enumerate(p + q):
                side[PF + a, which, here, :] = value

    def primal_side(which):
        for (i, row) in enumerate(starts):
            load, store, store_bar = side_refs(which, row)
            here = pl.ds(row, 8)
            p = [load(PF + a) for a in range(3)]
            q = [load(QF + a) for a in range(6)]
            prev_p = [
                pltpu.roll(p[0], 1, 1),
                side[PF + 1, which, pl.ds(row - 1, 8), :],
                pltpu.roll(p[2], SLOT, 1),
            ]
            next_q = [
                [pltpu.roll(q[j], LANES - 1, 1) for j in ROWS_OF_Q[0]],
                [side[QF + j, which, pl.ds(row + 1, 8), :] for j in ROWS_OF_Q[1]],
                [pltpu.roll(q[j], LANES - SLOT, 1) for j in ROWS_OF_Q[2]],
            ]
            new_u, new_v, bar = primal_step_of(
                load(U),
                [load(V + a) for a in range(3)],
                load(F),
                load(W),
                p,
                q,
                prev_p,
                next_q,
                (x_side[which][0], y_masks[i][0], z_side[0]),
                (x_side[which][1], y_masks[i][1], z_side[1]),
            )
            for a, value in enumerate([new_u] + new_v):
                store(U + a, value)
            for a in range(4):
                store_bar(a, bar[a])

    def out_copies(fields):
        own = (pl.ds(HALO, nz), pl.ds(ROW0, ny))
        return [
            pltpu.make_async_copy(ext.at[(field,) + own], out, sem) for field, out in fields
        ]

    duals = [(pl.ds(PF, 3), out_p), (pl.ds(QF, 6), out_q)]
    primals = [(U, out_u), (pl.ds(V, 3), out_v)]

    def iteration(step, carry):
        lax.fori_loop(step, levels - step, dual_main, 0)
        for which in (0, 1):
            dual_side(which)

        @pl.when(step == ITERS - 1)
        def _():
            for copy in out_copies(duals):
                copy.start()

        lax.fori_loop(step + 1, levels - 1 - step, primal_main, 0)
        for which in (0, 1):
            primal_side(which)
        return carry

    lax.fori_loop(0, ITERS, iteration, 0)
    for copy in out_copies(primals):
        copy.start()
    for copy in out_copies(duals + primals):
        copy.wait()


def per_device(sizes, noisy_image, fidelity, primal_u, primal_v, dual_p, dual_q):
    nz, ny, nx = extents = noisy_image.shape
    levels, rows = nz + 2 * HALO, ny + 2 * ROW0
    assert nx == LANES and ny % 8 == 0 and levels * SLOT <= LANES
    assert min(nz, ny) >= HALO
    xs, ys, zs = (colours(sizes[axis]) for axis in AXES)
    combos = list(itertools.product(zs, ys))
    pos = jnp.stack([lax.axis_index(axis) for axis in AXES])
    args = (noisy_image, fidelity, primal_u, primal_v, dual_p, dual_q)
    f32 = jnp.float32
    smem = pl.BlockSpec(memory_space=pltpu.SMEM)
    anywhere = pl.BlockSpec(memory_space=pl.ANY)
    vmem = pl.BlockSpec(memory_space=pltpu.VMEM)

    def shaped(*shape):
        return jax.ShapeDtypeStruct(shape, f32)

    def call(body, ins, outs, out_specs, name, limit, **more):
        return pl.pallas_call(
            body,
            in_specs=ins,
            out_specs=out_specs,
            out_shape=outs,
            name=name,
            compiler_params=pltpu.CompilerParams(vmem_limit_bytes=limit * 1024 * 1024),
            **more,
        )

    z_pay = call(
        functools.partial(pack_z, extents, zs),
        [smem] + [anywhere] * 6,
        [shaped(SENT, ny, nx)] * len(zs),
        [vmem] * len(zs),
        "pack_z",
        8,
        scratch_shapes=[pltpu.SemaphoreType.DMA],
    )(pos, *args)
    z_got = [exchange(pay, {"gz": c}, sizes) for c, pay in zip(zs, z_pay)]

    strip_rows = 8 * len(tile_starts(ny))
    ext_shape = shaped(FIELDS, levels, rows, nx)
    own = call(
        functools.partial(pack_own, extents, ys, zs),
        [smem] + [anywhere] * 6,
        [ext_shape]
        + [shaped(SENT, nz, nx)] * len(ys)
        + [shaped(SENT * HALO, nx)] * len(combos),
        [vmem] * (1 + len(ys) + len(combos)),
        "pack_own",
        16,
        scratch_shapes=[pltpu.SemaphoreType.DMA],
    )(pos, *args)
    ext, y_pay, yz_pay = own[0], own[1 : 1 + len(ys)], own[1 + len(ys) :]
    yz_got = [exchange(pay, {"gz": a, "gy": b}, sizes) for (a, b), pay in zip(combos, yz_pay)]
    y_got = [exchange(pay, {"gy": c}, sizes) for c, pay in zip(ys, y_pay)]

    joined = call(
        functools.partial(join_halo, extents, xs, ys, zs),
        [smem] + [vmem] * (1 + len(zs) + len(ys) + len(combos)),
        [ext_shape, shaped(FIELDS, rows, nx)] + [shaped(GROUPS, strip_rows, nx)] * len(xs),
        [vmem] * (2 + len(xs)),
        "join_halo",
        20,
        input_output_aliases={1: 0},
    )(pos, ext, *z_got, *y_got, *yz_got)
    ext, strip, x_pay = joined[0], joined[1], joined[2:]
    x_got = [exchange(pay, {"gx": c}, sizes) for c, pay in zip(xs, x_pay)]

    solved = call(
        functools.partial(solve, extents, sizes, xs),
        [smem] + [vmem] * (2 + len(xs)),
        [ext_shape] + [shaped(*a.shape) for a in (primal_u, primal_v, dual_p, dual_q)],
        [vmem] + [anywhere] * 4,
        "solve",
        24,
        input_output_aliases={1: 0},
        scratch_shapes=[
            pltpu.VMEM((FIELDS, 2, rows, nx), f32),
            pltpu.VMEM((4, levels + 2, rows, nx), f32),
            pltpu.VMEM((4, 2, rows, nx), f32),
            pltpu.SemaphoreType.DMA,
        ],
    )(pos, ext, strip, *x_got)
    return tuple(solved[1:])


def solution(mesh):
    sizes = {axis: mesh.shape[axis] for axis in AXES}
    scalar, stacked = P("gz", "gy", "gx"), P(None, "gz", "gy", "gx")
    return jax.shard_map(
        functools.partial(per_device, sizes),
        mesh=mesh,
        in_specs=(scalar,) * 3 + (stacked,) * 3,
        out_specs=(scalar,) + (stacked,) * 3,
        check_vma=False,
    )
```

time: 157 us -> 54.1 us (0.34); the launches traced: 154 us -> 53.6 us
  starting transfers between devices: 89.7 us -> 7.91 us
  waiting for transfers between devices: 47.1 us -> 11.2 us
  Pallas kernels: 0 us -> 22.1 us
  other arithmetic: 7.78 us -> 0.08 us
  local copies, waits for them, and re-layouts: 7.62 us -> 11.7 us
    ppermute x36 -> x7, starting transfers between devices: 89.7 us -> 7.91 us  [exchange(): return lax.ppermute(values, AXES, pairs)]
    ppermute x36 -> x7, waiting for transfers between devices: 47.1 us -> 11.2 us  [exchange(): return lax.ppermute(values, AXES, pairs)]
    pallas_call x0 -> x4, Pallas kernels: none -> 22.1 us  [the longest x1 11.6 us: per_device(): call(functools.partial(solve, extents, sizes, xs), [smem] + [vmem] * (2 +...]
    unnamed x18 -> x24, local copies, waits for them, and re-layouts: 2.56 us -> 11.7 us
    slice x54 -> x0, local copies, waits for them, and re-layouts: 4.94 us -> none  [the longest x18 2.54 us: last_layer(): return lax.slice_in_dim(values, extent - 1, extent, axis=axis_dim)]
    reduce_sum x5 -> x0, other arithmetic: 1.77 us -> none  [project(): jnp.sum(weights * stacked * stacked, axis=0, keepdims=True)]
  transfers between devices with their start and end apart: 36 -> 7, of which waited for: 12 -> 3; matrix products, arithmetic and copies ran while one was open for 3% -> 0% of each run, Pallas kernels for 0% -> 2%
where the time goes in v1:
time: 54.1 us; the launch traced here: 53.6 us
  Pallas kernels  22.1 us (41%)
  local copies, waits for them, and re-layouts  11.7 us (22%)
  waiting for transfers between devices  11.2 us (21%)
  starting transfers between devices  7.91 us (15%)
  between operations  0.68 us (1%)
    unnamed x24, local copies, waits for them, and re-layouts  11.7 us
    pallas_call x1, Pallas kernels, per_device(): call(functools.partial(solve, extents, sizes, xs), [smem] + [vmem] * (2 +...  11.6 us
    ppermute x7, waiting for transfers between devices, exchange(): return lax.ppermute(values, AXES, pairs)  11.2 us
    ppermute x7, starting transfers between devices, exchange(): return lax.ppermute(values, AXES, pairs)  7.91 us
    pallas_call x1, Pallas kernels, per_device(): call(functools.partial(join_halo, extents, xs, ys, zs), [smem] + [vmem] *...  7.38 us
    pallas_call x1, Pallas kernels, per_device(): call(functools.partial(pack_z, extents, zs), [smem] + [anywhere] * 6, [sh...  2.27 us
  transfers between devices with their start and end apart: 7, of which 3 were waited for; matrix products, arithmetic and copies ran while one was open for 0% of the time, Pallas kernels for 2%

profile of v1, /device:TPU:17, one launch (start us, length us, event | category | flops | bytes accessed | tf_op | source)
XLA Modules:
  0.0 53.6 jit_solution(5270404245175721685)
XLA Ops:
  0.6 0.1 pad_add_fusion.pos
  0.7 0.0 copy-start
  0.7 1.1 %copy-done = f32[6,8,32,128]{3,2,1,0:T(8,128)S(1)} copy-done((f32[6,8,32,128]{3,2,1,0:T(8,128)S(1)}, f32[6,8,32,128]{3,2,1,0:T(8,128)}, u32[]{:S(2)}) %copy-start) | copy-done | bytes 786456
  1.8 0.0 copy-start.2
  1.9 1.0 %copy-done.2 = f32[3,8,32,128]{3,2,1,0:T(8,128)S(1)} copy-done((f32[3,8,32,128]{3,2,1,0:T(8,128)S(1)}, f32[3,8,32,128]{3,2,1,0:T(8,128)}, u32[]{:S(2)}) %copy-start.2) | copy-done | bytes 393240
  2.8 0.0 copy-start.4
  2.8 1.0 %copy-done.4 = f32[3,8,32,128]{3,2,1,0:T(8,128)S(1)} copy-done((f32[3,8,32,128]{3,2,1,0:T(8,128)S(1)}, f32[3,8,32,128]{3,2,1,0:T(8,128)}, u32[]{:S(2)}) %copy-start.4) | copy-done | bytes 393240
  3.8 0.0 copy-start.6
  3.8 0.9 %copy-done.6 = f32[8,32,128]{2,1,0:T(8,128)S(1)} copy-done((f32[8,32,128]{2,1,0:T(8,128)S(1)}, f32[8,32,128]{2,1,0:T(8,128)}, u32[]{:S(2)}) %copy-start.6) | copy-done | bytes 131096
  4.7 0.0 copy-start.8
  4.7 0.9 %copy-done.8 = f32[8,32,128]{2,1,0:T(8,128)S(1)} copy-done((f32[8,32,128]{2,1,0:T(8,128)S(1)}, f32[8,32,128]{2,1,0:T(8,128)}, u32[]{:S(2)}) %copy-start.8) | copy-done | bytes 131096
  5.7 0.0 copy-start.10
  5.7 0.9 %copy-done.10 = f32[8,32,128]{2,1,0:T(8,128)S(1)} copy-done((f32[8,32,128]{2,1,0:T(8,128)S(1)}, f32[8,32,128]{2,1,0:T(8,128)}, u32[]{:S(2)}) %copy-start.10) | copy-done | bytes 131096
  6.6 2.3 %pack_z.1 = (f32[40,32,128]{2,1,0:T(8,128)S(1)}, f32[40,32,128]{2,1,0:T(8,128)S(1)}) custom-call(s32[3]{0:T(128)S(1)} %pad_add_fusion.pos, f32[8,32,128]{2,1,0:T(8,128)S(1)} %copy-done.6, f32[8,32,128]{2,1,0:T(8,128)S(1)} %copy-done.8, f32[8,32,128]{2,1,0:T(8,128)S(1)} %copy-done.10, f32[3,8,32,128]{3,2,1,0:T(8,128)S(1)} %copy-done.2, ...), custom_call_target="tpu_custom_call" | custom-call | tf_op jit(solution)/shard_map/pack_z/pallas_call | solution.py:585
  8.8 1.4 %collective-permute-start = (f32[40,32,128]{2,1,0:T(8,128)S(1)}, f32[40,32,128]{2,1,0:T(8,128)S(1)}, u32[]{:S(2)}, u32[]{:S(2)}) collective-permute-start(f32[40,32,128]{2,1,0:T(8,128)S(1)} %get-tuple-element.19), channel_id=1, source_target_pairs={{0,1},{1,0},{2,3},{3,2},{4,5},{5,4},{6,7},{7,6},{8,9},{9,8},{10,11... | collective-permute-start | bytes 1966088 | tf_op jit(solution)/shard_map/ppermute | solution.py:70
  10.2 0.0 collective-permute-start.1
  10.2 0.0 copy-start.1
  10.2 1.1 %copy-done.1 = f32[6,8,32,128]{3,2,1,0:T(8,128)S(1)} copy-done((f32[6,8,32,128]{3,2,1,0:T(8,128)S(1)}, f32[6,8,32,128]{3,2,1,0:T(8,128)}, u32[]{:S(2)}) %copy-start.1) | copy-done | bytes 786456
  11.3 0.0 copy-start.3
  11.3 1.0 %copy-done.3 = f32[3,8,32,128]{3,2,1,0:T(8,128)S(1)} copy-done((f32[3,8,32,128]{3,2,1,0:T(8,128)S(1)}, f32[3,8,32,128]{3,2,1,0:T(8,128)}, u32[]{:S(2)}) %copy-start.3) | copy-done | bytes 393240
  12.3 0.0 copy-start.5
  12.3 1.0 %copy-done.5 = f32[3,8,32,128]{3,2,1,0:T(8,128)S(1)} copy-done((f32[3,8,32,128]{3,2,1,0:T(8,128)S(1)}, f32[3,8,32,128]{3,2,1,0:T(8,128)}, u32[]{:S(2)}) %copy-start.5) | copy-done | bytes 393240
  13.3 0.0 copy-start.7
  13.3 0.9 %copy-done.7 = f32[8,32,128]{2,1,0:T(8,128)S(1)} copy-done((f32[8,32,128]{2,1,0:T(8,128)S(1)}, f32[8,32,128]{2,1,0:T(8,128)}, u32[]{:S(2)}) %copy-start.7) | copy-done | bytes 131096
  14.2 0.0 copy-start.9
  14.2 0.9 %copy-done.9 = f32[8,32,128]{2,1,0:T(8,128)S(1)} copy-done((f32[8,32,128]{2,1,0:T(8,128)S(1)}, f32[8,32,128]{2,1,0:T(8,128)}, u32[]{:S(2)}) %copy-start.9) | copy-done | bytes 131096
  15.1 0.0 copy-start.11
  15.1 0.9 %copy-done.11 = f32[8,32,128]{2,1,0:T(8,128)S(1)} copy-done((f32[8,32,128]{2,1,0:T(8,128)S(1)}, f32[8,32,128]{2,1,0:T(8,128)}, u32[]{:S(2)}) %copy-start.11) | copy-done | bytes 131096
  16.0 0.9 %pack_own.1 = (f32[15,14,48,128]{3,2,1,0:T(8,128)S(1)}, f32[40,8,128]{2,1,0:T(8,128)S(1)}, f32[120,128]{1,0:T(8,128)S(1)}, f32[120,128]{1,0:T(8,128)S(1)}) custom-call(s32[3]{0:T(128)S(1)} %pad_add_fusion.pos, f32[8,32,128]{2,1,0:T(8,128)S(1)} %copy-done.7, f32[8,32,128]{2,1,0:T(8,128)S(1)} %copy-done.9, f32[8,32,128]{2,1,0:T(8,128)S(1)} %copy-done.11, ...), custom_call_target="tpu_custom_call" | custom-call | tf_op jit(solution)/shard_map/pack_own/pallas_call | solution.py:598
  16.9 1.3 %collective-permute-start.2 = (f32[40,8,128]{2,1,0:T(8,128)S(1)}, f32[40,8,128]{2,1,0:T(8,128)S(1)}, u32[]{:S(2)}, u32[]{:S(2)}) collective-permute-start(f32[40,8,128]{2,1,0:T(8,128)S(1)} %get-tuple-element.21), channel_id=1, source_target_pairs={{0,4},{1,5},{2,6},{3,7},{4,0},{5,1},{6,2},{7,3},{8,12},{9,13},{10,... | collective-permute-start | bytes 491528 | tf_op jit(solution)/shard_map/ppermute | solution.py:70
  18.2 1.1 %collective-permute-start.3 = (f32[120,128]{1,0:T(8,128)S(1)}, f32[120,128]{1,0:T(8,128)S(1)}, u32[]{:S(2)}, u32[]{:S(2)}) collective-permute-start(f32[120,128]{1,0:T(8,128)S(1)} %get-tuple-element.22), channel_id=1, source_target_pairs={{0,5},{1,4},{2,7},{3,6},{4,1},{5,0},{6,3},{7,2},{8,13},{9,12},{10,... | collective-permute-start | bytes 184328 | tf_op jit(solution)/shard_map/ppermute | solution.py:70
  19.3 1.1 %collective-permute-start.4 = (f32[120,128]{1,0:T(8,128)S(1)}, f32[120,128]{1,0:T(8,128)S(1)}, u32[]{:S(2)}, u32[]{:S(2)}) collective-permute-start(f32[120,128]{1,0:T(8,128)S(1)} %get-tuple-element.23), channel_id=1, source_target_pairs={{0,8},{1,6},{2,5},{3,11},{4,12},{5,2},{6,1},{7,15},{8,0},{9,14},{1... | collective-permute-start | bytes 184328 | tf_op jit(solution)/shard_map/ppermute | solution.py:70
  20.4 6.1 %collective-permute-done.3.rest_3_ = f32[120,128]{1,0:T(8,128)S(1)} collective-permute-done((f32[120,128]{1,0:T(8,128)S(1)}, f32[120,128]{1,0:T(8,128)S(1)}, u32[]{:S(2)}, u32[]{:S(2)}) %collective-permute-start.3) | collective-permute-done | bytes 61472 | tf_op jit(solution)/shard_map/ppermute | solution.py:70
  26.5 1.3 %collective-permute-done.4.rest_4_ = f32[120,128]{1,0:T(8,128)S(1)} collective-permute-done((f32[120,128]{1,0:T(8,128)S(1)}, f32[120,128]{1,0:T(8,128)S(1)}, u32[]{:S(2)}, u32[]{:S(2)}) %collective-permute-start.4) | collective-permute-done | bytes 61472 | tf_op jit(solution)/shard_map/ppermute | solution.py:70
  27.8 0.0 collective-permute-done.2.rest_2_
  27.8 0.0 collective-permute-done.rest_0_
  27.8 0.0 collective-permute-done.1.rest_1_
  27.8 7.4 %join_halo.1 = (f32[15,14,48,128]{3,2,1,0:T(8,128)S(1)}, f32[15,48,128]{2,1,0:T(8,128)S(1)}, f32[8,40,128]{2,1,0:T(8,128)S(1)}, f32[8,40,128]{2,1,0:T(8,128)S(1)}) custom-call(s32[3]{0:T(128)S(1)} %pad_add_fusion.pos, f32[15,14,48,128]{3,2,1,0:T(8,128)S(1)} %get-tuple-element.18.ext_in, ...), custom_call_target="tpu_custom_call", output_to_operand_aliasing={{0}: (1, {})} | custom-call | tf_op jit(solution)/shard_map/join_halo/pallas_call | solution.py:613
  35.2 1.9 %collective-permute-start.5 = (f32[8,40,128]{2,1,0:T(8,128)S(1)}, f32[8,40,128]{2,1,0:T(8,128)S(1)}, u32[]{:S(2)}, u32[]{:S(2)}) collective-permute-start(f32[8,40,128]{2,1,0:T(8,128)S(1)} %get-tuple-element.26), channel_id=1, source_target_pairs={{0,8},{1,9},{2,10},{3,11},{4,12},{5,13},{6,14},{7,15},{8,0},{9,1},... | collective-permute-start | bytes 491528 | tf_op jit(solution)/shard_map/ppermute | solution.py:70
  37.1 1.2 %collective-permute-start.6 = (f32[8,40,128]{2,1,0:T(8,128)S(1)}, f32[8,40,128]{2,1,0:T(8,128)S(1)}, u32[]{:S(2)}, u32[]{:S(2)}) collective-permute-start(f32[8,40,128]{2,1,0:T(8,128)S(1)} %get-tuple-element.27), channel_id=1, source_target_pairs={{0,4},{1,5},{2,6},{3,7},{4,0},{5,1},{6,2},{7,3},{8,16},{9,17},{10,... | collective-permute-start | bytes 491528 | tf_op jit(solution)/shard_map/ppermute | solution.py:70
  38.3 0.0 collective-permute-done.5.rest_0_
  38.3 3.8 %collective-permute-done.6.rest_1_ = f32[8,40,128]{2,1,0:T(8,128)S(1)} collective-permute-done((f32[8,40,128]{2,1,0:T(8,128)S(1)}, f32[8,40,128]{2,1,0:T(8,128)S(1)}, u32[]{:S(2)}, u32[]{:S(2)}) %collective-permute-start.6) | collective-permute-done | bytes 163872 | tf_op jit(solution)/shard_map/ppermute | solution.py:70
  42.1 11.6 %solve.1 = (f32[15,14,48,128]{3,2,1,0:T(8,128)S(1)}, f32[8,32,128]{2,1,0:T(8,128)}, f32[3,8,32,128]{3,2,1,0:T(8,128)}, f32[3,8,32,128]{3,2,1,0:T(8,128)}, f32[6,8,32,128]{3,2,1,0:T(8,128)}) custom-call(s32[3]{0:T(128)S(1)} %pad_add_fusion.pos, f32[15,14,48,128]{3,2,1,0:T(8,128)S(1)} %get-tuple-element.24.ext_in, ...), custom_call_target="tpu_custom_call", output_to_operand_aliasing={{0}: (1, {})} | custom-call | tf_op jit(solution)/shard_map/solve/pallas_call | solution.py:625
Async XLA Ops:
  0.7 1.1 %copy-start = (f32[6,8,32,128]{3,2,1,0:T(8,128)S(1)}, f32[6,8,32,128]{3,2,1,0:T(8,128)}, u32[]{:S(2)}) copy-start(f32[6,8,32,128]{3,2,1,0:T(8,128)} %q.3) | copy-start | bytes 2359300
  1.8 1.0 %copy-start.2 = (f32[3,8,32,128]{3,2,1,0:T(8,128)S(1)}, f32[3,8,32,128]{3,2,1,0:T(8,128)}, u32[]{:S(2)}) copy-start(f32[3,8,32,128]{3,2,1,0:T(8,128)} %v.3) | copy-start | bytes 1179652
  2.8 1.0 %copy-start.4 = (f32[3,8,32,128]{3,2,1,0:T(8,128)S(1)}, f32[3,8,32,128]{3,2,1,0:T(8,128)}, u32[]{:S(2)}) copy-start(f32[3,8,32,128]{3,2,1,0:T(8,128)} %p.3) | copy-start | bytes 1179652
  3.8 0.9 %copy-start.6 = (f32[8,32,128]{2,1,0:T(8,128)S(1)}, f32[8,32,128]{2,1,0:T(8,128)}, u32[]{:S(2)}) copy-start(f32[8,32,128]{2,1,0:T(8,128)} %f.3) | copy-start | bytes 393220
  4.7 0.9 %copy-start.8 = (f32[8,32,128]{2,1,0:T(8,128)S(1)}, f32[8,32,128]{2,1,0:T(8,128)}, u32[]{:S(2)}) copy-start(f32[8,32,128]{2,1,0:T(8,128)} %w.3) | copy-start | bytes 393220
  5.7 0.9 %copy-start.10 = (f32[8,32,128]{2,1,0:T(8,128)S(1)}, f32[8,32,128]{2,1,0:T(8,128)}, u32[]{:S(2)}) copy-start(f32[8,32,128]{2,1,0:T(8,128)} %u.3) | copy-start | bytes 393220
  8.8 19.0 %collective-permute-start = (f32[40,32,128]{2,1,0:T(8,128)S(1)}, f32[40,32,128]{2,1,0:T(8,128)S(1)}, u32[]{:S(2)}, u32[]{:S(2)}) collective-permute-start(f32[40,32,128]{2,1,0:T(8,128)S(1)} %get-tuple-element.19), channel_id=1, source_target_pairs={{0,1},{1,0},{2,3},{3,2},{4,5},{5,4},{6,7},{7,6},{8,9},{9,8},{10,11... | collective-permute-start | bytes 1966088 | tf_op jit(solution)/shard_map/ppermute | solution.py:70
  10.2 17.6 %collective-permute-start.1 = (f32[40,32,128]{2,1,0:T(8,128)S(1)}, f32[40,32,128]{2,1,0:T(8,128)S(1)}, u32[]{:S(2)}, u32[]{:S(2)}) collective-permute-start(f32[40,32,128]{2,1,0:T(8,128)S(1)} %get-tuple-element.20), channel_id=1, source_target_pairs={{0,8},{1,2},{2,1},{3,11},{4,12},{5,6},{6,5},{7,15},{8,0},{9,10},{1... | collective-permute-start | bytes 1966088 | tf_op jit(solution)/shard_map/ppermute | solution.py:70
  10.2 1.1 %copy-start.1 = (f32[6,8,32,128]{3,2,1,0:T(8,128)S(1)}, f32[6,8,32,128]{3,2,1,0:T(8,128)}, u32[]{:S(2)}) copy-start(f32[6,8,32,128]{3,2,1,0:T(8,128)} %q.3) | copy-start | bytes 2359300
  11.3 1.0 %copy-start.3 = (f32[3,8,32,128]{3,2,1,0:T(8,128)S(1)}, f32[3,8,32,128]{3,2,1,0:T(8,128)}, u32[]{:S(2)}) copy-start(f32[3,8,32,128]{3,2,1,0:T(8,128)} %v.3) | copy-start | bytes 1179652
  12.3 1.0 %copy-start.5 = (f32[3,8,32,128]{3,2,1,0:T(8,128)S(1)}, f32[3,8,32,128]{3,2,1,0:T(8,128)}, u32[]{:S(2)}) copy-start(f32[3,8,32,128]{3,2,1,0:T(8,128)} %p.3) | copy-start | bytes 1179652
  13.3 0.9 %copy-start.7 = (f32[8,32,128]{2,1,0:T(8,128)S(1)}, f32[8,32,128]{2,1,0:T(8,128)}, u32[]{:S(2)}) copy-start(f32[8,32,128]{2,1,0:T(8,128)} %f.3) | copy-start | bytes 393220
  14.2 0.9 %copy-start.9 = (f32[8,32,128]{2,1,0:T(8,128)S(1)}, f32[8,32,128]{2,1,0:T(8,128)}, u32[]{:S(2)}) copy-start(f32[8,32,128]{2,1,0:T(8,128)} %w.3) | copy-start | bytes 393220
  15.1 0.9 %copy-start.11 = (f32[8,32,128]{2,1,0:T(8,128)S(1)}, f32[8,32,128]{2,1,0:T(8,128)}, u32[]{:S(2)}) copy-start(f32[8,32,128]{2,1,0:T(8,128)} %u.3) | copy-start | bytes 393220
  16.9 10.8 %collective-permute-start.2 = (f32[40,8,128]{2,1,0:T(8,128)S(1)}, f32[40,8,128]{2,1,0:T(8,128)S(1)}, u32[]{:S(2)}, u32[]{:S(2)}) collective-permute-start(f32[40,8,128]{2,1,0:T(8,128)S(1)} %get-tuple-element.21), channel_id=1, source_target_pairs={{0,4},{1,5},{2,6},{3,7},{4,0},{5,1},{6,2},{7,3},{8,12},{9,13},{10,... | collective-permute-start | bytes 491528 | tf_op jit(solution)/shard_map/ppermute | solution.py:70
  18.2 8.3 %collective-permute-start.3 = (f32[120,128]{1,0:T(8,128)S(1)}, f32[120,128]{1,0:T(8,128)S(1)}, u32[]{:S(2)}, u32[]{:S(2)}) collective-permute-start(f32[120,128]{1,0:T(8,128)S(1)} %get-tuple-element.22), channel_id=1, source_target_pairs={{0,5},{1,4},{2,7},{3,6},{4,1},{5,0},{6,3},{7,2},{8,13},{9,12},{10,... | collective-permute-start | bytes 184328 | tf_op jit(solution)/shard_map/ppermute | solution.py:70
  19.3 8.5 %collective-permute-start.4 = (f32[120,128]{1,0:T(8,128)S(1)}, f32[120,128]{1,0:T(8,128)S(1)}, u32[]{:S(2)}, u32[]{:S(2)}) collective-permute-start(f32[120,128]{1,0:T(8,128)S(1)} %get-tuple-element.23), channel_id=1, source_target_pairs={{0,8},{1,6},{2,5},{3,11},{4,12},{5,2},{6,1},{7,15},{8,0},{9,14},{1... | collective-permute-start | bytes 184328 | tf_op jit(solution)/shard_map/ppermute | solution.py:70
  35.2 3.1 %collective-permute-start.5 = (f32[8,40,128]{2,1,0:T(8,128)S(1)}, f32[8,40,128]{2,1,0:T(8,128)S(1)}, u32[]{:S(2)}, u32[]{:S(2)}) collective-permute-start(f32[8,40,128]{2,1,0:T(8,128)S(1)} %get-tuple-element.26), channel_id=1, source_target_pairs={{0,8},{1,9},{2,10},{3,11},{4,12},{5,13},{6,14},{7,15},{8,0},{9,1},... | collective-permute-start | bytes 491528 | tf_op jit(solution)/shard_map/ppermute | solution.py:70
  37.1 5.0 %collective-permute-start.6 = (f32[8,40,128]{2,1,0:T(8,128)S(1)}, f32[8,40,128]{2,1,0:T(8,128)S(1)}, u32[]{:S(2)}, u32[]{:S(2)}) collective-permute-start(f32[8,40,128]{2,1,0:T(8,128)S(1)} %get-tuple-element.27), channel_id=1, source_target_pairs={{0,4},{1,5},{2,6},{3,7},{4,0},{5,1},{6,2},{7,3},{8,16},{9,17},{10,... | collective-permute-start | bytes 491528 | tf_op jit(solution)/shard_map/ppermute | solution.py:70

commit v2 on v1

--- a/solution.py
+++ b/solution.py
@@ -220,18 +220,16 @@
                         ext[field, HALO + at, pl.ds(row, HALO), :] = got[pl.ds(i * HALO, HALO), :]
 
     lane = lax.broadcasted_iota(jnp.int32, (8, LANES), 1)
-    for row in tile_starts(ny):
-
-        def gather(field, carry):
+    def gather(field, carry):
+        for row in tile_starts(ny):
             total = jnp.zeros((8, LANES), jnp.float32)
             for level in range(levels):
                 turned = pltpu.roll(ext[field, level, pl.ds(row, 8), :], level * SLOT + HALO, 1)
-                here = lane < (level + 1) * SLOT
-                total = jnp.where(jnp.logical_and(here, lane >= level * SLOT), turned, total)
+                total = jnp.where(lane >= level * SLOT, turned, total)
             strip[field, pl.ds(row, 8), :] = total
-            return carry
-
-        lax.fori_loop(0, FIELDS, gather, 0)
+        return carry
+
+    lax.fori_loop(0, FIELDS, gather, 0)
 
     slot = lane % SLOT
     for colour in xs:
@@ -364,6 +362,16 @@
 
         return load, store, store_bar
 
+    def paired_loop(start, stop, body):
+        many = 2 if levels % 2 == 0 else 1
+
+        def trip(i, carry):
+            for j in range(many):
+                body(start + many * i + j, carry)
+            return carry
+
+        lax.fori_loop(0, (stop - start) // many, trip, 0)
+
     def prepare_level(level, carry):
         for row in starts:
             prepare(*main_refs(level, row))
@@ -371,7 +379,7 @@
 
     for which, row in itertools.product((0, 1), starts):
         prepare(*side_refs(which, row))
-    lax.fori_loop(0, levels, prepare_level, 0)
+    paired_loop(0, levels, prepare_level)
 
     first, last = lane == 0, lane == LANES - 1
 
@@ -533,7 +541,7 @@
     primals = [(U, out_u), (pl.ds(V, 3), out_v)]
 
     def iteration(step, carry):
-        lax.fori_loop(step, levels - step, dual_main, 0)
+        paired_loop(step, levels - step, dual_main)
         for which in (0, 1):
             dual_side(which)
 
@@ -542,7 +550,7 @@
             for copy in out_copies(duals):
                 copy.start()
 
-        lax.fori_loop(step + 1, levels - 1 - step, primal_main, 0)
+        paired_loop(step + 1, levels - 1 - step, primal_main)
         for which in (0, 1):
             primal_side(which)
         return carry
@@ -562,10 +570,10 @@
     xs, ys, zs = (colours(sizes[axis]) for axis in AXES)
     combos = list(itertools.product(zs, ys))
     pos = jnp.stack([lax.axis_index(axis) for axis in AXES])
-    args = (noisy_image, fidelity, primal_u, primal_v, dual_p, dual_q)
+    args = tuple(pltpu.with_memory_space_constraint(a, pltpu.HBM) for a in (noisy_image, fidelity, primal_u, primal_v, dual_p, dual_q))
     f32 = jnp.float32
     smem = pl.BlockSpec(memory_space=pltpu.SMEM)
-    anywhere = pl.BlockSpec(memory_space=pl.ANY)
+    anywhere = pl.BlockSpec(memory_space=pltpu.HBM)
     vmem = pl.BlockSpec(memory_space=pltpu.VMEM)
 
     def shaped(*shape):

time: 54.1 us -> 40.8 us (0.75)
  local copies, waits for them, and re-layouts: 11.7 us -> 0 us
  Pallas kernels: 22.1 us -> 16.2 us
  waiting for transfers between devices: 11.2 us -> 15.7 us
    unnamed x24 -> x0, local copies, waits for them, and re-layouts: 11.7 us -> none
    ppermute x7, waiting for transfers between devices: 11.2 us -> 15.7 us  [exchange(): return lax.ppermute(values, AXES, pairs)]
    pallas_call x1, Pallas kernels: 7.38 us -> 3.12 us  [per_device(): call(functools.partial(join_halo, extents, xs, ys, zs), [smem] + [vmem] *...]
    pallas_call x1, Pallas kernels: 11.6 us -> 9.03 us  [per_device(): call(functools.partial(solve, extents, sizes, xs), [smem] + [vmem] * (2 +...]
    pallas_call x1, Pallas kernels: 0.89 us -> 2.26 us  [per_device(): call(functools.partial(pack_own, extents, ys, zs), [smem] + [anywhere] *...]
  transfers between devices with their start and end apart: 7 -> 7, of which waited for: 3 -> 3; matrix products, arithmetic and copies ran while one was open for 0% -> 0% of each run, Pallas kernels for 2% -> 6%
where the time goes in v2:
time: 40.8 us; the launch traced here: 40.6 us
  Pallas kernels  16.2 us (40%)
  waiting for transfers between devices  15.7 us (38%)
  starting transfers between devices  7.92 us (19%)
  between operations  0.67 us (2%)
    ppermute x7, waiting for transfers between devices, exchange(): return lax.ppermute(values, AXES, pairs)  15.7 us
    pallas_call x1, Pallas kernels, per_device(): call(functools.partial(solve, extents, sizes, xs), [smem] + [vmem] * (2 +...  9.03 us
    ppermute x7, starting transfers between devices, exchange(): return lax.ppermute(values, AXES, pairs)  7.92 us
    pallas_call x1, Pallas kernels, per_device(): call(functools.partial(join_halo, extents, xs, ys, zs), [smem] + [vmem] *...  3.12 us
    pallas_call x1, Pallas kernels, per_device(): call(functools.partial(pack_own, extents, ys, zs), [smem] + [anywhere] *...  2.26 us
    pallas_call x1, Pallas kernels, per_device(): call(functools.partial(pack_z, extents, zs), [smem] + [anywhere] * 6, [sh...  1.83 us
  transfers between devices with their start and end apart: 7, of which 3 were waited for; matrix products, arithmetic and copies ran while one was open for 0% of the time, Pallas kernels for 6%

profile of v2, /device:TPU:17, one launch (start us, length us, event | category | flops | bytes accessed | tf_op | source)
XLA Modules:
  0.0 40.6 jit_solution(18382617897425517530)
XLA Ops:
  0.6 0.1 pad_add_fusion.pos
  0.7 1.8 %pack_z.1 = (f32[40,32,128]{2,1,0:T(8,128)S(1)}, f32[40,32,128]{2,1,0:T(8,128)S(1)}) custom-call(s32[3]{0:T(128)S(1)} %pad_add_fusion.pos, f32[8,32,128]{2,1,0:T(8,128)} %f.3, f32[8,32,128]{2,1,0:T(8,128)} %w.3, f32[8,32,128]{2,1,0:T(8,128)} %u.3, f32[3,8,32,128]{3,2,1,0:T(8,128)} %v.3, f32[3,8,32,128]{3,2,1,0:T(8,128)} %p.3, f32[6,8,32,128]{3,2,1,0:T(8,128)} %q.3), custom_call_target="tpu_custom_call" | custom-call | tf_op jit(solution)/shard_map/pack_z/pallas_call | solution.py:593
  2.6 1.4 %collective-permute-start = (f32[40,32,128]{2,1,0:T(8,128)S(1)}, f32[40,32,128]{2,1,0:T(8,128)S(1)}, u32[]{:S(2)}, u32[]{:S(2)}) collective-permute-start(f32[40,32,128]{2,1,0:T(8,128)S(1)} %get-tuple-element.19), channel_id=1, source_target_pairs={{0,1},{1,0},{2,3},{3,2},{4,5},{5,4},{6,7},{7,6},{8,9},{9,8},{10,11... | collective-permute-start | bytes 1966088 | tf_op jit(solution)/shard_map/ppermute | solution.py:70
  3.9 0.0 collective-permute-start.1
  3.9 2.3 %pack_own.1 = (f32[15,14,48,128]{3,2,1,0:T(8,128)S(1)}, f32[40,8,128]{2,1,0:T(8,128)S(1)}, f32[120,128]{1,0:T(8,128)S(1)}, f32[120,128]{1,0:T(8,128)S(1)}) custom-call(s32[3]{0:T(128)S(1)} %pad_add_fusion.pos, f32[8,32,128]{2,1,0:T(8,128)} %f.3, f32[8,32,128]{2,1,0:T(8,128)} %w.3, f32[8,32,128]{2,1,0:T(8,128)} %u.3, f32[3,8,32,128]{3,2,1,0:T(8,128)} %v.3, ...), custom_call_target="tpu_custom_call" | custom-call | tf_op jit(solution)/shard_map/pack_own/pallas_call | solution.py:606
  6.2 1.3 %collective-permute-start.2 = (f32[40,8,128]{2,1,0:T(8,128)S(1)}, f32[40,8,128]{2,1,0:T(8,128)S(1)}, u32[]{:S(2)}, u32[]{:S(2)}) collective-permute-start(f32[40,8,128]{2,1,0:T(8,128)S(1)} %get-tuple-element.21), channel_id=1, source_target_pairs={{0,4},{1,5},{2,6},{3,7},{4,0},{5,1},{6,2},{7,3},{8,12},{9,13},{10,... | collective-permute-start | bytes 491528 | tf_op jit(solution)/shard_map/ppermute | solution.py:70
  7.5 1.1 %collective-permute-start.3 = (f32[120,128]{1,0:T(8,128)S(1)}, f32[120,128]{1,0:T(8,128)S(1)}, u32[]{:S(2)}, u32[]{:S(2)}) collective-permute-start(f32[120,128]{1,0:T(8,128)S(1)} %get-tuple-element.22), channel_id=1, source_target_pairs={{0,5},{1,4},{2,7},{3,6},{4,1},{5,0},{6,3},{7,2},{8,13},{9,12},{10,... | collective-permute-start | bytes 184328 | tf_op jit(solution)/shard_map/ppermute | solution.py:70
  8.6 1.1 %collective-permute-start.4 = (f32[120,128]{1,0:T(8,128)S(1)}, f32[120,128]{1,0:T(8,128)S(1)}, u32[]{:S(2)}, u32[]{:S(2)}) collective-permute-start(f32[120,128]{1,0:T(8,128)S(1)} %get-tuple-element.23), channel_id=1, source_target_pairs={{0,8},{1,6},{2,5},{3,11},{4,12},{5,2},{6,1},{7,15},{8,0},{9,14},{1... | collective-permute-start | bytes 184328 | tf_op jit(solution)/shard_map/ppermute | solution.py:70
  9.7 10.5 %collective-permute-done.3.rest_3_ = f32[120,128]{1,0:T(8,128)S(1)} collective-permute-done((f32[120,128]{1,0:T(8,128)S(1)}, f32[120,128]{1,0:T(8,128)S(1)}, u32[]{:S(2)}, u32[]{:S(2)}) %collective-permute-start.3) | collective-permute-done | bytes 61472 | tf_op jit(solution)/shard_map/ppermute | solution.py:70
  20.2 1.3 %collective-permute-done.4.rest_4_ = f32[120,128]{1,0:T(8,128)S(1)} collective-permute-done((f32[120,128]{1,0:T(8,128)S(1)}, f32[120,128]{1,0:T(8,128)S(1)}, u32[]{:S(2)}, u32[]{:S(2)}) %collective-permute-start.4) | collective-permute-done | bytes 61472 | tf_op jit(solution)/shard_map/ppermute | solution.py:70
  21.5 0.0 collective-permute-done.2.rest_2_
  21.5 0.0 collective-permute-done.rest_0_
  21.5 0.0 collective-permute-done.1.rest_1_
  21.5 3.1 %join_halo.1 = (f32[15,14,48,128]{3,2,1,0:T(8,128)S(1)}, f32[15,48,128]{2,1,0:T(8,128)S(1)}, f32[8,40,128]{2,1,0:T(8,128)S(1)}, f32[8,40,128]{2,1,0:T(8,128)S(1)}) custom-call(s32[3]{0:T(128)S(1)} %pad_add_fusion.pos, f32[15,14,48,128]{3,2,1,0:T(8,128)S(1)} %get-tuple-element.18.ext_in, ...), custom_call_target="tpu_custom_call", output_to_operand_aliasing={{0}: (1, {})} | custom-call | tf_op jit(solution)/shard_map/join_halo/pallas_call | solution.py:621
  24.7 1.9 %collective-permute-start.5 = (f32[8,40,128]{2,1,0:T(8,128)S(1)}, f32[8,40,128]{2,1,0:T(8,128)S(1)}, u32[]{:S(2)}, u32[]{:S(2)}) collective-permute-start(f32[8,40,128]{2,1,0:T(8,128)S(1)} %get-tuple-element.26), channel_id=1, source_target_pairs={{0,8},{1,9},{2,10},{3,11},{4,12},{5,13},{6,14},{7,15},{8,0},{9,1},... | collective-permute-start | bytes 491528 | tf_op jit(solution)/shard_map/ppermute | solution.py:70
  26.5 1.2 %collective-permute-start.6 = (f32[8,40,128]{2,1,0:T(8,128)S(1)}, f32[8,40,128]{2,1,0:T(8,128)S(1)}, u32[]{:S(2)}, u32[]{:S(2)}) collective-permute-start(f32[8,40,128]{2,1,0:T(8,128)S(1)} %get-tuple-element.27), channel_id=1, source_target_pairs={{0,4},{1,5},{2,6},{3,7},{4,0},{5,1},{6,2},{7,3},{8,16},{9,17},{10,... | collective-permute-start | bytes 491528 | tf_op jit(solution)/shard_map/ppermute | solution.py:70
  27.7 0.0 collective-permute-done.5.rest_0_
  27.7 3.8 %collective-permute-done.6.rest_1_ = f32[8,40,128]{2,1,0:T(8,128)S(1)} collective-permute-done((f32[8,40,128]{2,1,0:T(8,128)S(1)}, f32[8,40,128]{2,1,0:T(8,128)S(1)}, u32[]{:S(2)}, u32[]{:S(2)}) %collective-permute-start.6) | collective-permute-done | bytes 163872 | tf_op jit(solution)/shard_map/ppermute | solution.py:70
  31.5 9.0 %solve.1 = (f32[15,14,48,128]{3,2,1,0:T(8,128)S(1)}, f32[8,32,128]{2,1,0:T(8,128)}, f32[3,8,32,128]{3,2,1,0:T(8,128)}, f32[3,8,32,128]{3,2,1,0:T(8,128)}, f32[6,8,32,128]{3,2,1,0:T(8,128)}) custom-call(s32[3]{0:T(128)S(1)} %pad_add_fusion.pos, f32[15,14,48,128]{3,2,1,0:T(8,128)S(1)} %get-tuple-element.24.ext_in, ...), custom_call_target="tpu_custom_call", output_to_operand_aliasing={{0}: (1, {})} | custom-call | tf_op jit(solution)/shard_map/solve/pallas_call | solution.py:633
Async XLA Ops:
  2.6 19.0 %collective-permute-start = (f32[40,32,128]{2,1,0:T(8,128)S(1)}, f32[40,32,128]{2,1,0:T(8,128)S(1)}, u32[]{:S(2)}, u32[]{:S(2)}) collective-permute-start(f32[40,32,128]{2,1,0:T(8,128)S(1)} %get-tuple-element.19), channel_id=1, source_target_pairs={{0,1},{1,0},{2,3},{3,2},{4,5},{5,4},{6,7},{7,6},{8,9},{9,8},{10,11... | collective-permute-start | bytes 1966088 | tf_op jit(solution)/shard_map/ppermute | solution.py:70
  3.9 17.6 %collective-permute-start.1 = (f32[40,32,128]{2,1,0:T(8,128)S(1)}, f32[40,32,128]{2,1,0:T(8,128)S(1)}, u32[]{:S(2)}, u32[]{:S(2)}) collective-permute-start(f32[40,32,128]{2,1,0:T(8,128)S(1)} %get-tuple-element.20), channel_id=1, source_target_pairs={{0,8},{1,2},{2,1},{3,11},{4,12},{5,6},{6,5},{7,15},{8,0},{9,10},{1... | collective-permute-start | bytes 1966088 | tf_op jit(solution)/shard_map/ppermute | solution.py:70
  6.2 15.3 %collective-permute-start.2 = (f32[40,8,128]{2,1,0:T(8,128)S(1)}, f32[40,8,128]{2,1,0:T(8,128)S(1)}, u32[]{:S(2)}, u32[]{:S(2)}) collective-permute-start(f32[40,8,128]{2,1,0:T(8,128)S(1)} %get-tuple-element.21), channel_id=1, source_target_pairs={{0,4},{1,5},{2,6},{3,7},{4,0},{5,1},{6,2},{7,3},{8,12},{9,13},{10,... | collective-permute-start | bytes 491528 | tf_op jit(solution)/shard_map/ppermute | solution.py:70
  7.5 12.7 %collective-permute-start.3 = (f32[120,128]{1,0:T(8,128)S(1)}, f32[120,128]{1,0:T(8,128)S(1)}, u32[]{:S(2)}, u32[]{:S(2)}) collective-permute-start(f32[120,128]{1,0:T(8,128)S(1)} %get-tuple-element.22), channel_id=1, source_target_pairs={{0,5},{1,4},{2,7},{3,6},{4,1},{5,0},{6,3},{7,2},{8,13},{9,12},{10,... | collective-permute-start | bytes 184328 | tf_op jit(solution)/shard_map/ppermute | solution.py:70
  8.6 13.0 %collective-permute-start.4 = (f32[120,128]{1,0:T(8,128)S(1)}, f32[120,128]{1,0:T(8,128)S(1)}, u32[]{:S(2)}, u32[]{:S(2)}) collective-permute-start(f32[120,128]{1,0:T(8,128)S(1)} %get-tuple-element.23), channel_id=1, source_target_pairs={{0,8},{1,6},{2,5},{3,11},{4,12},{5,2},{6,1},{7,15},{8,0},{9,14},{1... | collective-permute-start | bytes 184328 | tf_op jit(solution)/shard_map/ppermute | solution.py:70
  24.7 3.1 %collective-permute-start.5 = (f32[8,40,128]{2,1,0:T(8,128)S(1)}, f32[8,40,128]{2,1,0:T(8,128)S(1)}, u32[]{:S(2)}, u32[]{:S(2)}) collective-permute-start(f32[8,40,128]{2,1,0:T(8,128)S(1)} %get-tuple-element.26), channel_id=1, source_target_pairs={{0,8},{1,9},{2,10},{3,11},{4,12},{5,13},{6,14},{7,15},{8,0},{9,1},... | collective-permute-start | bytes 491528 | tf_op jit(solution)/shard_map/ppermute | solution.py:70
  26.5 5.0 %collective-permute-start.6 = (f32[8,40,128]{2,1,0:T(8,128)S(1)}, f32[8,40,128]{2,1,0:T(8,128)S(1)}, u32[]{:S(2)}, u32[]{:S(2)}) collective-permute-start(f32[8,40,128]{2,1,0:T(8,128)S(1)} %get-tuple-element.27), channel_id=1, source_target_pairs={{0,4},{1,5},{2,6},{3,7},{4,0},{5,1},{6,2},{7,3},{8,16},{9,17},{10,... | collective-permute-start | bytes 491528 | tf_op jit(solution)/shard_map/ppermute | solution.py:70

commit v3 on v2

v3 whole, which is shorter than its diff:
```python
import functools
import itertools

import jax
import jax.numpy as jnp
from jax import lax
from jax.experimental import pallas as pl
from jax.experimental.pallas import tpu as pltpu
from jax.sharding import PartitionSpec as P


ITERS = 3
HALO = ITERS
ROW0 = 8
SLOT = 8
LANES = 128

first_alpha = 0.5
second_alpha = 1.0
dual_step = 0.2
primal_step = 0.2

AXES = ("gx", "gy", "gz")
FIELDS = 15
F, W, U, V, PF, QF = 0, 1, 2, 3, 6, 9
GROUPS = (FIELDS + 1) // 2


def spans(low):
    chosen = [(F, 2), (W, 2), (U, 3), (V, 3), (V + 1, 3), (V + 2, 3)]
    chosen += [(PF + i, 2 if low else 3) for i in range(3)]
    chosen += [(QF + i, 3 if low else 2) for i in range(6)]
    if not low:
        chosen += [(U, 3)]
    return [(field, 0 if low else -count, count) for field, count in chosen]


def entries(low):
    return [(field, first + i) for field, first, count in spans(low) for i in range(count)]


SENT = len(entries(True))


def colours(size):
    return ("even", "odd")[: min(size - 1, 2)]


def partner(place, colour, size):
    other = place ^ 1 if colour == "even" else ((place + 1) ^ 1) - 1
    return other if 0 <= other < size else None


def exchange(values, moves, sizes):
    pairs = []
    for place in itertools.product(*(range(sizes[axis]) for axis in AXES)):
        other = list(place)
        for axis, colour in moves.items():
            other[AXES.index(axis)] = partner(place[AXES.index(axis)], colour, sizes[axis])
        if None in other:
            spare = [axis for axis in AXES if axis not in moves and sizes[axis] % 2 == 0]
            if not spare:
                continue
            other = list(place)
            other[AXES.index(spare[0])] ^= 1
        source, target = 0, 0
        for axis, here, there in zip(AXES, place, other):
            source = source * sizes[axis] + here
            target = target * sizes[axis] + there
        pairs.append((source, target))
    return lax.ppermute(values, AXES, pairs)


def sends_low(colour, parity):
    return (colour == "even") == (parity == 1)


def colour_of(side, parity):
    return "even" if (side == "low") == (parity == 1) else "odd"


def pick(received, colour):
    return received.get(colour, received["even"])


def pack(extents, ys, zs, pos, f, w, u, v, p, q, ext, *rest):
    nz, ny, _ = extents
    rows = ny + 2 * ROW0
    y_outs = dict(zip(ys, rest))
    z_outs = dict(zip(zs, rest[len(ys) :]))
    own_sem, z_sem = rest[-2:]
    arrays = ((F, f, 1), (W, w, 1), (U, u, 1), (V, v, 3), (PF, p, 3), (QF, q, 6))
    own = (pl.ds(HALO, nz), pl.ds(ROW0, ny))
    copies = []
    for base, array, count in arrays:
        fields = base if count == 1 else pl.ds(base, count)
        copies.append(pltpu.make_async_copy(array, ext.at[(fields,) + own], own_sem))
    for copy in copies:
        copy.start()

    def source(field, first, count):
        layers = pl.ds(first % nz, count)
        base, array, stack = [item for item in arrays if item[0] <= field][-1]
        return array.at[layers] if stack == 1 else array.at[field - base, layers]

    def z_copies(parity):
        for colour, out in z_outs.items():
            at = 0
            for field, first, count in spans(sends_low(colour, parity)):
                target = out.at[pl.ds(at, count)]
                yield pltpu.make_async_copy(source(field, first, count), target, z_sem)
                at += count

    for parity in (0, 1):

        @pl.when(pos[2] % 2 == parity)
        def _():
            for copy in z_copies(parity):
                copy.start()

    for copy in copies:
        copy.wait()
    flat = ext.reshape(FIELDS * (nz + 2 * HALO) * rows, LANES)
    for parity in (0, 1):

        @pl.when(pos[1] % 2 == parity)
        def _():
            for colour, out in y_outs.items():
                for i, (field, at) in enumerate(entries(sends_low(colour, parity))):
                    start = (field * (nz + 2 * HALO) + HALO) * rows + ROW0 + at % ny
                    out[i] = flat[pl.ds(start, nz, stride=rows), :]

    for copy in z_copies(0):
        copy.wait()


def tile_starts(ny):
    return [ROW0 - HALO + 8 * i for i in range(-(-(ny + 2 * HALO) // 8))]


def lanes_of():
    lane = lax.broadcasted_iota(jnp.int32, (8, LANES), 1)
    return lane, lane % SLOT


def placed(side, extent):
    if side == "low":
        return entries(False)[: SENT - HALO]
    return [(field, extent + at) for field, at in entries(True)]


def columns_of(values, level, shift=0):
    return pltpu.roll(values, (level * SLOT + HALO + shift) % LANES, 1)


def join_y(extents, ys, pos, ext_in, *rest):
    del ext_in
    nz, ny, _ = extents
    rows = ny + 2 * ROW0
    levels = nz + 2 * HALO
    y_got = dict(zip(ys, rest))
    ext, payload = rest[len(ys) :]
    flat = ext.reshape(FIELDS * levels * rows, LANES)
    for parity in (0, 1):

        @pl.when(pos[1] % 2 == parity)
        def _():
            for side in ("low", "high"):
                got = pick(y_got, colour_of(side, parity))
                for i, (field, at) in enumerate(placed(side, ny)):
                    start = (field * levels + HALO) * rows + ROW0 + at
                    flat[pl.ds(start, nz, stride=rows), :] = got[i]

    lane, _ = lanes_of()
    pieces = []
    for half, level in itertools.product((0, 1), range(HALO, HALO + nz)):
        shift = half * (LANES // 2)
        pieces.append(((level * SLOT + shift) % LANES, half, level, shift))
    pieces.sort()

    def group(i, carry):
        pair = (2 * i, jnp.minimum(2 * i + 1, FIELDS - 1))
        totals = []
        for row in tile_starts(ny):
            total = None
            for at, half, level, shift in pieces:
                turned = columns_of(ext[pair[half], level, pl.ds(row, 8), :], level, shift)
                total = turned if total is None else jnp.where(lane >= at, turned, total)
            totals.append(total)
        for j, total in enumerate(totals):
            payload[i, pl.ds(8 * j, 8), :] = total
        return carry

    lax.fori_loop(0, GROUPS, group, 0)


BLOCK = HALO * SLOT
PER_TILE = LANES // BLOCK
BLOCKS = -(-FIELDS // PER_TILE)


def join_x(extents, xs, ys, zs, pos, ext, payload, *rest):
    nz, ny, _ = extents
    x_got = dict(zip(xs, rest))
    side = rest[len(xs)]
    z_outs = dict(zip(zs, rest[len(xs) + 1 :]))
    lane, slot = lanes_of()
    starts = tile_starts(ny)
    half = LANES // 2

    def build(got_low, got_high, outs):
        def group(i, carry):
            sides = []
            for j in range(len(starts)):
                at = pl.ds(8 * j, 8)
                own = payload[i, at, :]
                left = jnp.where(slot < HALO, got_low[i, at, :], own)
                right = jnp.where(slot < HALO, own, got_high[i, at, :])
                sides.append((left, right, pltpu.roll(left, half, 1), pltpu.roll(right, half, 1)))
            for values, row in zip(sides, starts):
                for k in range(4):
                    side[2 * i + k // 2, k % 2, pl.ds(row, 8), :] = values[k]
            return carry

        lax.fori_loop(0, GROUPS, group, 0)

        def border(j, carry):
            at = pl.ds(pl.multiple_of(8 * j, 8), 8)
            came = [
                jnp.where(slot < HALO, got_low[i, at, :], got_high[i, at, :]) for i in range(GROUPS)
            ]
            made = []
            for low, out in outs.items():
                for block in range(BLOCKS):
                    total = None
                    for k in range(min(PER_TILE, FIELDS - block * PER_TILE)):
                        i, odd = divmod(block * PER_TILE + k, 2)
                        first = HALO * SLOT if low else nz * SLOT
                        turned = pltpu.roll(came[i], (odd * half + k * BLOCK - first) % LANES, 1)
                        total = turned if total is None else jnp.where(lane >= k * BLOCK, turned, total)
                    made.append((out, block, total))
            for out, block, total in made:
                here = pl.ds(pl.multiple_of(8 * (block * len(starts) + j), 8), 8)
                out[here, :] = total
            return carry

        lax.fori_loop(0, len(starts), border, 0)

    for x_parity, z_parity in itertools.product((0, 1), (0, 1)):

        @pl.when(jnp.logical_and(pos[0] % 2 == x_parity, pos[2] % 2 == z_parity))
        def _():
            build(
                pick(x_got, colour_of("low", x_parity)),
                pick(x_got, colour_of("high", x_parity)),
                {sends_low(colour, z_parity): out for colour, out in z_outs.items()},
            )

    for z_parity, y_parity in itertools.product((0, 1), (0, 1)):

        @pl.when(jnp.logical_and(pos[2] % 2 == z_parity, pos[1] % 2 == y_parity))
        def _():
            for z_colour, out in z_outs.items():
                for n, y_colour in enumerate(ys):
                    low = colour_of("low", y_parity) == y_colour
                    row = ROW0 - HALO if low else ROW0 + ny
                    first = BLOCKS * 8 * len(starts) + n * SENT * HALO
                    for i, (field, at) in enumerate(entries(sends_low(z_colour, z_parity))):
                        out[pl.ds(first + i * HALO, HALO), :] = ext[
                            field, HALO + at % nz, pl.ds(row, HALO), :
                        ]


def shrink(total, bound):
    return lax.rsqrt(jnp.maximum(1.0, total * (1.0 / (bound * bound))))


def masked(mask, values):
    return values if mask is None else mask * values


def p_step(bar, next_bar, p, upper):
    t = [p[a] + masked(upper[a], next_bar[a] - bar[0]) - bar[1 + a] for a in range(3)]
    scale = shrink(t[0] * t[0] + t[1] * t[1] + t[2] * t[2], first_alpha)
    return [value * scale for value in t]


def q_step(bar, prev_bar, q, lower):
    d = [[masked(lower[b], bar[a] - prev_bar[b][a]) for a in range(3)] for b in range(3)]
    s = [q[a] + d[a][a] for a in range(3)]
    for i, (a, b) in enumerate(((0, 1), (0, 2), (1, 2))):
        s.append(q[3 + i] + 0.5 * (d[b][a] + d[a][b]))
    off = s[3] * s[3] + s[4] * s[4] + s[5] * s[5]
    scale = shrink(s[0] * s[0] + s[1] * s[1] + s[2] * s[2] + (off + off), second_alpha)
    return [value * scale for value in s]


ROWS_OF_Q = ((0, 3, 4), (3, 1, 5), (4, 5, 2))


def primal_step_of(u, v, a_map, b_map, p, q, prev_p, next_q, upper, lower):
    div = None
    for a in range(3):
        term = masked(upper[a], p[a]) - masked(lower[a], prev_p[a])
        div = term if div is None else div + term
    new_u = (u + primal_step * div) * b_map + a_map
    new_v = []
    for a in range(3):
        total = p[a]
        for b in range(3):
            total = total + (masked(upper[b], next_q[b][a]) - masked(lower[b], q[ROWS_OF_Q[b][a]]))
        new_v.append(v[a] + primal_step * total)
    bar = [(2.0 * dual_step) * new_u - dual_step * u]
    bar += [(2.0 * dual_step) * new_v[a] - dual_step * v[a] for a in range(3)]
    return new_u, new_v, bar


class Steps:
    def __init__(self, extents, sizes, pos, ext, bars, side, side_bars):
        self.nz, self.ny, self.nx = nz, ny, nx = extents
        self.levels = nz + 2 * HALO
        self.pos, self.ext, self.bars, self.side, self.side_bars = pos, ext, bars, side, side_bars
        self.starts = tile_starts(ny)
        self.lane, slot = lanes_of()
        sub = lax.broadcasted_iota(jnp.int32, (8, LANES), 0)
        self.full = full = [sizes[axis] * extent for axis, extent in zip(AXES, (nx, ny, nz))]

        def masks(places, extent):
            upper = jnp.logical_and(places >= 0, places < extent - 1)
            lower = jnp.logical_and(places > 0, places < extent)
            return upper.astype(jnp.float32), lower.astype(jnp.float32)

        outer = (self.starts[0], self.starts[-1])
        self.y_masks = [
            masks(pos[1] * ny + (row - ROW0) + sub, full[1]) if row in outer else (None, None)
            for row in self.starts
        ]
        self.x_main = masks(pos[0] * nx + self.lane, full[0])
        self.x_side = [masks(pos[0] * nx + at + slot, full[0]) for at in (-HALO, nx - HALO)]
        self.z_side = masks(pos[2] * nz - HALO + self.lane // SLOT, full[2])
        self.first, self.last = self.lane == 0, self.lane == LANES - 1

    def z_main(self, level):
        place = self.pos[2] * self.nz - HALO + level
        upper = jnp.logical_and(place >= 0, place < self.full[2] - 1)
        lower = jnp.logical_and(place > 0, place < self.full[2])
        one, none = jnp.float32(1.0), jnp.float32(0.0)
        return jnp.where(upper, one, none), jnp.where(lower, one, none)

    def from_low(self, values, level):
        return pltpu.roll(values, LANES - HALO + 1 - SLOT * level, 1)

    def from_high(self, values, level):
        return pltpu.roll(values, LANES - 1 - HALO - SLOT * level, 1)

    def next_x(self, values, field_values, level):
        return jnp.where(self.last, self.from_high(field_values, level), pltpu.roll(values, LANES - 1, 1))

    def prev_x(self, values, field_values, level):
        return jnp.where(self.first, self.from_low(field_values, level), pltpu.roll(values, 1, 1))

    @staticmethod
    def maps(f, w):
        inverse = 1.0 / (1.0 + primal_step * w)
        return (primal_step * w * f) * inverse, inverse

    def prepare_main(self, level):
        for row in self.starts:
            here = pl.ds(row, 8)
            maps = self.maps(self.ext[F, level, here, :], self.ext[W, level, here, :])
            self.ext[F, level, here, :], self.ext[W, level, here, :] = maps
            for a in range(4):
                self.bars[a, level + 1, here, :] = dual_step * self.ext[U + a, level, here, :]

    def prepare_side(self, which, row, fields):
        here = pl.ds(row, 8)
        for field, values in enumerate(list(self.maps(fields[F], fields[W])) + fields[U:]):
            self.side[field, which, here, :] = values
        for a in range(4):
            self.side_bars[a, which, here, :] = dual_step * fields[U + a]

    def p_main(self, level):
        ext, bars = self.ext, self.bars
        upper_z, _ = self.z_main(level)
        for i, row in enumerate(self.starts):
            here = pl.ds(row, 8)
            bar = [bars[a, level + 1, here, :] for a in range(4)]
            next_bar = [
                self.next_x(bar[0], self.side_bars[0, 1, here, :], level),
                bars[0, level + 1, pl.ds(row + 1, 8), :],
                bars[0, level + 2, here, :],
            ]
            p = [ext[PF + a, level, here, :] for a in range(3)]
            p = p_step(bar, next_bar, p, (self.x_main[0], self.y_masks[i][0], upper_z))
            for a in range(3):
                ext[PF + a, level, here, :] = p[a]

    def q_main(self, level):
        ext, bars = self.ext, self.bars
        _, lower_z = self.z_main(level)
        for i, row in enumerate(self.starts):
            here = pl.ds(row, 8)
            bar = [bars[1 + a, level + 1, here, :] for a in range(3)]
            prev_bar = [
                [self.prev_x(bar[a], self.side_bars[1 + a, 0, here, :], level) for a in range(3)],
                [bars[1 + a, level + 1, pl.ds(row - 1, 8), :] for a in range(3)],
                [bars[1 + a, level, here, :] for a in range(3)],
            ]
            q = [ext[QF + a, level, here, :] for a in range(6)]
            q = q_step(bar, prev_bar, q, (self.x_main[1], self.y_masks[i][1], lower_z))
            for a in range(6):
                ext[QF + a, level, here, :] = q[a]

    def primal_main(self, level):
        ext, bars, side = self.ext, self.bars, self.side
        upper_z, lower_z = self.z_main(level)
        for i, row in enumerate(self.starts):
            here = pl.ds(row, 8)
            p = [ext[PF + a, level, here, :] for a in range(3)]
            q = [ext[QF + a, level, here, :] for a in range(6)]
            prev_p = [
                self.prev_x(p[0], side[PF, 0, here, :], level),
                ext[PF + 1, level, pl.ds(row - 1, 8), :],
                ext[PF + 2, level - 1, here, :],
            ]
            next_q = [
                [self.next_x(q[j], side[QF + j, 1, here, :], level) for j in ROWS_OF_Q[0]],
                [ext[QF + j, level, pl.ds(row + 1, 8), :] for j in ROWS_OF_Q[1]],
                [ext[QF + j, level + 1, here, :] for j in ROWS_OF_Q[2]],
            ]
            new_u, new_v, bar = primal_step_of(
                ext[U, level, here, :],
                [ext[V + a, level, here, :] for a in range(3)],
                ext[F, level, here, :],
                ext[W, level, here, :],
                p,
                q,
                prev_p,
                next_q,
                (self.x_main[0], self.y_masks[i][0], upper_z),
                (self.x_main[1], self.y_masks[i][1], lower_z),
            )
            for a, value in enumerate([new_u] + new_v):
                ext[U + a, level, here, :] = value
            for a in range(4):
                bars[a, level + 1, here, :] = bar[a]

    def dual_side(self):
        side, side_bars = self.side, self.side_bars
        for which, (i, row) in itertools.product((0, 1), enumerate(self.starts)):
            here = pl.ds(row, 8)
            bar = [side_bars[a, which, here, :] for a in range(4)]
            next_bar = [
                pltpu.roll(bar[0], LANES - 1, 1),
                side_bars[0, which, pl.ds(row + 1, 8), :],
                pltpu.roll(bar[0], LANES - SLOT, 1),
            ]
            prev_bar = [
                [pltpu.roll(bar[1 + a], 1, 1) for a in range(3)],
                [side_bars[1 + a, which, pl.ds(row - 1, 8), :] for a in range(3)],
                [pltpu.roll(bar[1 + a], SLOT, 1) for a in range(3)],
            ]
            upper = (self.x_side[which][0], self.y_masks[i][0], self.z_side[0])
            lower = (self.x_side[which][1], self.y_masks[i][1], self.z_side[1])
            p = p_step(bar, next_bar, [side[PF + a, which, here, :] for a in range(3)], upper)
            q = q_step(bar[1:], prev_bar, [side[QF + a, which, here, :] for a in range(6)], lower)
            for a, value in enumerate(p + q):
                side[PF + a, which, here, :] = value

    def primal_side(self):
        side, side_bars = self.side, self.side_bars
        for which, (i, row) in itertools.product((0, 1), enumerate(self.starts)):
            here = pl.ds(row, 8)
            p = [side[PF + a, which, here, :] for a in range(3)]
            q = [side[QF + a, which, here, :] for a in range(6)]
            prev_p = [
                pltpu.roll(p[0], 1, 1),
                side[PF + 1, which, pl.ds(row - 1, 8), :],
                pltpu.roll(p[2], SLOT, 1),
            ]
            next_q = [
                [pltpu.roll(q[j], LANES - 1, 1) for j in ROWS_OF_Q[0]],
                [side[QF + j, which, pl.ds(row + 1, 8), :] for j in ROWS_OF_Q[1]],
                [pltpu.roll(q[j], LANES - SLOT, 1) for j in ROWS_OF_Q[2]],
            ]
            new_u, new_v, bar = primal_step_of(
                side[U, which, here, :],
                [side[V + a, which, here, :] for a in range(3)],
                side[F, which, here, :],
                side[W, which, here, :],
                p,
                q,
                prev_p,
                next_q,
                (self.x_side[which][0], self.y_masks[i][0], self.z_side[0]),
                (self.x_side[which][1], self.y_masks[i][1], self.z_side[1]),
            )
            for a, value in enumerate([new_u] + new_v):
                side[U + a, which, here, :] = value
            for a in range(4):
                side_bars[a, which, here, :] = bar[a]


def level_loop(start, stop, *bodies):
    count = max(stop - start, 0)

    def trip(i, carry):
        for body in bodies:
            for j in (0, 1):
                body(start + 2 * i + j)
        return carry

    lax.fori_loop(0, count // 2, trip, 0)
    if count % 2:
        for body in bodies:
            body(stop - 1)


def solve_inner(extents, sizes, pos, ext_in, side_in, ext, bars, side, side_bars):
    del ext_in
    nz, _, _ = extents
    steps = Steps(extents, sizes, pos, ext, bars, side, side_bars)
    for which, row in itertools.product((0, 1), steps.starts):
        fields = [side_in[field, which, pl.ds(row, 8), :] for field in range(FIELDS)]
        steps.prepare_side(which, row, fields)
    level_loop(HALO, HALO + nz, steps.prepare_main)
    for step in range(ITERS):
        low, high = HALO + step, HALO + nz - step
        if high - 1 <= low:
            break
        level_loop(low, high - 1, steps.p_main, lambda level: steps.q_main(level + 1))
        if high - 2 < low + 1:
            break
        steps.dual_side()
        level_loop(low + 1, high - 1, steps.primal_main)
        if step + 1 < ITERS:
            steps.primal_side()


def solve_outer(extents, sizes, ys, zs, pos, ext_in, bars_in, side_in, *rest):
    del ext_in, bars_in
    nz, ny, _ = extents
    z_got = dict(zip(zs, rest))
    rest = rest[len(zs) :]
    frame_got = dict(zip(zs, rest))
    ext, bars, out_u, out_v, out_p, out_q, side, side_bars, sem = rest[len(zs) :]
    steps = Steps(extents, sizes, pos, ext, bars, side, side_bars)
    starts = steps.starts
    lane, slot = lanes_of()
    sides = ("low", "high")

    for z_parity in (0, 1):

        @pl.when(pos[2] % 2 == z_parity)
        def _():
            for z_side in sides:
                got = pick(z_got, colour_of(z_side, z_parity))
                for i, (field, at) in enumerate(placed(z_side, nz)):
                    ext[field, HALO + at, pl.ds(ROW0, ny), :] = got[i]

    for z_parity, y_parity in itertools.product((0, 1), (0, 1)):

        @pl.when(jnp.logical_and(pos[2] % 2 == z_parity, pos[1] % 2 == y_parity))
        def _():
            for z_side, y_side in itertools.product(sides, sides):
                got = pick(frame_got, colour_of(z_side, z_parity))
                y_colour = colour_of(y_side, y_parity)
                n = ys.index(y_colour) if y_colour in ys else 0
                first = BLOCKS * 8 * len(starts) + n * SENT * HALO
                row = ROW0 + (-HALO if y_side == "low" else ny)
                for i, (field, at) in enumerate(placed(z_side, nz)):
                    ext[field, HALO + at, pl.ds(row, HALO), :] = got[pl.ds(first + i * HALO, HALO), :]

    top = (HALO + nz) * SLOT
    below, above = lane < BLOCK, lane >= top
    low_levels, high_levels = range(HALO), range(HALO + nz, nz + 2 * HALO)

    outer = jnp.logical_or(below, above)

    def strips(got_low, got_high):
        ready = None
        for j, row in enumerate(starts):
            here = pl.ds(row, 8)
            fields = ([], [])
            for field in range(FIELDS):
                block, k = divmod(field, PER_TILE)
                columns = None
                for level in list(low_levels) + list(high_levels):
                    turned = columns_of(ext[field, level, here, :], level)
                    columns = turned if columns is None else jnp.where(lane >= level * SLOT, turned, columns)
                at = (pl.ds(8 * (block * len(starts) + j), 8), slice(None))
                came = jnp.where(
                    above,
                    pltpu.roll(got_high[at], (top - k * BLOCK) % LANES, 1),
                    pltpu.roll(got_low[at], (-k * BLOCK) % LANES, 1),
                )
                left = jnp.where(slot < HALO, came, columns)
                right = jnp.where(slot < HALO, columns, came)
                fields[0].append(jnp.where(outer, left, side_in[field, 0, here, :]))
                fields[1].append(jnp.where(outer, right, side_in[field, 1, here, :]))
            for done in (ready, (row, fields)):
                if done is not None and (done is ready or row == starts[-1]):
                    for which in (0, 1):
                        steps.prepare_side(which, done[0], done[1][which])
            ready = (row, fields)

    for z_parity in (0, 1):

        @pl.when(pos[2] % 2 == z_parity)
        def _():
            strips(
                pick(frame_got, colour_of("low", z_parity)),
                pick(frame_got, colour_of("high", z_parity)),
            )

    for level in list(low_levels) + list(high_levels):
        steps.prepare_main(level)

    def out_copies(fields):
        own = (pl.ds(HALO, nz), pl.ds(ROW0, ny))
        return [pltpu.make_async_copy(ext.at[(field,) + own], out, sem) for field, out in fields]

    duals = [(pl.ds(PF, 3), out_p), (pl.ds(QF, 6), out_q)]
    primals = [(U, out_u), (pl.ds(V, 3), out_v)]
    apart = nz >= 2 * ITERS

    def outer_levels(low_first, high_first):
        if apart:
            return [first + j for first in (low_first, high_first) for j in range(HALO)]
        return sorted({first + j for first in (low_first, high_first) for j in range(HALO)})

    def iteration(step, carry):
        top_level = HALO + nz - 1 - step
        for level in outer_levels(step, top_level):
            steps.p_main(level)
        for level in outer_levels(step + 1, top_level + 1):
            steps.q_main(level)

        @pl.when(step == ITERS - 1)
        def _():
            for copy in out_copies(duals):
                copy.start()

        steps.dual_side()
        for level in outer_levels(step + 1, top_level):
            steps.primal_main(level)
        pl.when(step < ITERS - 1)(steps.primal_side)
        return carry

    if apart:
        lax.fori_loop(0, ITERS, iteration, 0)
    else:
        for step in range(ITERS):
            iteration(step, 0)
    for copy in out_copies(primals):
        copy.start()
    for copy in out_copies(duals + primals):
        copy.wait()


def per_device(sizes, noisy_image, fidelity, primal_u, primal_v, dual_p, dual_q):
    nz, ny, nx = extents = noisy_image.shape
    levels, rows = nz + 2 * HALO, ny + 2 * ROW0
    assert nx == LANES and ny % 8 == 0 and nz * SLOT <= LANES // 2
    assert min(nz, ny) >= HALO and min(sizes.values()) > 1
    xs, ys, zs = (colours(sizes[axis]) for axis in AXES)
    pos = jnp.stack([lax.axis_index(axis) for axis in AXES])
    args = tuple(pltpu.with_memory_space_constraint(a, pltpu.HBM) for a in (noisy_image, fidelity, primal_u, primal_v, dual_p, dual_q))
    f32 = jnp.float32
    smem = pl.BlockSpec(memory_space=pltpu.SMEM)
    anywhere = pl.BlockSpec(memory_space=pltpu.HBM)
    vmem = pl.BlockSpec(memory_space=pltpu.VMEM)

    def shaped(*shape):
        return jax.ShapeDtypeStruct(shape, f32)

    def call(body, ins, outs, out_specs, limit, **more):
        return pl.pallas_call(
            body,
            in_specs=ins,
            out_specs=out_specs,
            out_shape=outs,
            compiler_params=pltpu.CompilerParams(vmem_limit_bytes=limit * 1024 * 1024),
            **more,
        )

    strip_rows = 8 * len(tile_starts(ny))
    ext_shape = shaped(FIELDS, levels, rows, nx)
    packed = call(
        functools.partial(pack, extents, ys, zs),
        [smem] + [anywhere] * 6,
        [ext_shape] + [shaped(SENT, nz, nx)] * len(ys) + [shaped(SENT, ny, nx)] * len(zs),
        [vmem] * (1 + len(ys) + len(zs)),
        16,
        scratch_shapes=[pltpu.SemaphoreType.DMA, pltpu.SemaphoreType.DMA],
    )(pos, *args)
    ext, y_pay, z_pay = packed[0], packed[1 : 1 + len(ys)], packed[1 + len(ys) :]
    y_got = [exchange(pay, {"gy": c}, sizes) for c, pay in zip(ys, y_pay)]
    z_got = [exchange(pay, {"gz": c}, sizes) for c, pay in zip(zs, z_pay)]

    ext, x_pay = call(
        functools.partial(join_y, extents, ys),
        [smem] + [vmem] * (1 + len(ys)),
        [ext_shape, shaped(GROUPS, strip_rows, nx)],
        [vmem] * 2,
        16,
        input_output_aliases={1: 0},
    )(pos, ext, *y_got)
    x_got = [exchange(x_pay, {"gx": c}, sizes) for c in xs]

    both = shaped(FIELDS, 2, rows, nx)
    frame = shaped(BLOCKS * strip_rows + len(ys) * SENT * HALO, nx)
    side, *frame_pay = call(
        functools.partial(join_x, extents, xs, ys, zs),
        [smem] + [vmem] * (2 + len(xs)),
        [shaped(2 * GROUPS, 2, rows, nx)] + [frame] * len(zs),
        [vmem] * (1 + len(zs)),
        16,
    )(pos, ext, x_pay, *x_got)
    frame_got = [exchange(pay, {"gz": c}, sizes) for c, pay in zip(zs, frame_pay)]

    bar_shape = shaped(4, levels + 2, rows, nx)
    scratch = [pltpu.VMEM(both.shape, f32), pltpu.VMEM((4,) + both.shape[1:], f32)]
    ext, bars = call(
        functools.partial(solve_inner, extents, sizes),
        [smem] + [vmem] * 2,
        [ext_shape, bar_shape],
        [vmem] * 2,
        16,
        input_output_aliases={1: 0},
        scratch_shapes=scratch,
    )(pos, ext, side)

    solved = call(
        functools.partial(solve_outer, extents, sizes, ys, zs),
        [smem] + [vmem] * (3 + 2 * len(zs)),
        [ext_shape, bar_shape] + [shaped(*a.shape) for a in (primal_u, primal_v, dual_p, dual_q)],
        [vmem] * 2 + [anywhere] * 4,
        24,
        input_output_aliases={1: 0, 2: 1},
        scratch_shapes=scratch + [pltpu.SemaphoreType.DMA],
    )(pos, ext, bars, side, *z_got, *frame_got)
    return tuple(solved[2:])


def solution(mesh):
    sizes = {axis: mesh.shape[axis] for axis in AXES}
    scalar, stacked = P("gz", "gy", "gx"), P(None, "gz", "gy", "gx")

    def body(*args):
        return per_device(sizes, *args)

    return jax.shard_map(
        body,
        mesh=mesh,
        in_specs=(scalar,) * 3 + (stacked,) * 3,
        out_specs=(scalar,) + (stacked,) * 3,
        check_vma=False,
    )
```

time: 40.8 us -> 34.4 us (0.84)
  the two profiles are of different devices: /device:TPU:17 before, /device:TPU:1 now
where the time goes in v3:
time: 34.4 us; the launch traced here: 34.2 us
  Pallas kernels  16.4 us (48%)
  starting transfers between devices  9.63 us (28%)
  waiting for transfers between devices  7.48 us (22%)
  between operations  0.7 us (2%)
    ppermute x7, starting transfers between devices, exchange(): return lax.ppermute(values, AXES, pairs)  9.63 us
    ppermute x7, waiting for transfers between devices, exchange(): return lax.ppermute(values, AXES, pairs)  7.48 us
    pallas_call x1, Pallas kernels, per_device(): call(functools.partial(solve_outer, extents, sizes, ys, zs), [smem] + [vm...  6.48 us
    pallas_call x1, Pallas kernels, per_device(): call(functools.partial(solve_inner, extents, sizes), [smem] + [vmem] * 2,...  3.81 us
    pallas_call x1, Pallas kernels, per_device(): call(functools.partial(pack, extents, ys, zs), [smem] + [anywhere] * 6, [...  2.44 us
    pallas_call x1, Pallas kernels, per_device(): call(functools.partial(join_y, extents, ys), [smem] + [vmem] * (1 + len(y...  1.86 us
    pallas_call x1, Pallas kernels, per_device(): call(functools.partial(join_x, extents, xs, ys, zs), [smem] + [vmem] * (2...  1.76 us
  transfers between devices with their start and end apart: 7, of which 2 were waited for; matrix products, arithmetic and copies ran while one was open for 0% of the time, Pallas kernels for 22%

profile of v3, /device:TPU:1, one launch (start us, length us, event | category | flops | bytes accessed | tf_op | source)
XLA Modules:
  0.0 34.2 jit_solution(15928963498944668803)
XLA Ops:
  0.6 0.1 pad_add_fusion.pos
  0.7 2.4 %shard_map.93 = (f32[15,14,48,128]{3,2,1,0:T(8,128)S(1)}, f32[40,8,128]{2,1,0:T(8,128)S(1)}, f32[40,32,128]{2,1,0:T(8,128)S(1)}, f32[40,32,128]{2,1,0:T(8,128)S(1)}) custom-call(s32[3]{0:T(128)S(1)} %pad_add_fusion.pos, f32[8,32,128]{2,1,0:T(8,128)} %f.1, f32[8,32,128]{2,1,0:T(8,128)} %w.1, f32[8,32,128]{2,1,0:T(8,128)} %u.1, f32[3,8,32,128]{3,2,1,0:T(8,128)} %v.1, ...), custom_call_target="tpu_custom_call" | custom-call | tf_op jit(solution)/shard_map/pallas_call | solution.py:689
  3.2 2.2 %collective-permute-start.3 = (f32[40,32,128]{2,1,0:T(8,128)S(1)}, f32[40,32,128]{2,1,0:T(8,128)S(1)}, u32[]{:S(2)}, u32[]{:S(2)}) collective-permute-start(f32[40,32,128]{2,1,0:T(8,128)S(1)} %get-tuple-element.26), channel_id=1, source_target_pairs={{0,1},{1,0},{2,3},{3,2},{4,5},{5,4},{6,7},{7,6},{8,9},{9,8},{10,11... | collective-permute-start | bytes 1966088 | tf_op jit(solution)/shard_map/ppermute | solution.py:71
  5.3 1.0 %collective-permute-start.4 = (f32[40,32,128]{2,1,0:T(8,128)S(1)}, f32[40,32,128]{2,1,0:T(8,128)S(1)}, u32[]{:S(2)}, u32[]{:S(2)}) collective-permute-start(f32[40,32,128]{2,1,0:T(8,128)S(1)} %get-tuple-element.27), channel_id=1, source_target_pairs={{0,8},{1,2},{2,1},{3,11},{4,12},{5,6},{6,5},{7,15},{8,0},{9,10},{1... | collective-permute-start | bytes 1966088 | tf_op jit(solution)/shard_map/ppermute | solution.py:71
  6.3 1.2 %collective-permute-start = (f32[40,8,128]{2,1,0:T(8,128)S(1)}, f32[40,8,128]{2,1,0:T(8,128)S(1)}, u32[]{:S(2)}, u32[]{:S(2)}) collective-permute-start(f32[40,8,128]{2,1,0:T(8,128)S(1)} %get-tuple-element.20), channel_id=1, source_target_pairs={{0,4},{1,5},{2,6},{3,7},{4,0},{5,1},{6,2},{7,3},{8,12},{9,13},{10,... | collective-permute-start | bytes 491528 | tf_op jit(solution)/shard_map/ppermute | solution.py:71
  7.5 4.5 %collective-permute-done.rest_0_ = f32[40,8,128]{2,1,0:T(8,128)S(1)} collective-permute-done((f32[40,8,128]{2,1,0:T(8,128)S(1)}, f32[40,8,128]{2,1,0:T(8,128)S(1)}, u32[]{:S(2)}, u32[]{:S(2)}) %collective-permute-start) | collective-permute-done | bytes 163872 | tf_op jit(solution)/shard_map/ppermute | solution.py:71
  12.0 1.9 %shard_map.94 = (f32[15,14,48,128]{3,2,1,0:T(8,128)S(1)}, f32[8,40,128]{2,1,0:T(8,128)S(1)}) custom-call(s32[3]{0:T(128)S(1)} %pad_add_fusion.pos, f32[15,14,48,128]{3,2,1,0:T(8,128)S(1)} %get-tuple-element.19.ext_in, f32[40,8,128]{2,1,0:T(8,128)S(1)} %collective-permute-done.rest_0_), custom_call_target="tpu_custom_call", output_to_operand_aliasing={{0}: (1, {})} | custom-call | tf_op jit(solution)/shard_map/pallas_call | solution.py:701
  13.9 2.1 %collective-permute-start.2 = (f32[8,40,128]{2,1,0:T(8,128)S(1)}, f32[8,40,128]{2,1,0:T(8,128)S(1)}, u32[]{:S(2)}, u32[]{:S(2)}) collective-permute-start(f32[8,40,128]{2,1,0:T(8,128)S(1)} %get-tuple-element.22.payload), channel_id=1, source_target_pairs={{0,4},{1,5},{2,6},{3,7},{4,0},{5,1},{6,2},{7,3},{8,16},{9,17},{10,... | collective-permute-start | bytes 491528 | tf_op jit(solution)/shard_map/ppermute | solution.py:71
  15.9 0.4 %collective-permute-start.1 = (f32[8,40,128]{2,1,0:T(8,128)S(1)}, f32[8,40,128]{2,1,0:T(8,128)S(1)}, u32[]{:S(2)}, u32[]{:S(2)}) collective-permute-start(f32[8,40,128]{2,1,0:T(8,128)S(1)} %get-tuple-element.22.payload), channel_id=1, source_target_pairs={{0,8},{1,9},{2,10},{3,11},{4,12},{5,13},{6,14},{7,15},{8,0},{9,1},... | collective-permute-start | bytes 491528 | tf_op jit(solution)/shard_map/ppermute | solution.py:71
  16.3 2.9 %collective-permute-done.2.rest_1_ = f32[8,40,128]{2,1,0:T(8,128)S(1)} collective-permute-done((f32[8,40,128]{2,1,0:T(8,128)S(1)}, f32[8,40,128]{2,1,0:T(8,128)S(1)}, u32[]{:S(2)}, u32[]{:S(2)}) %collective-permute-start.2) | collective-permute-done | bytes 163872 | tf_op jit(solution)/shard_map/ppermute | solution.py:71
  19.2 0.0 collective-permute-done.1.rest_0_
  19.3 1.8 %shard_map.95 = (f32[16,2,48,128]{3,2,1,0:T(8,128)S(1)}, f32[240,128]{1,0:T(8,128)S(1)}, f32[240,128]{1,0:T(8,128)S(1)}) custom-call(s32[3]{0:T(128)S(1)} %pad_add_fusion.pos, f32[15,14,48,128]{3,2,1,0:T(8,128)S(1)} %get-tuple-element.21.ext.ext_in, f32[8,40,128]{2,1,0:T(8,128)S(1)} %get-tuple-element.22.payload, ...), custom_call_target="tpu_custom_call" | custom-call | tf_op jit(solution)/shard_map/pallas_call | solution.py:713
  21.0 1.7 %collective-permute-start.5 = (f32[240,128]{1,0:T(8,128)S(1)}, f32[240,128]{1,0:T(8,128)S(1)}, u32[]{:S(2)}, u32[]{:S(2)}) collective-permute-start(f32[240,128]{1,0:T(8,128)S(1)} %get-tuple-element.28), channel_id=1, source_target_pairs={{0,1},{1,0},{2,3},{3,2},{4,5},{5,4},{6,7},{7,6},{8,9},{9,8},{10,11... | collective-permute-start | bytes 368648 | tf_op jit(solution)/shard_map/ppermute | solution.py:71
  22.7 1.2 %collective-permute-start.6 = (f32[240,128]{1,0:T(8,128)S(1)}, f32[240,128]{1,0:T(8,128)S(1)}, u32[]{:S(2)}, u32[]{:S(2)}) collective-permute-start(f32[240,128]{1,0:T(8,128)S(1)} %get-tuple-element.29), channel_id=1, source_target_pairs={{0,8},{1,2},{2,1},{3,11},{4,12},{5,6},{6,5},{7,15},{8,0},{9,10},{1... | collective-permute-start | bytes 368648 | tf_op jit(solution)/shard_map/ppermute | solution.py:71
  23.9 3.8 %shard_map.96 = (f32[15,14,48,128]{3,2,1,0:T(8,128)S(1)}, f32[4,16,48,128]{3,2,1,0:T(8,128)S(1)}) custom-call(s32[3]{0:T(128)S(1)} %pad_add_fusion.pos, f32[15,14,48,128]{3,2,1,0:T(8,128)S(1)} %get-tuple-element.21.ext.ext_in, f32[16,2,48,128]{3,2,1,0:T(8,128)S(1)} %get-tuple-element.23.side_in), custom_call_target="tpu_custom_call", output_to_operand_aliasing={{0}: (1, {})} | custom-call | tf_op jit(solution)/shard_map/pallas_call | solution.py:724
  27.7 0.0 collective-permute-done.5.rest_2_
  27.7 0.0 collective-permute-done.6.rest_3_
  27.7 0.0 collective-permute-done.3.rest_0_
  27.7 0.0 collective-permute-done.4.rest_1_
  27.8 6.5 %shard_map.97 = (f32[15,14,48,128]{3,2,1,0:T(8,128)S(1)}, f32[4,16,48,128]{3,2,1,0:T(8,128)S(1)}, f32[8,32,128]{2,1,0:T(8,128)}, f32[3,8,32,128]{3,2,1,0:T(8,128...) custom-call(s32[3]{0:T(128)S(1)} %pad_add_fusion.pos, ...), custom_call_target="tpu_custom_call", output_to_operand_aliasing={{0}: (1, {}), {1}: (2, {})} | custom-call | tf_op jit(solution)/shard_map/pallas_call | solution.py:734
Async XLA Ops:
  3.2 24.6 %collective-permute-start.3 = (f32[40,32,128]{2,1,0:T(8,128)S(1)}, f32[40,32,128]{2,1,0:T(8,128)S(1)}, u32[]{:S(2)}, u32[]{:S(2)}) collective-permute-start(f32[40,32,128]{2,1,0:T(8,128)S(1)} %get-tuple-element.26), channel_id=1, source_target_pairs={{0,1},{1,0},{2,3},{3,2},{4,5},{5,4},{6,7},{7,6},{8,9},{9,8},{10,11... | collective-permute-start | bytes 1966088 | tf_op jit(solution)/shard_map/ppermute | solution.py:71
  5.3 22.4 %collective-permute-start.4 = (f32[40,32,128]{2,1,0:T(8,128)S(1)}, f32[40,32,128]{2,1,0:T(8,128)S(1)}, u32[]{:S(2)}, u32[]{:S(2)}) collective-permute-start(f32[40,32,128]{2,1,0:T(8,128)S(1)} %get-tuple-element.27), channel_id=1, source_target_pairs={{0,8},{1,2},{2,1},{3,11},{4,12},{5,6},{6,5},{7,15},{8,0},{9,10},{1... | collective-permute-start | bytes 1966088 | tf_op jit(solution)/shard_map/ppermute | solution.py:71
  6.3 5.8 %collective-permute-start = (f32[40,8,128]{2,1,0:T(8,128)S(1)}, f32[40,8,128]{2,1,0:T(8,128)S(1)}, u32[]{:S(2)}, u32[]{:S(2)}) collective-permute-start(f32[40,8,128]{2,1,0:T(8,128)S(1)} %get-tuple-element.20), channel_id=1, source_target_pairs={{0,4},{1,5},{2,6},{3,7},{4,0},{5,1},{6,2},{7,3},{8,12},{9,13},{10,... | collective-permute-start | bytes 491528 | tf_op jit(solution)/shard_map/ppermute | solution.py:71
  13.9 5.3 %collective-permute-start.2 = (f32[8,40,128]{2,1,0:T(8,128)S(1)}, f32[8,40,128]{2,1,0:T(8,128)S(1)}, u32[]{:S(2)}, u32[]{:S(2)}) collective-permute-start(f32[8,40,128]{2,1,0:T(8,128)S(1)} %get-tuple-element.22.payload), channel_id=1, source_target_pairs={{0,4},{1,5},{2,6},{3,7},{4,0},{5,1},{6,2},{7,3},{8,16},{9,17},{10,... | collective-permute-start | bytes 491528 | tf_op jit(solution)/shard_map/ppermute | solution.py:71
  15.9 3.3 %collective-permute-start.1 = (f32[8,40,128]{2,1,0:T(8,128)S(1)}, f32[8,40,128]{2,1,0:T(8,128)S(1)}, u32[]{:S(2)}, u32[]{:S(2)}) collective-permute-start(f32[8,40,128]{2,1,0:T(8,128)S(1)} %get-tuple-element.22.payload), channel_id=1, source_target_pairs={{0,8},{1,9},{2,10},{3,11},{4,12},{5,13},{6,14},{7,15},{8,0},{9,1},... | collective-permute-start | bytes 491528 | tf_op jit(solution)/shard_map/ppermute | solution.py:71
  21.0 6.7 %collective-permute-start.5 = (f32[240,128]{1,0:T(8,128)S(1)}, f32[240,128]{1,0:T(8,128)S(1)}, u32[]{:S(2)}, u32[]{:S(2)}) collective-permute-start(f32[240,128]{1,0:T(8,128)S(1)} %get-tuple-element.28), channel_id=1, source_target_pairs={{0,1},{1,0},{2,3},{3,2},{4,5},{5,4},{6,7},{7,6},{8,9},{9,8},{10,11... | collective-permute-start | bytes 368648 | tf_op jit(solution)/shard_map/ppermute | solution.py:71
  22.7 5.0 %collective-permute-start.6 = (f32[240,128]{1,0:T(8,128)S(1)}, f32[240,128]{1,0:T(8,128)S(1)}, u32[]{:S(2)}, u32[]{:S(2)}) collective-permute-start(f32[240,128]{1,0:T(8,128)S(1)} %get-tuple-element.29), channel_id=1, source_target_pairs={{0,8},{1,2},{2,1},{3,11},{4,12},{5,6},{6,5},{7,15},{8,0},{9,10},{1... | collective-permute-start | bytes 368648 | tf_op jit(solution)/shard_map/ppermute | solution.py:71

commit v4 on v3

--- a/solution.py
+++ b/solution.py
@@ -83,7 +83,8 @@
     return received.get(colour, received["even"])
 
 
-def pack(extents, ys, zs, pos, f, w, u, v, p, q, ext, *rest):
+def pack(extents, ys, zs, f, w, u, v, p, q, ext, *rest):
+    pos = place_of()
     nz, ny, _ = extents
     rows = ny + 2 * ROW0
     y_outs = dict(zip(ys, rest))
@@ -138,6 +139,10 @@
     return [ROW0 - HALO + 8 * i for i in range(-(-(ny + 2 * HALO) // 8))]
 
 
+def place_of():
+    return [lax.axis_index(axis) for axis in AXES]
+
+
 def lanes_of():
     lane = lax.broadcasted_iota(jnp.int32, (8, LANES), 1)
     return lane, lane % SLOT
@@ -153,7 +158,8 @@
     return pltpu.roll(values, (level * SLOT + HALO + shift) % LANES, 1)
 
 
-def join_y(extents, ys, pos, ext_in, *rest):
+def join_y(extents, ys, ext_in, *rest):
+    pos = place_of()
     del ext_in
     nz, ny, _ = extents
     rows = ny + 2 * ROW0
@@ -199,7 +205,8 @@
 BLOCKS = -(-FIELDS // PER_TILE)
 
 
-def join_x(extents, xs, ys, zs, pos, ext, payload, *rest):
+def join_x(extents, xs, ys, zs, ext, payload, *rest):
+    pos = place_of()
     nz, ny, _ = extents
     x_got = dict(zip(xs, rest))
     side = rest[len(xs)]
@@ -298,21 +305,35 @@
 ROWS_OF_Q = ((0, 3, 4), (3, 1, 5), (4, 5, 2))
 
 
-def primal_step_of(u, v, a_map, b_map, p, q, prev_p, next_q, upper, lower):
+def primal_step_of(u, v, a_map, b_map, p, q, prev_p, next_q, upper, lower, far_upper, far_lower):
     div = None
     for a in range(3):
-        term = masked(upper[a], p[a]) - masked(lower[a], prev_p[a])
+        term = masked(upper[a], p[a]) - masked(far_lower[a], prev_p[a])
         div = term if div is None else div + term
     new_u = (u + primal_step * div) * b_map + a_map
     new_v = []
     for a in range(3):
         total = p[a]
         for b in range(3):
-            total = total + (masked(upper[b], next_q[b][a]) - masked(lower[b], q[ROWS_OF_Q[b][a]]))
+            here = masked(lower[b], q[ROWS_OF_Q[b][a]])
+            total = total + (masked(far_upper[b], next_q[b][a]) - here)
         new_v.append(v[a] + primal_step * total)
     bar = [(2.0 * dual_step) * new_u - dual_step * u]
     bar += [(2.0 * dual_step) * new_v[a] - dual_step * v[a] for a in range(3)]
     return new_u, new_v, bar
+
+
+DEPTH = 2
+
+
+def pipelined(*passes):
+    waiting = []
+    for store in itertools.chain(*passes):
+        waiting.append(store)
+        if len(waiting) > DEPTH:
+            waiting.pop(0)()
+    for store in waiting:
+        store()
 
 
 class Steps:
@@ -330,22 +351,32 @@
             lower = jnp.logical_and(places > 0, places < extent)
             return upper.astype(jnp.float32), lower.astype(jnp.float32)
 
-        outer = (self.starts[0], self.starts[-1])
-        self.y_masks = [
-            masks(pos[1] * ny + (row - ROW0) + sub, full[1]) if row in outer else (None, None)
-            for row in self.starts
-        ]
+        def tiles(rows):
+            outer = (rows[0], rows[-1])
+            return [
+                (row,) + (masks(pos[1] * ny + (row - ROW0) + sub, full[1]) if row in outer else (None, None))
+                for row in rows
+            ]
+
+        self.tiles = tiles(self.starts)
+        self.own_tiles = tiles(list(range(ROW0, ROW0 + ny, 8)))
         self.x_main = masks(pos[0] * nx + self.lane, full[0])
         self.x_side = [masks(pos[0] * nx + at + slot, full[0]) for at in (-HALO, nx - HALO)]
         self.z_side = masks(pos[2] * nz - HALO + self.lane // SLOT, full[2])
         self.first, self.last = self.lane == 0, self.lane == LANES - 1
+        at_first, at_last = pos[0] == 0, pos[0] == sizes["gx"] - 1
+        self.beyond = (
+            jnp.logical_and(slot == HALO - 1, at_first),
+            jnp.logical_and(slot == HALO, at_last),
+        )
 
     def z_main(self, level):
         place = self.pos[2] * self.nz - HALO + level
         upper = jnp.logical_and(place >= 0, place < self.full[2] - 1)
         lower = jnp.logical_and(place > 0, place < self.full[2])
         one, none = jnp.float32(1.0), jnp.float32(0.0)
-        return jnp.where(upper, one, none), jnp.where(lower, one, none)
+        upper, lower = jnp.where(upper, one, none), jnp.where(lower, one, none)
+        return (upper if level == HALO + self.nz - 1 else None), (lower if level == HALO else None)
 
     def from_low(self, values, level):
         return pltpu.roll(values, LANES - HALO + 1 - SLOT * level, 1)
@@ -368,21 +399,32 @@
         for row in self.starts:
             here = pl.ds(row, 8)
             maps = self.maps(self.ext[F, level, here, :], self.ext[W, level, here, :])
-            self.ext[F, level, here, :], self.ext[W, level, here, :] = maps
-            for a in range(4):
-                self.bars[a, level + 1, here, :] = dual_step * self.ext[U + a, level, here, :]
+            bar = [dual_step * self.ext[U + a, level, here, :] for a in range(4)]
+
+            def store(here=here, maps=maps, bar=bar):
+                self.ext[F, level, here, :], self.ext[W, level, here, :] = maps
+                for a in range(4):
+                    self.bars[a, level + 1, here, :] = bar[a]
+
+            yield store
 
     def prepare_side(self, which, row, fields):
         here = pl.ds(row, 8)
-        for field, values in enumerate(list(self.maps(fields[F], fields[W])) + fields[U:]):
-            self.side[field, which, here, :] = values
-        for a in range(4):
-            self.side_bars[a, which, here, :] = dual_step * fields[U + a]
+        values = list(self.maps(fields[F], fields[W])) + fields[U:]
+        bar = [dual_step * fields[U + a] for a in range(4)]
+
+        def store():
+            for field in range(FIELDS):
+                self.side[field, which, here, :] = values[field]
+            for a in range(4):
+                self.side_bars[a, which, here, :] = bar[a]
+
+        return store
 
     def p_main(self, level):
         ext, bars = self.ext, self.bars
         upper_z, _ = self.z_main(level)
-        for i, row in enumerate(self.starts):
+        for row, upper_y, _ in self.tiles:
             here = pl.ds(row, 8)
             bar = [bars[a, level + 1, here, :] for a in range(4)]
             next_bar = [
@@ -391,14 +433,18 @@
                 bars[0, level + 2, here, :],
             ]
             p = [ext[PF + a, level, here, :] for a in range(3)]
-            p = p_step(bar, next_bar, p, (self.x_main[0], self.y_masks[i][0], upper_z))
-            for a in range(3):
-                ext[PF + a, level, here, :] = p[a]
+            p = p_step(bar, next_bar, p, (self.x_main[0], upper_y, upper_z))
+
+            def store(here=here, p=p):
+                for a in range(3):
+                    ext[PF + a, level, here, :] = p[a]
+
+            yield store
 
     def q_main(self, level):
         ext, bars = self.ext, self.bars
         _, lower_z = self.z_main(level)
-        for i, row in enumerate(self.starts):
+        for row, _, lower_y in self.tiles:
             here = pl.ds(row, 8)
             bar = [bars[1 + a, level + 1, here, :] for a in range(3)]
             prev_bar = [
@@ -407,14 +453,18 @@
                 [bars[1 + a, level, here, :] for a in range(3)],
             ]
             q = [ext[QF + a, level, here, :] for a in range(6)]
-            q = q_step(bar, prev_bar, q, (self.x_main[1], self.y_masks[i][1], lower_z))
-            for a in range(6):
-                ext[QF + a, level, here, :] = q[a]
-
-    def primal_main(self, level):
+            q = q_step(bar, prev_bar, q, (self.x_main[1], lower_y, lower_z))
+
+            def store(here=here, q=q):
+                for a in range(6):
+                    ext[QF + a, level, here, :] = q[a]
+
+            yield store
+
+    def primal_main(self, level, final=False):
         ext, bars, side = self.ext, self.bars, self.side
         upper_z, lower_z = self.z_main(level)
-        for i, row in enumerate(self.starts):
+        for row, upper_y, lower_y in self.own_tiles if final else self.tiles:
             here = pl.ds(row, 8)
             p = [ext[PF + a, level, here, :] for a in range(3)]
             q = [ext[QF + a, level, here, :] for a in range(6)]
@@ -437,39 +487,63 @@
                 q,
                 prev_p,
                 next_q,
-                (self.x_main[0], self.y_masks[i][0], upper_z),
-                (self.x_main[1], self.y_masks[i][1], lower_z),
+                (self.x_main[0], upper_y, upper_z),
+                (self.x_main[1], lower_y, lower_z),
+                (None, upper_y, upper_z),
+                (None, lower_y, lower_z),
             )
-            for a, value in enumerate([new_u] + new_v):
-                ext[U + a, level, here, :] = value
-            for a in range(4):
-                bars[a, level + 1, here, :] = bar[a]
-
-    def dual_side(self):
+
+            def store(here=here, values=[new_u] + new_v, bar=bar):
+                for a in range(4):
+                    ext[U + a, level, here, :] = values[a]
+                for a in () if final else range(4):
+                    bars[a, level + 1, here, :] = bar[a]
+
+            yield store
+
+    def dual_side(self, z_masks, final=False):
         side, side_bars = self.side, self.side_bars
-        for which, (i, row) in itertools.product((0, 1), enumerate(self.starts)):
+        z_upper, z_lower = z_masks
+        for which, (row, upper_y, lower_y) in itertools.product((0, 1), self.tiles):
             here = pl.ds(row, 8)
             bar = [side_bars[a, which, here, :] for a in range(4)]
-            next_bar = [
-                pltpu.roll(bar[0], LANES - 1, 1),
-                side_bars[0, which, pl.ds(row + 1, 8), :],
-                pltpu.roll(bar[0], LANES - SLOT, 1),
-            ]
-            prev_bar = [
-                [pltpu.roll(bar[1 + a], 1, 1) for a in range(3)],
-                [side_bars[1 + a, which, pl.ds(row - 1, 8), :] for a in range(3)],
-                [pltpu.roll(bar[1 + a], SLOT, 1) for a in range(3)],
-            ]
-            upper = (self.x_side[which][0], self.y_masks[i][0], self.z_side[0])
-            lower = (self.x_side[which][1], self.y_masks[i][1], self.z_side[1])
-            p = p_step(bar, next_bar, [side[PF + a, which, here, :] for a in range(3)], upper)
-            q = q_step(bar[1:], prev_bar, [side[QF + a, which, here, :] for a in range(6)], lower)
-            for a, value in enumerate(p + q):
-                side[PF + a, which, here, :] = value
-
-    def primal_side(self):
+            if not (final and which == 1):
+                next_bar = [
+                    pltpu.roll(bar[0], LANES - 1, 1),
+                    side_bars[0, which, pl.ds(row + 1, 8), :],
+                    pltpu.roll(bar[0], LANES - SLOT, 1),
+                ]
+                upper = (self.x_side[which][0], upper_y, z_upper)
+                p = p_step(bar, next_bar, [side[PF + a, which, here, :] for a in range(3)], upper)
+                if which == 0:
+                    p[0] = jnp.where(self.beyond[0], 0.0, p[0])
+
+                def store(which=which, here=here, p=p):
+                    for a in range(3):
+                        side[PF + a, which, here, :] = p[a]
+
+                yield store
+            if not (final and which == 0):
+                prev_bar = [
+                    [pltpu.roll(bar[1 + a], 1, 1) for a in range(3)],
+                    [side_bars[1 + a, which, pl.ds(row - 1, 8), :] for a in range(3)],
+                    [pltpu.roll(bar[1 + a], SLOT, 1) for a in range(3)],
+                ]
+                lower = (self.x_side[which][1], lower_y, z_lower)
+                q = q_step(bar[1:], prev_bar, [side[QF + a, which, here, :] for a in range(6)], lower)
+                if which == 1:
+                    for a in ROWS_OF_Q[0]:
+                        q[a] = jnp.where(self.beyond[1], 0.0, q[a])
+
+                def store(which=which, here=here, q=q):
+                    for a in range(6):
+                        side[QF + a, which, here, :] = q[a]
+
+                yield store
+
+    def primal_side(self, z_masks):
         side, side_bars = self.side, self.side_bars
-        for which, (i, row) in itertools.product((0, 1), enumerate(self.starts)):
+        for which, (row, upper_y, lower_y) in itertools.product((0, 1), self.tiles):
             here = pl.ds(row, 8)
             p = [side[PF + a, which, here, :] for a in range(3)]
             q = [side[QF + a, which, here, :] for a in range(6)]
@@ -483,6 +557,8 @@
                 [side[QF + j, which, pl.ds(row + 1, 8), :] for j in ROWS_OF_Q[1]],
                 [pltpu.roll(q[j], LANES - SLOT, 1) for j in ROWS_OF_Q[2]],
             ]
+            upper = (self.x_side[which][0], upper_y, z_masks[0])
+            lower = (self.x_side[which][1], lower_y, z_masks[1])
             new_u, new_v, bar = primal_step_of(
                 side[U, which, here, :],
                 [side[V + a, which, here, :] for a in range(3)],
@@ -492,52 +568,49 @@
                 q,
                 prev_p,
                 next_q,
-                (self.x_side[which][0], self.y_masks[i][0], self.z_side[0]),
-                (self.x_side[which][1], self.y_masks[i][1], self.z_side[1]),
+                upper,
+                lower,
+                upper,
+                lower,
             )
-            for a, value in enumerate([new_u] + new_v):
-                side[U + a, which, here, :] = value
-            for a in range(4):
-                side_bars[a, which, here, :] = bar[a]
-
-
-def level_loop(start, stop, *bodies):
-    count = max(stop - start, 0)
-
-    def trip(i, carry):
-        for body in bodies:
-            for j in (0, 1):
-                body(start + 2 * i + j)
-        return carry
-
-    lax.fori_loop(0, count // 2, trip, 0)
-    if count % 2:
-        for body in bodies:
-            body(stop - 1)
-
-
-def solve_inner(extents, sizes, pos, ext_in, side_in, ext, bars, side, side_bars):
+
+            def store(which=which, here=here, values=[new_u] + new_v, bar=bar):
+                for a in range(4):
+                    side[U + a, which, here, :] = values[a]
+                    side_bars[a, which, here, :] = bar[a]
+
+            yield store
+
+
+def solve_inner(extents, sizes, ext_in, side_in, ext, bars, side, side_bars):
+    pos = place_of()
     del ext_in
     nz, _, _ = extents
     steps = Steps(extents, sizes, pos, ext, bars, side, side_bars)
-    for which, row in itertools.product((0, 1), steps.starts):
-        fields = [side_in[field, which, pl.ds(row, 8), :] for field in range(FIELDS)]
-        steps.prepare_side(which, row, fields)
-    level_loop(HALO, HALO + nz, steps.prepare_main)
+
+    def strips():
+        for which, row in itertools.product((0, 1), steps.starts):
+            fields = [side_in[field, which, pl.ds(row, 8), :] for field in range(FIELDS)]
+            yield steps.prepare_side(which, row, fields)
+
+    pipelined(strips(), *(steps.prepare_main(level) for level in range(HALO, HALO + nz)))
+    inside = (None, None)
     for step in range(ITERS):
+        final = step == ITERS - 1
         low, high = HALO + step, HALO + nz - step
-        if high - 1 <= low:
-            break
-        level_loop(low, high - 1, steps.p_main, lambda level: steps.q_main(level + 1))
-        if high - 2 < low + 1:
-            break
-        steps.dual_side()
-        level_loop(low + 1, high - 1, steps.primal_main)
-        if step + 1 < ITERS:
-            steps.primal_side()
-
-
-def solve_outer(extents, sizes, ys, zs, pos, ext_in, bars_in, side_in, *rest):
+        pipelined(
+            steps.dual_side(inside, final),
+            *(steps.p_main(level) for level in range(low, high - 1)),
+            *(steps.q_main(level) for level in range(low + 1, high)),
+        )
+        pipelined(
+            *(() if final else (steps.primal_side(inside),)),
+            *(steps.primal_main(level, final) for level in range(low + 1, high - 1)),
+        )
+
+
+def solve_outer(extents, sizes, ys, zs, ext_in, bars_in, side_in, *rest):
+    pos = place_of()
     del ext_in, bars_in
     nz, ny, _ = extents
     z_got = dict(zip(zs, rest))
@@ -578,7 +651,6 @@
     outer = jnp.logical_or(below, above)
 
     def strips(got_low, got_high):
-        ready = None
         for j, row in enumerate(starts):
             here = pl.ds(row, 8)
             fields = ([], [])
@@ -598,23 +670,17 @@
                 right = jnp.where(slot < HALO, columns, came)
                 fields[0].append(jnp.where(outer, left, side_in[field, 0, here, :]))
                 fields[1].append(jnp.where(outer, right, side_in[field, 1, here, :]))
-            for done in (ready, (row, fields)):
-                if done is not None and (done is ready or row == starts[-1]):
-                    for which in (0, 1):
-                        steps.prepare_side(which, done[0], done[1][which])
-            ready = (row, fields)
+            made = [steps.prepare_side(which, row, fields[which]) for which in (0, 1)]
+            yield from made
 
     for z_parity in (0, 1):
 
         @pl.when(pos[2] % 2 == z_parity)
         def _():
-            strips(
-                pick(frame_got, colour_of("low", z_parity)),
-                pick(frame_got, colour_of("high", z_parity)),
-            )
-
-    for level in list(low_levels) + list(high_levels):
-        steps.prepare_main(level)
+            low, high = (pick(frame_got, colour_of(z_side, z_parity)) for z_side in sides)
+            pipelined(strips(low, high))
+
+    pipelined(*(steps.prepare_main(level) for level in list(low_levels) + list(high_levels)))
 
     def out_copies(fields):
         own = (pl.ds(HALO, nz), pl.ds(ROW0, ny))
@@ -622,36 +688,25 @@
 
     duals = [(pl.ds(PF, 3), out_p), (pl.ds(QF, 6), out_q)]
     primals = [(U, out_u), (pl.ds(V, 3), out_v)]
-    apart = nz >= 2 * ITERS
 
     def outer_levels(low_first, high_first):
-        if apart:
-            return [first + j for first in (low_first, high_first) for j in range(HALO)]
         return sorted({first + j for first in (low_first, high_first) for j in range(HALO)})
 
-    def iteration(step, carry):
+    for step in range(ITERS):
+        final = step == ITERS - 1
         top_level = HALO + nz - 1 - step
-        for level in outer_levels(step, top_level):
-            steps.p_main(level)
-        for level in outer_levels(step + 1, top_level + 1):
-            steps.q_main(level)
-
-        @pl.when(step == ITERS - 1)
-        def _():
+        pipelined(
+            steps.dual_side(steps.z_side, final),
+            *(steps.p_main(level) for level in outer_levels(step, top_level)),
+            *(steps.q_main(level) for level in outer_levels(step + 1, top_level + 1)),
+        )
+        if final:
             for copy in out_copies(duals):
                 copy.start()
-
-        steps.dual_side()
-        for level in outer_levels(step + 1, top_level):
-            steps.primal_main(level)
-        pl.when(step < ITERS - 1)(steps.primal_side)
-        return carry
-
-    if apart:
-        lax.fori_loop(0, ITERS, iteration, 0)
-    else:
-        for step in range(ITERS):
-            iteration(step, 0)
+        pipelined(
+            *(() if final else (steps.primal_side(steps.z_side),)),
+            *(steps.primal_main(level, final) for level in outer_levels(step + 1, top_level)),
+        )
     for copy in out_copies(primals):
         copy.start()
     for copy in out_copies(duals + primals):
@@ -664,10 +719,8 @@
     assert nx == LANES and ny % 8 == 0 and nz * SLOT <= LANES // 2
     assert min(nz, ny) >= HALO and min(sizes.values()) > 1
     xs, ys, zs = (colours(sizes[axis]) for axis in AXES)
-    pos = jnp.stack([lax.axis_index(axis) for axis in AXES])
     args = tuple(pltpu.with_memory_space_constraint(a, pltpu.HBM) for a in (noisy_image, fidelity, primal_u, primal_v, dual_p, dual_q))
     f32 = jnp.float32
-    smem = pl.BlockSpec(memory_space=pltpu.SMEM)
     anywhere = pl.BlockSpec(memory_space=pltpu.HBM)
     vmem = pl.BlockSpec(memory_space=pltpu.VMEM)
 
@@ -688,58 +741,58 @@
     ext_shape = shaped(FIELDS, levels, rows, nx)
     packed = call(
         functools.partial(pack, extents, ys, zs),
-        [smem] + [anywhere] * 6,
+        [anywhere] * 6,
         [ext_shape] + [shaped(SENT, nz, nx)] * len(ys) + [shaped(SENT, ny, nx)] * len(zs),
         [vmem] * (1 + len(ys) + len(zs)),
         16,
         scratch_shapes=[pltpu.SemaphoreType.DMA, pltpu.SemaphoreType.DMA],
-    )(pos, *args)
+    )(*args)
     ext, y_pay, z_pay = packed[0], packed[1 : 1 + len(ys)], packed[1 + len(ys) :]
     y_got = [exchange(pay, {"gy": c}, sizes) for c, pay in zip(ys, y_pay)]
     z_got = [exchange(pay, {"gz": c}, sizes) for c, pay in zip(zs, z_pay)]
 
     ext, x_pay = call(
         functools.partial(join_y, extents, ys),
-        [smem] + [vmem] * (1 + len(ys)),
+        [vmem] * (1 + len(ys)),
         [ext_shape, shaped(GROUPS, strip_rows, nx)],
         [vmem] * 2,
         16,
-        input_output_aliases={1: 0},
-    )(pos, ext, *y_got)
+        input_output_aliases={0: 0},
+    )(ext, *y_got)
     x_got = [exchange(x_pay, {"gx": c}, sizes) for c in xs]
 
     both = shaped(FIELDS, 2, rows, nx)
     frame = shaped(BLOCKS * strip_rows + len(ys) * SENT * HALO, nx)
     side, *frame_pay = call(
         functools.partial(join_x, extents, xs, ys, zs),
-        [smem] + [vmem] * (2 + len(xs)),
+        [vmem] * (2 + len(xs)),
         [shaped(2 * GROUPS, 2, rows, nx)] + [frame] * len(zs),
         [vmem] * (1 + len(zs)),
         16,
-    )(pos, ext, x_pay, *x_got)
+    )(ext, x_pay, *x_got)
     frame_got = [exchange(pay, {"gz": c}, sizes) for c, pay in zip(zs, frame_pay)]
 
     bar_shape = shaped(4, levels + 2, rows, nx)
     scratch = [pltpu.VMEM(both.shape, f32), pltpu.VMEM((4,) + both.shape[1:], f32)]
     ext, bars = call(
         functools.partial(solve_inner, extents, sizes),
-        [smem] + [vmem] * 2,
+        [vmem] * 2,
         [ext_shape, bar_shape],
         [vmem] * 2,
         16,
-        input_output_aliases={1: 0},
+        input_output_aliases={0: 0},
         scratch_shapes=scratch,
-    )(pos, ext, side)
+    )(ext, side)
 
     solved = call(
         functools.partial(solve_outer, extents, sizes, ys, zs),
-        [smem] + [vmem] * (3 + 2 * len(zs)),
+        [vmem] * (3 + 2 * len(zs)),
         [ext_shape, bar_shape] + [shaped(*a.shape) for a in (primal_u, primal_v, dual_p, dual_q)],
         [vmem] * 2 + [anywhere] * 4,
         24,
-        input_output_aliases={1: 0, 2: 1},
+        input_output_aliases={0: 0, 1: 1},
         scratch_shapes=scratch + [pltpu.SemaphoreType.DMA],
-    )(pos, ext, bars, side, *z_got, *frame_got)
+    )(ext, bars, side, *z_got, *frame_got)
     return tuple(solved[2:])
 
 

time: 34.4 us -> 29.6 us (0.86)
  the two profiles are of different devices: /device:TPU:1 before, /device:TPU:0 now
where the time goes in v4:
time: 29.6 us; the launch traced here: 29.5 us
  Pallas kernels  10.5 us (35%)
  waiting for transfers between devices  10 us (34%)
  starting transfers between devices  8.27 us (28%)
  between operations  0.66 us (2%)
    ppermute x7, waiting for transfers between devices, exchange(): return lax.ppermute(values, AXES, pairs)  10 us
    ppermute x7, starting transfers between devices, exchange(): return lax.ppermute(values, AXES, pairs)  8.27 us
    pallas_call x1, Pallas kernels, per_device(): call(functools.partial(solve_outer, extents, sizes, ys, zs), [vmem] * (3...  4.26 us
    pallas_call x1, Pallas kernels, per_device(): call(functools.partial(pack, extents, ys, zs), [anywhere] * 6, [ext_shape...  1.91 us
    pallas_call x1, Pallas kernels, per_device(): call(functools.partial(solve_inner, extents, sizes), [vmem] * 2, [ext_sha...  1.89 us
    pallas_call x1, Pallas kernels, per_device(): call(functools.partial(join_y, extents, ys), [vmem] * (1 + len(ys)), [ext...  1.3 us
    pallas_call x1, Pallas kernels, per_device(): call(functools.partial(join_x, extents, xs, ys, zs), [vmem] * (2 + len(xs...  1.15 us
  transfers between devices with their start and end apart: 7, of which 3 were waited for; matrix products, arithmetic and copies ran while one was open for 0% of the time, Pallas kernels for 15%

profile of v4, /device:TPU:0, one launch (start us, length us, event | category | flops | bytes accessed | tf_op | source)
XLA Modules:
  0.0 29.5 jit_solution(10131117474437155683)
XLA Ops:
  0.6 1.9 %shard_map.93 = (f32[15,14,48,128]{3,2,1,0:T(8,128)S(1)}, f32[40,8,128]{2,1,0:T(8,128)S(1)}, f32[40,32,128]{2,1,0:T(8,128)S(1)}, f32[40,32,128]{2,1,0:T(8,128)S(1)}) custom-call(f32[8,32,128]{2,1,0:T(8,128)} %f.1, f32[8,32,128]{2,1,0:T(8,128)} %w.1, f32[8,32,128]{2,1,0:T(8,128)} %u.1, f32[3,8,32,128]{3,2,1,0:T(8,128)} %v.1, f32[3,8,32,128]{3,2,1,0:T(8,128)} %p.1, ...), custom_call_target="tpu_custom_call" | custom-call | tf_op jit(solution)/shard_map/pallas_call | solution.py:742
  2.5 3.1 %collective-permute-start.3 = (f32[40,32,128]{2,1,0:T(8,128)S(1)}, f32[40,32,128]{2,1,0:T(8,128)S(1)}, u32[]{:S(2)}, u32[]{:S(2)}) collective-permute-start(f32[40,32,128]{2,1,0:T(8,128)S(1)} %get-tuple-element.26), channel_id=1, source_target_pairs={{0,1},{1,0},{2,3},{3,2},{4,5},{5,4},{6,7},{7,6},{8,9},{9,8},{10,11... | collective-permute-start | bytes 1966088 | tf_op jit(solution)/shard_map/ppermute | solution.py:71
  5.6 0.0 collective-permute-start.4
  5.6 1.5 %collective-permute-start = (f32[40,8,128]{2,1,0:T(8,128)S(1)}, f32[40,8,128]{2,1,0:T(8,128)S(1)}, u32[]{:S(2)}, u32[]{:S(2)}) collective-permute-start(f32[40,8,128]{2,1,0:T(8,128)S(1)} %get-tuple-element.20), channel_id=1, source_target_pairs={{0,4},{1,5},{2,6},{3,7},{4,0},{5,1},{6,2},{7,3},{8,12},{9,13},{10,... | collective-permute-start | bytes 491528 | tf_op jit(solution)/shard_map/ppermute | solution.py:71
  7.1 5.1 %collective-permute-done.rest_0_ = f32[40,8,128]{2,1,0:T(8,128)S(1)} collective-permute-done((f32[40,8,128]{2,1,0:T(8,128)S(1)}, f32[40,8,128]{2,1,0:T(8,128)S(1)}, u32[]{:S(2)}, u32[]{:S(2)}) %collective-permute-start) | collective-permute-done | bytes 163872 | tf_op jit(solution)/shard_map/ppermute | solution.py:71
  12.3 1.3 %shard_map.94 = (f32[15,14,48,128]{3,2,1,0:T(8,128)S(1)}, f32[8,40,128]{2,1,0:T(8,128)S(1)}) custom-call(f32[15,14,48,128]{3,2,1,0:T(8,128)S(1)} %get-tuple-element.19.ext_in, f32[40,8,128]{2,1,0:T(8,128)S(1)} %collective-permute-done.rest_0_), custom_call_target="tpu_custom_call", output_to_operand_aliasing={{0}: (0, {})} | custom-call | tf_op jit(solution)/shard_map/pallas_call | solution.py:754
  13.6 1.6 %collective-permute-start.2 = (f32[8,40,128]{2,1,0:T(8,128)S(1)}, f32[8,40,128]{2,1,0:T(8,128)S(1)}, u32[]{:S(2)}, u32[]{:S(2)}) collective-permute-start(f32[8,40,128]{2,1,0:T(8,128)S(1)} %get-tuple-element.22.payload), channel_id=1, source_target_pairs={{0,4},{1,5},{2,6},{3,7},{4,0},{5,1},{6,2},{7,3},{8,16},{9,17},{10,... | collective-permute-start | bytes 491528 | tf_op jit(solution)/shard_map/ppermute | solution.py:71
  15.1 0.1 collective-permute-start.1
  15.3 3.7 %collective-permute-done.2.rest_1_ = f32[8,40,128]{2,1,0:T(8,128)S(1)} collective-permute-done((f32[8,40,128]{2,1,0:T(8,128)S(1)}, f32[8,40,128]{2,1,0:T(8,128)S(1)}, u32[]{:S(2)}, u32[]{:S(2)}) %collective-permute-start.2) | collective-permute-done | bytes 163872 | tf_op jit(solution)/shard_map/ppermute | solution.py:71
  19.0 0.0 collective-permute-done.1.rest_0_
  19.0 1.1 %shard_map.95 = (f32[16,2,48,128]{3,2,1,0:T(8,128)S(1)}, f32[240,128]{1,0:T(8,128)S(1)}, f32[240,128]{1,0:T(8,128)S(1)}) custom-call(f32[15,14,48,128]{3,2,1,0:T(8,128)S(1)} %get-tuple-element.21.ext.ext_in, f32[8,40,128]{2,1,0:T(8,128)S(1)} %get-tuple-element.22.payload, f32[8,40,128]{2,1,0:T(8,128)S(1)} %collective-permute-done.1.rest_0_, ...), custom_call_target="tpu_custom_call" | custom-call | tf_op jit(solution)/shard_map/pallas_call | solution.py:766
  20.1 2.0 %collective-permute-start.5 = (f32[240,128]{1,0:T(8,128)S(1)}, f32[240,128]{1,0:T(8,128)S(1)}, u32[]{:S(2)}, u32[]{:S(2)}) collective-permute-start(f32[240,128]{1,0:T(8,128)S(1)} %get-tuple-element.28), channel_id=1, source_target_pairs={{0,1},{1,0},{2,3},{3,2},{4,5},{5,4},{6,7},{7,6},{8,9},{9,8},{10,11... | collective-permute-start | bytes 368648 | tf_op jit(solution)/shard_map/ppermute | solution.py:71
  22.1 0.0 collective-permute-start.6
  22.1 1.9 %shard_map.96 = (f32[15,14,48,128]{3,2,1,0:T(8,128)S(1)}, f32[4,16,48,128]{3,2,1,0:T(8,128)S(1)}) custom-call(f32[15,14,48,128]{3,2,1,0:T(8,128)S(1)} %get-tuple-element.21.ext.ext_in, f32[16,2,48,128]{3,2,1,0:T(8,128)S(1)} %get-tuple-element.23.side_in), custom_call_target="tpu_custom_call", output_to_operand_aliasing={{0}: (0, {})} | custom-call | tf_op jit(solution)/shard_map/pallas_call | solution.py:777
  24.0 1.2 %collective-permute-done.5.rest_2_ = f32[240,128]{1,0:T(8,128)S(1)} collective-permute-done((f32[240,128]{1,0:T(8,128)S(1)}, f32[240,128]{1,0:T(8,128)S(1)}, u32[]{:S(2)}, u32[]{:S(2)}) %collective-permute-start.5) | collective-permute-done | bytes 122912 | tf_op jit(solution)/shard_map/ppermute | solution.py:71
  25.2 0.0 collective-permute-done.6.rest_3_
  25.2 0.0 collective-permute-done.3.rest_0_
  25.2 0.0 collective-permute-done.4.rest_1_
  25.2 4.3 %shard_map.97 = (f32[15,14,48,128]{3,2,1,0:T(8,128)S(1)}, f32[4,16,48,128]{3,2,1,0:T(8,128)S(1)}, f32[8,32,128]{2,1,0:T(8,128)}, f32[3,8,32,128]{3,2,1,0:T(8,128...) custom-call(f32[15,14,48,128]{3,2,1,0:T(8,128)S(1)} %get-tuple-element.24.e, ...), custom_call_target="tpu_custom_call", output_to_operand_aliasing={{0}: (0, {}), {1}: (1, {})} | custom-call | tf_op jit(solution)/shard_map/pallas_call | solution.py:787
Async XLA Ops:
  2.5 22.6 %collective-permute-start.3 = (f32[40,32,128]{2,1,0:T(8,128)S(1)}, f32[40,32,128]{2,1,0:T(8,128)S(1)}, u32[]{:S(2)}, u32[]{:S(2)}) collective-permute-start(f32[40,32,128]{2,1,0:T(8,128)S(1)} %get-tuple-element.26), channel_id=1, source_target_pairs={{0,1},{1,0},{2,3},{3,2},{4,5},{5,4},{6,7},{7,6},{8,9},{9,8},{10,11... | collective-permute-start | bytes 1966088 | tf_op jit(solution)/shard_map/ppermute | solution.py:71
  5.6 19.5 %collective-permute-start.4 = (f32[40,32,128]{2,1,0:T(8,128)S(1)}, f32[40,32,128]{2,1,0:T(8,128)S(1)}, u32[]{:S(2)}, u32[]{:S(2)}) collective-permute-start(f32[40,32,128]{2,1,0:T(8,128)S(1)} %get-tuple-element.27), channel_id=1, source_target_pairs={{0,8},{1,2},{2,1},{3,11},{4,12},{5,6},{6,5},{7,15},{8,0},{9,10},{1... | collective-permute-start | bytes 1966088 | tf_op jit(solution)/shard_map/ppermute | solution.py:71
  5.6 6.6 %collective-permute-start = (f32[40,8,128]{2,1,0:T(8,128)S(1)}, f32[40,8,128]{2,1,0:T(8,128)S(1)}, u32[]{:S(2)}, u32[]{:S(2)}) collective-permute-start(f32[40,8,128]{2,1,0:T(8,128)S(1)} %get-tuple-element.20), channel_id=1, source_target_pairs={{0,4},{1,5},{2,6},{3,7},{4,0},{5,1},{6,2},{7,3},{8,12},{9,13},{10,... | collective-permute-start | bytes 491528 | tf_op jit(solution)/shard_map/ppermute | solution.py:71
  13.6 5.4 %collective-permute-start.2 = (f32[8,40,128]{2,1,0:T(8,128)S(1)}, f32[8,40,128]{2,1,0:T(8,128)S(1)}, u32[]{:S(2)}, u32[]{:S(2)}) collective-permute-start(f32[8,40,128]{2,1,0:T(8,128)S(1)} %get-tuple-element.22.payload), channel_id=1, source_target_pairs={{0,4},{1,5},{2,6},{3,7},{4,0},{5,1},{6,2},{7,3},{8,16},{9,17},{10,... | collective-permute-start | bytes 491528 | tf_op jit(solution)/shard_map/ppermute | solution.py:71
  15.1 3.8 %collective-permute-start.1 = (f32[8,40,128]{2,1,0:T(8,128)S(1)}, f32[8,40,128]{2,1,0:T(8,128)S(1)}, u32[]{:S(2)}, u32[]{:S(2)}) collective-permute-start(f32[8,40,128]{2,1,0:T(8,128)S(1)} %get-tuple-element.22.payload), channel_id=1, source_target_pairs={{0,8},{1,9},{2,10},{3,11},{4,12},{5,13},{6,14},{7,15},{8,0},{9,1},... | collective-permute-start | bytes 491528 | tf_op jit(solution)/shard_map/ppermute | solution.py:71
  20.1 5.1 %collective-permute-start.5 = (f32[240,128]{1,0:T(8,128)S(1)}, f32[240,128]{1,0:T(8,128)S(1)}, u32[]{:S(2)}, u32[]{:S(2)}) collective-permute-start(f32[240,128]{1,0:T(8,128)S(1)} %get-tuple-element.28), channel_id=1, source_target_pairs={{0,1},{1,0},{2,3},{3,2},{4,5},{5,4},{6,7},{7,6},{8,9},{9,8},{10,11... | collective-permute-start | bytes 368648 | tf_op jit(solution)/shard_map/ppermute | solution.py:71
  22.1 3.1 %collective-permute-start.6 = (f32[240,128]{1,0:T(8,128)S(1)}, f32[240,128]{1,0:T(8,128)S(1)}, u32[]{:S(2)}, u32[]{:S(2)}) collective-permute-start(f32[240,128]{1,0:T(8,128)S(1)} %get-tuple-element.29), channel_id=1, source_target_pairs={{0,8},{1,2},{2,1},{3,11},{4,12},{5,6},{6,5},{7,15},{8,0},{9,10},{1... | collective-permute-start | bytes 368648 | tf_op jit(solution)/shard_map/ppermute | solution.py:71
